TPU v7x, 32 devices: a whole 2x2x4 slice. The times are simulated.
32 devices in a mesh: groups: 2 (over y), src: 4 (over z), act: 4 (over x, core).
Axes of the slice: x: 2, y: 2, z: 4, core: 2. Of those that a mesh axis runs over, the one named last changes fastest.
Arguments:
- star_state: float32 [12, 4096], P(None, ('groups', 'src')), parts along dimension 1, may hold values from -6 to 6
- masses: float32 [4096], P(('groups', 'src')), parts along dimension 0, may hold values from 0.25 to 4
- phases: float32 [4096], P(('groups', 'src')), parts along dimension 0, may hold values from 0 to 1
- levels: int32 [4096], P(('groups', 'src')), parts along dimension 0, may hold values from 0 to 4, as said below
- active_list: int32 [2048], P(('groups', 'src', 'act')), parts along dimension 0, may hold values from 0 to 511, as said below
- active_count: int32 [32], P(('groups', 'src', 'act')), parts along dimension 0, may hold values from 0 to 64, as said below
Outputs:
- stepped_state: float32 [12, 4096], P(None, ('groups', 'src')), parts along dimension 1
There are 2 independent parts, one for each index of `groups`. A program takes and returns all parts, laid end to end along the dimension named above; each array names one. Nothing has to cross between parts.
Inputs may be any that keep to these rules, and one draw needn't show every extreme that they name: `levels`: levels_j = 4 exactly for the stars that appear among the live entries of the lists. `active_list`: live entries (the first active_count ones of a device's 64) are distinct indices within the device's src shard; every active star of a shard is live in exactly one list of that shard's 4 devices; later slots hold arbitrary indices of the shard. `active_count`: at most 64 a device, reached in every draw; the counts of one src shard's devices sum to at most 128, reached by some shard in every draw.
All inputs are finite; a program needn't handle non-finite values.
Results may differ from a plain program's by a relative error of at most 0.0003.
Values sent between devices are 32-bit elements; how exact they have to be, the bound alone decides.
No kernel may reach another device: no remote copies, remote signals or barrier semaphores. Data moves between devices by JAX's collectives and lax.ppermute only.
A program may use at most 64 MiB of HBM per device.

v0:
```python
import jax
import jax.numpy as jnp
from jax import lax
from jax.sharding import PartitionSpec as P

LEVELS = 5
STEPS = 2


soften_sq = 0.0004
fine_step = 0.03125


def predict(star_state, elapsed):
    interval = elapsed[None, :]
    position = star_state[0:3] + interval * (
        star_state[3:6] + interval * (0.5 * star_state[6:9] + interval * star_state[9:12] / 6.0)
    )
    velocity = star_state[3:6] + interval * (star_state[6:9] + 0.5 * interval * star_state[9:12])
    return jnp.concatenate([position, velocity], axis=0)


def pair_block(targets, sources):
    delta_pos = sources[0:3, None, :] - targets[0:3, :, None]
    delta_vel = sources[3:6, None, :] - targets[3:6, :, None]
    dist_sq = (
        delta_pos[0] * delta_pos[0]
        + delta_pos[1] * delta_pos[1]
        + delta_pos[2] * delta_pos[2]
        + soften_sq
    )
    inverse = lax.rsqrt(dist_sq)
    inv_sq = inverse * inverse
    weight = sources[6][None, :] * inverse * inv_sq
    radial = (
        (delta_pos[0] * delta_vel[0] + delta_pos[1] * delta_vel[1] + delta_pos[2] * delta_vel[2])
        * inv_sq
        * 3.0
    )
    acceleration = jnp.sum(weight[None] * delta_pos, axis=2)
    jerk_sum = jnp.sum(weight[None] * (delta_vel - radial[None] * delta_pos), axis=2)
    return jnp.concatenate([acceleration, jerk_sum], axis=0)


def over_sources(targets, sources):
    count_src = sources.shape[1]
    width = 512
    blocks = sources.reshape(7, count_src // width, width).transpose(1, 0, 2)

    def accumulate(running, portion):
        return (running + pair_block(targets, portion), None)

    init = jnp.zeros((6, targets.shape[1]), jnp.float32)
    running, unused = lax.scan(accumulate, init, blocks)
    return running


def pair_forces(targets, sources):
    return over_sources(targets, sources)


def correct(old_state, predicted_rows, forces):
    acc_old = old_state[6:9]
    jerk_old = old_state[9:12]
    acc_new = forces[0:3]
    jerk_new = forces[3:6]
    snap_term = (-6.0 * (acc_old - acc_new) - fine_step * (4.0 * jerk_old + 2.0 * jerk_new)) / (
        fine_step * fine_step
    )
    crackle = (12.0 * (acc_old - acc_new) + 6.0 * fine_step * (jerk_old + jerk_new)) / (
        fine_step * fine_step * fine_step
    )
    position = (
        predicted_rows[0:3] + fine_step**4 / 24.0 * snap_term + fine_step**5 / 120.0 * crackle
    )
    velocity = predicted_rows[3:6] + fine_step**3 / 6.0 * snap_term + fine_step**4 / 24.0 * crackle
    return jnp.concatenate([position, velocity, acc_new, jerk_new], axis=0)


def per_device(star_state, masses, phases, levels, active_list, active_count):
    shard_size = star_state.shape[1]
    total_stars = shard_size * lax.axis_size("src")
    weights = masses / total_stars
    slot_count = active_list.shape[0]
    live = jnp.arange(slot_count, dtype=jnp.int32) < active_count[0]
    write_index = jnp.where(live, active_list, shard_size)
    tick_count = jnp.left_shift(jnp.int32(1), LEVELS - 1 - levels).astype(jnp.float32)
    state_now = star_state
    for substep in range(STEPS):
        elapsed = (
            jnp.where(levels == LEVELS - 1, 1.0, phases * (tick_count - STEPS) + (substep + 1))
            * fine_step
        )
        predicted = predict(state_now, elapsed)
        sources = jnp.concatenate([predicted, weights[None, :]], axis=0)
        targets = predicted[:, active_list]
        forces = pair_forces(targets, lax.all_gather(sources, "src", axis=1, tiled=True))
        new_state = correct(state_now[:, active_list], targets, forces)
        all_new, all_index = (
            lax.all_gather(new_state, "act", axis=1, tiled=True),
            lax.all_gather(write_index, "act", axis=0, tiled=True),
        )
        state_now = state_now.at[:, all_index].set(all_new, mode="drop")
    return state_now


def solution(mesh):
    in_specs = (
        P(None, ("groups", "src")),
        P(("groups", "src")),
        P(("groups", "src")),
        P(("groups", "src")),
        P(("groups", "src", "act")),
        P(("groups", "src", "act")),
    )
    out_specs = P(None, ("groups", "src"))
    return jax.shard_map(
        per_device, mesh=mesh, in_specs=in_specs, out_specs=out_specs, check_vma=False
    )
```

profile of v0, /device:TPU:0, one launch (start us, length us, event | category | flops | bytes accessed | tf_op | source)
XLA Modules:
  0.0 61.3 jit_solution(9982953898039574721)
XLA Ops:
  0.0 0.7 %fusion.13 = (f32[512]{0:T(512)S(1)}, f32[512]{0:T(512)S(1)}, pred[512]{0:T(512)(128)(4,1)S(1)}) fusion(f32[512]{0:T(512)} %param.12, s32[512]{0:T(512)} %param.13), kind=kLoop, calls=%fused_computation.72 | loop fusion | flops 4608 | bytes 8704 | tf_op jit(solution)/shard_map/mul | solution.py:91
  0.7 0.9 %multiply_add_fusion.3 = (f32[3,512]{1,0:T(4,128)S(1)}, f32[3,512]{1,0:T(4,128)S(1)}) fusion(f32[12,512]{1,0:T(8,128)} %param.10, f32[512]{0:T(512)S(1)} %get-tuple-element.168, f32[512]{0:T(512)S(1)} %get-tuple-element.167), kind=kLoop, calls=%fused_computation.51 | loop fusion | flops 18432 | bytes 40960 | tf_op jit(solution)/shard_map/add | solution.py:16
  1.8 0.6 %copy-done.3 = u32[32]{0:T(128)S(1)} copy-done((u32[32]{0:T(128)S(1)}, u32[32]{0:T(128)}, u32[]{:S(2)}) %copy-start.3) | copy-done | bytes 152
  2.4 0.6 dynamic-slice
  4.3 0.6 %copy-done.2 = s32[64]{0:T(128)S(1)} copy-done((s32[64]{0:T(128)S(1)}, s32[64]{0:T(128)}, u32[]{:S(2)}) %copy-start.2) | copy-done | bytes 280
  5.1 0.6 gather_fusion
  5.7 0.6 copy-done.1
  6.4 14.9 %all_gather.17 = f32[7,2048]{1,0:T(8,128)S(1)} all-gather(f32[7,512]{1,0:T(8,128)S(1)} %pad_maximum_fusion.1), channel_id=1, replica_groups=mesh['groups'=2,'src'=4,'act'=4] {'src'}, dimensions={1}, use_global_device_ids=true | all-gather | bytes 71680 | tf_op jit(solution)/shard_map/all_gather | solution.py:97
  21.3 2.4 %while.22 = (s32[]{:T(128)}, f32[6,64]{1,0:T(8,128)S(1)}, f32[4,7,512]{2,1,0:T(8,128)S(1)}, f32[6,64]{1,0:T(8,128)S(1)}, s32[]{:T(128)}, /*index=5*/s32[]{:T(128)}, s32[]{}, s32[]{}) while((s32[]{:T(128)}, f32[6,64]{1,0:T(8,128)S(1)}, f32[4,7,512]{2,1,0:T(8,128)S(1)}, f32[6,64]{1,0:T(8,128)S(1)}, s32[]{:T(128)}, ...), condition=%wide.region_3.4_spmd.clone, body=%wide.region_0.3_spmd.clone.sunk | while | flops 1508101 | bytes 2164871 | solution.py:54
  21.6 0.3 multiply_reduce_fusion.6
  22.2 0.3 multiply_reduce_fusion.6
  22.8 0.3 multiply_reduce_fusion.6
  23.9 0.6 gather_fusion.1
  24.6 5.2 %all-gather = f32[4,64,12]{1,2,0:T(8,128)S(1)} all-gather(f32[1,64,12]{1,2,0:T(8,128)S(1)} %maximum_bitcast_fusion), channel_id=1, replica_groups=mesh['groups'=2,'src'=4,'act'=4] {'act'}, dimensions={0}, use_global_device_ids=true | all-gather | bytes 15360 | tf_op jit(solution)/shard_map/all_gather | solution.py:100
  29.9 4.9 %all-reduce = s32[256]{0:T(256)S(1)} all-reduce(s32[256]{0:T(256)S(1)} %get-tuple-element.170), channel_id=1, replica_groups=mesh['groups'=2,'src'=4,'act'=4] {'act'}, use_global_device_ids=true, to_apply=%add | all-reduce | flops 256 | bytes 2048
  34.8 1.3 %scatter_fusion = f32[12,512]{0,1:T(8,128)S(1)} fusion(f32[12,512]{0,1:T(8,128)S(1)} %copy.145, s32[256]{0:T(256)S(1)} %compare_select_fusion, f32[256,12]{1,0:T(8,128)S(1)} %bitcast.60), kind=kCustom, calls=%fused_computation.4 | custom fusion | bytes 37888 | tf_op jit(solution)/shard_map/scatter | solution.py:103
  37.1 0.6 gather_fusion.2
  37.8 13.1 %all_gather.19 = f32[7,2048]{1,0:T(8,128)S(1)} all-gather(f32[7,512]{1,0:T(8,128)S(1)} %pad_maximum_fusion), channel_id=1, replica_groups=mesh['groups'=2,'src'=4,'act'=4] {'src'}, dimensions={1}, use_global_device_ids=true | all-gather | bytes 71680 | tf_op jit(solution)/shard_map/all_gather | solution.py:97
  50.9 2.4 %while.23 = (s32[]{:T(128)}, f32[6,64]{1,0:T(8,128)S(1)}, f32[4,7,512]{2,1,0:T(8,128)S(1)}, f32[6,64]{1,0:T(8,128)S(1)}, s32[]{:T(128)}, /*index=5*/s32[]{:T(128)}, s32[]{}, s32[]{}) while((s32[]{:T(128)}, f32[6,64]{1,0:T(8,128)S(1)}, f32[4,7,512]{2,1,0:T(8,128)S(1)}, f32[6,64]{1,0:T(8,128)S(1)}, s32[]{:T(128)}, ...), condition=%wide.region_8.9_spmd.clone, body=%wide.region_5.8_spmd.clone.sunk | while | flops 1508101 | bytes 2164871 | solution.py:54
  51.2 0.3 multiply_reduce_fusion.7
  53.3 0.6 gather_fusion.3
  54.0 5.2 %all-gather.1 = f32[4,64,12]{1,2,0:T(8,128)S(1)} all-gather(f32[1,64,12]{1,2,0:T(8,128)S(1)} %maximum_bitcast_fusion.1), channel_id=1, replica_groups=mesh['groups'=2,'src'=4,'act'=4] {'act'}, dimensions={0}, use_global_device_ids=true | all-gather | bytes 15360 | tf_op jit(solution)/shard_map/all_gather | solution.py:100
  59.3 1.3 %scatter_fusion.1 = f32[12,512]{0,1:T(8,128)S(1)} fusion(f32[12,512]{0,1:T(8,128)S(1)} %scatter_fusion, s32[256]{0:T(256)S(1)} %compare_select_fusion, f32[256,12]{1,0:T(8,128)S(1)} %bitcast.61), kind=kCustom, calls=%fused_computation.5 | custom fusion | bytes 37888 | tf_op jit(solution)/shard_map/scatter | solution.py:103
  60.6 0.7 %copy.157 = f32[12,512]{1,0:T(8,128)} copy(f32[12,512]{0,1:T(8,128)S(1)} %scatter_fusion.1) | data formatting | bytes 49152 | tf_op jit(solution)/shard_map/scatter | solution.py:103
  (90 shorter events, 5.1 us)
Async XLA Ops:
  1.8 0.7 %copy-start.3 = (u32[32]{0:T(128)S(1)}, u32[32]{0:T(128)}, u32[]{:S(2)}) copy-start(u32[32]{0:T(128)} %constant.95) | copy-start | bytes 388
  4.3 0.7 %copy-start.2 = (s32[64]{0:T(128)S(1)}, s32[64]{0:T(128)}, u32[]{:S(2)}) copy-start(s32[64]{0:T(128)} %param.14) | copy-start | bytes 772
  5.7 0.7 %copy-start.1 = (f32[512]{0:T(512)S(1)}, f32[512]{0:T(512)}, u32[]{:S(2)}) copy-start(f32[512]{0:T(512)} %param.11) | copy-start | bytes 6148
  21.3 2.4 %copy-start = (f32[12,512]{1,0:T(8,128)S(1)}, f32[12,512]{1,0:T(8,128)}, u32[]{:S(2)}) copy-start(f32[12,512]{1,0:T(8,128)} %param.10) | copy-start | bytes 73732
where the time goes:
time: 61.7 us; the launch traced here: 61.3 us
  blocking collectives  43.4 us (70%)
  local copies, waits for them, and re-layouts  10.1 us (16%)
  other arithmetic  5.94 us (10%)
  between operations  1.49 us (2%)
    all_gather x2, blocking collectives, per_device(): lax.all_gather(sources, 'src', axis=1, tiled=True)  28.1 us
    all_gather x2, blocking collectives, per_device(): lax.all_gather(new_state, 'act', axis=1, tiled=True)  10.4 us
    unnamed x1, blocking collectives  4.94 us
    scatter x3, local copies, waits for them, and re-layouts, per_device(): state_now = state_now.at[:, all_index].set(all_new, mode='drop')  3.27 us
    unnamed x15, local copies, waits for them, and re-layouts  3.09 us
    reduce_sum x8, other arithmetic, pair_block(): acceleration = jnp.sum(weight[None] * delta_pos, axis=2)  2.3 us
    gather x4, local copies, waits for them, and re-layouts, per_device(): new_state = correct(state_now[:, active_list], targets, forces)  1.35 us
    gather x4, local copies, waits for them, and re-layouts, per_device(): targets = predicted[:, active_list]  1.34 us

commit v1 on v0

--- a/solution.py
+++ b/solution.py
@@ -1,10 +1,13 @@
 import jax
 import jax.numpy as jnp
 from jax import lax
+from jax.experimental import pallas as pl
+from jax.experimental.pallas import tpu as pltpu
 from jax.sharding import PartitionSpec as P
 
 LEVELS = 5
 STEPS = 2
+MAX_DIRECT = 8
 
 
 soften_sq = 0.0004
@@ -55,29 +58,31 @@
     return running
 
 
-def pair_forces(targets, sources):
-    return over_sources(targets, sources)
-
-
-def correct(old_state, predicted_rows, forces):
-    acc_old = old_state[6:9]
-    jerk_old = old_state[9:12]
-    acc_new = forces[0:3]
-    jerk_new = forces[3:6]
+def corrected(acc_old, jerk_old, position, velocity, acc_new, jerk_new):
     snap_term = (-6.0 * (acc_old - acc_new) - fine_step * (4.0 * jerk_old + 2.0 * jerk_new)) / (
         fine_step * fine_step
     )
     crackle = (12.0 * (acc_old - acc_new) + 6.0 * fine_step * (jerk_old + jerk_new)) / (
         fine_step * fine_step * fine_step
     )
-    position = (
-        predicted_rows[0:3] + fine_step**4 / 24.0 * snap_term + fine_step**5 / 120.0 * crackle
-    )
-    velocity = predicted_rows[3:6] + fine_step**3 / 6.0 * snap_term + fine_step**4 / 24.0 * crackle
-    return jnp.concatenate([position, velocity, acc_new, jerk_new], axis=0)
-
-
-def per_device(star_state, masses, phases, levels, active_list, active_count):
+    new_position = position + fine_step**4 / 24.0 * snap_term + fine_step**5 / 120.0 * crackle
+    new_velocity = velocity + fine_step**3 / 6.0 * snap_term + fine_step**4 / 24.0 * crackle
+    return new_position, new_velocity
+
+
+def correct(old_state, predicted_rows, forces):
+    new_position, new_velocity = corrected(
+        old_state[6:9],
+        old_state[9:12],
+        predicted_rows[0:3],
+        predicted_rows[3:6],
+        forces[0:3],
+        forces[3:6],
+    )
+    return jnp.concatenate([new_position, new_velocity, forces], axis=0)
+
+
+def gather_per_device(star_state, masses, phases, levels, active_list, active_count):
     shard_size = star_state.shape[1]
     total_stars = shard_size * lax.axis_size("src")
     weights = masses / total_stars
@@ -94,7 +99,7 @@
         predicted = predict(state_now, elapsed)
         sources = jnp.concatenate([predicted, weights[None, :]], axis=0)
         targets = predicted[:, active_list]
-        forces = pair_forces(targets, lax.all_gather(sources, "src", axis=1, tiled=True))
+        forces = over_sources(targets, lax.all_gather(sources, "src", axis=1, tiled=True))
         new_state = correct(state_now[:, active_list], targets, forces)
         all_new, all_index = (
             lax.all_gather(new_state, "act", axis=1, tiled=True),
@@ -102,6 +107,193 @@
         )
         state_now = state_now.at[:, all_index].set(all_new, mode="drop")
     return state_now
+
+
+def three_terms(x):
+    high = x.astype(jnp.bfloat16)
+    rest = x - high.astype(jnp.float32)
+    middle = rest.astype(jnp.bfloat16)
+    low = (rest - middle.astype(jnp.float32)).astype(jnp.bfloat16)
+    return jnp.concatenate([high, middle, low], axis=0)
+
+
+def add_terms(y):
+    rows = y.shape[0] // 3
+    return (y[0:rows] + y[rows : 2 * rows]) + y[2 * rows : 3 * rows]
+
+
+def advance(position, velocity, acceleration, jerk, step):
+    ahead = position + step * (velocity + step * (0.5 * acceleration + step * jerk / 6.0))
+    speed = velocity + step * (acceleration + 0.5 * step * jerk)
+    return ahead, speed
+
+
+def prepare(slots, total_stars, state_ref, mass_ref, phase_ref, level_ref, out_ref, place_ref):
+    size = state_ref.shape[1]
+    level = level_ref[...]
+    active = level == LEVELS - 1
+    mask = jnp.where(active, 1.0, 0.0)
+    blocks = size // 128
+    grouped = jnp.concatenate(
+        [mask[:, 128 * b : 128 * (b + 1)] for b in range(blocks)]
+        + [jnp.zeros((16 - blocks, 128), jnp.float32)],
+        axis=0,
+    ).astype(jnp.bfloat16)
+    lane_in = lax.broadcasted_iota(jnp.int32, (128, 256), 0)
+    lane_out = lax.broadcasted_iota(jnp.int32, (128, 256), 1)
+    counting = jnp.where((lane_in <= lane_out) | (lane_out >= 128), 1.0, 0.0).astype(jnp.bfloat16)
+    counts = jnp.dot(grouped, counting, preferred_element_type=jnp.float32)
+    so_far = []
+    before = jnp.zeros((1, 128), jnp.float32)
+    for b in range(blocks):
+        so_far.append(counts[b : b + 1, 0:128] + before)
+        before = before + counts[b : b + 1, 128:256]
+    rank = jnp.concatenate(so_far, axis=1)
+    total = jnp.concatenate([before] * blocks, axis=1)
+    star = lax.broadcasted_iota(jnp.int32, (1, size), 1).astype(jnp.float32)
+    place = jnp.where(active, rank - 1.0, total + star - rank)
+    place_ref[0:1, :] = place
+    place_ref[1:2, :] = mask
+    place_ref[2:8, :] = jnp.zeros((6, size), jnp.float32)
+
+    tick_count = jnp.left_shift(jnp.int32(1), LEVELS - 1 - level).astype(jnp.float32)
+    offset = phase_ref[...] * (tick_count - STEPS)
+    position, velocity = state_ref[0:3, :], state_ref[3:6, :]
+    acceleration, jerk = state_ref[6:9, :], state_ref[9:12, :]
+    rows = []
+    for substep in range(STEPS):
+        elapsed = jnp.where(active, 1.0, offset + (substep + 1)) * fine_step
+        rows.extend(advance(position, velocity, acceleration, jerk, elapsed))
+        if substep == 0:
+            rows.append(mass_ref[...] / total_stars)
+            rows.append(mask)
+    rows.append(jnp.zeros((2, size), jnp.float32))
+    rows.extend([acceleration, jerk, jnp.zeros((10, size), jnp.float32)])
+    terms = three_terms(jnp.concatenate(rows, axis=0))
+    slot = lax.broadcasted_iota(jnp.int32, (size, size), 0).astype(jnp.float32)
+    chosen = jnp.where(slot == place, 1.0, 0.0).astype(jnp.bfloat16)
+    moved = add_terms(
+        lax.dot_general(
+            terms, chosen, (((1,), (1,)), ((), ())), preferred_element_type=jnp.float32
+        )
+    )
+    out_ref[...] = moved[0:16]
+    across = size // slots
+    for k in range(6):
+        out_ref[14 + k // across : 15 + k // across, slots * (k % across) : slots * (k % across + 1)] = (
+            moved[16 + k : 17 + k, 0:slots]
+        )
+
+
+def pair_terms(source, target, sums):
+    sx, sy, sz, su, sv, sw, weight = source
+    tx, ty, tz, tu, tv, tw = target
+    dx, dy, dz = sx - tx, sy - ty, sz - tz
+    du, dv, dw = su - tu, sv - tv, sw - tw
+    inverse = lax.rsqrt(dx * dx + dy * dy + dz * dz + soften_sq)
+    inv_sq = inverse * inverse
+    pull = weight * inverse * inv_sq
+    radial = (dx * du + dy * dv + dz * dw) * (inv_sq * 3.0)
+    ax, ay, az, jx, jy, jz = sums
+    return (
+        ax + pull * dx,
+        ay + pull * dy,
+        az + pull * dz,
+        jx + pull * (du - radial * dx),
+        jy + pull * (dv - radial * dy),
+        jz + pull * (dw - radial * dz),
+    )
+
+
+def pair_sums(columns_ref, targets, unroll):
+    count = columns_ref.shape[0] // 8
+    lanes = targets[0].shape[1]
+    spread = [
+        [jnp.broadcast_to(t[r : r + 1], (8, lanes)) for r in range(6)] for t in targets
+    ]
+
+    def body(step, sums):
+        for inner in range(unroll):
+            group = columns_ref[pl.ds((step * unroll + inner) * 8, 8), :]
+            source = [jnp.broadcast_to(group[:, r : r + 1], (8, lanes)) for r in range(7)]
+            sums = tuple(pair_terms(source, t, s) for t, s in zip(spread, sums))
+        return sums
+
+    zero = jnp.zeros((8, lanes), jnp.float32)
+    sums = lax.fori_loop(0, count // unroll, body, tuple((zero,) * 6 for _ in targets))
+    return [jnp.concatenate([jnp.sum(q, axis=0, keepdims=True) for q in s], axis=0) for s in sums]
+
+
+def advance_stars(slots, shards, *refs):
+    sent = refs[:shards]
+    state_ref, place_ref, out_ref, columns_ref = refs[shards:]
+    size = state_ref.shape[1]
+    across = size // slots
+    for d in range(shards):
+        columns_ref[d * size : (d + 1) * size, :] = jnp.transpose(sent[d][0:8, :])
+    targets = [sent[d][0:6, 0:slots] for d in range(shards)]
+    forces = pair_sums(columns_ref, targets, 8)
+    own = None
+    for d in range(shards):
+        first = [
+            sent[d][14 + k // across : 15 + k // across, slots * (k % across) : slots * (k % across + 1)]
+            for k in range(6)
+        ]
+        first = jnp.concatenate(first, axis=0)
+        acceleration, jerk = forces[d][0:3], forces[d][3:6]
+        position, velocity = corrected(
+            first[0:3], first[3:6], targets[d][0:3], targets[d][3:6], acceleration, jerk
+        )
+        ahead, speed = advance(position, velocity, acceleration, jerk, fine_step)
+        active = sent[d][7:8, 0:slots] > 0.5
+        still = sent[d][8:14, 0:slots]
+        again = jnp.where(active, jnp.concatenate([ahead, speed], axis=0), still)
+        if d == 0:
+            own = again
+        later = jnp.concatenate([again, sent[d][8:14, slots:size]], axis=1)
+        later = jnp.concatenate([later, sent[d][6:8, :]], axis=0)
+        columns_ref[d * size : (d + 1) * size, :] = jnp.transpose(later)
+    second = pair_sums(columns_ref, [own], 16)[0]
+    position, velocity = corrected(
+        forces[0][0:3], forces[0][3:6], own[0:3], own[3:6], second[0:3], second[3:6]
+    )
+    new_rows = jnp.concatenate(
+        [position, velocity, second, jnp.zeros((4, slots), jnp.float32)], axis=0
+    )
+    slot = lax.broadcasted_iota(jnp.int32, (slots, size), 0).astype(jnp.float32)
+    chosen = jnp.where(slot == place_ref[0:1, :], 1.0, 0.0).astype(jnp.bfloat16)
+    back = add_terms(jnp.dot(three_terms(new_rows), chosen, preferred_element_type=jnp.float32))
+    out_ref[...] = jnp.where(place_ref[1:2, :] > 0.5, back[0:12], state_ref[...])
+
+
+def direct_per_device(star_state, masses, phases, levels, active_list, active_count):
+    del active_count
+    size = star_state.shape[1]
+    shards = lax.axis_size("src")
+    slots = 2 * active_list.shape[0]
+    whole = pl.BlockSpec(memory_space=pltpu.VMEM)
+    message, place = pl.pallas_call(
+        lambda *refs: prepare(slots, size * shards, *refs),
+        out_shape=(
+            jax.ShapeDtypeStruct((16, size), jnp.float32),
+            jax.ShapeDtypeStruct((8, size), jnp.float32),
+        ),
+        in_specs=[whole] * 4,
+        out_specs=(whole, whole),
+        name="prepare",
+    )(star_state, masses.reshape(1, size), phases.reshape(1, size), levels.reshape(1, size))
+    sent = [message]
+    for shift in range(1, shards):
+        pairs = [(d, (d + shift) % shards) for d in range(shards)]
+        sent.append(lax.ppermute(message, "src", pairs))
+    return pl.pallas_call(
+        lambda *refs: advance_stars(slots, shards, *refs),
+        out_shape=jax.ShapeDtypeStruct((12, size), jnp.float32),
+        in_specs=[whole] * (shards + 2),
+        out_specs=whole,
+        scratch_shapes=[pltpu.VMEM((shards * size, 8), jnp.float32)],
+        name="advance_stars",
+    )(*sent, star_state, place)
 
 
 def solution(mesh):
@@ -114,6 +306,11 @@
         P(("groups", "src", "act")),
     )
     out_specs = P(None, ("groups", "src"))
+    few = mesh.shape["src"] <= MAX_DIRECT
     return jax.shard_map(
-        per_device, mesh=mesh, in_specs=in_specs, out_specs=out_specs, check_vma=False
-    )
+        direct_per_device if few else gather_per_device,
+        mesh=mesh,
+        in_specs=in_specs,
+        out_specs=out_specs,
+        check_vma=False,
+    )

time: 61.7 us -> 29 us (0.47)
  blocking collectives: 43.4 us -> 0 us
  Pallas kernels: 0 us -> 17.2 us
  local copies, waits for them, and re-layouts: 10.1 us -> 0.61 us
  starting transfers between devices: 0 us -> 6.09 us
  other arithmetic: 5.94 us -> 0 us
  waiting for transfers between devices: 0 us -> 4.91 us
  between operations: 1.49 us -> 0.01 us
    all_gather x4 -> x0, blocking collectives: 38.4 us -> none  [the longest x2 28.1 us: per_device(): lax.all_gather(sources, 'src', axis=1, tiled=True)]
    pallas_call x0 -> x2, Pallas kernels: none -> 17.2 us  [the longest x1 15.3 us: direct_per_device(): pl.pallas_call(lambda *refs: advance_stars(slots, shards, *refs), out_sha...]
    ppermute x0 -> x3, starting transfers between devices: none -> 6.09 us  [direct_per_device(): sent.append(lax.ppermute(message, 'src', pairs))]
    unnamed x1 -> x0, blocking collectives: 4.94 us -> none
    ppermute x0 -> x3, waiting for transfers between devices: none -> 4.91 us  [direct_per_device(): sent.append(lax.ppermute(message, 'src', pairs))]
    scatter x3 -> x0, local copies, waits for them, and re-layouts: 3.27 us -> none  [per_device(): state_now = state_now.at[:, all_index].set(all_new, mode='drop')]
    gather x8 -> x0, local copies, waits for them, and re-layouts: 2.69 us -> none  [the longest x4 1.35 us: per_device(): new_state = correct(state_now[:, active_list], targets, forces)]
    unnamed x15 -> x6, local copies, waits for them, and re-layouts: 3.09 us -> 0.61 us
  transfers between devices with their start and end apart: 0 -> 3, of which waited for: 0 -> 3; matrix products, arithmetic and copies ran while one was open for 0% -> 0% of each run, Pallas kernels for 0% -> 0%
where the time goes in v1:
time: 29 us; the launch traced here: 28.8 us
  Pallas kernels  17.2 us (59%)
  starting transfers between devices  6.09 us (21%)
  waiting for transfers between devices  4.91 us (17%)
  local copies, waits for them, and re-layouts  0.61 us (2%)
    pallas_call x1, Pallas kernels, direct_per_device(): pl.pallas_call(lambda *refs: advance_stars(slots, shards, *refs), out_sha...  15.3 us
    ppermute x3, starting transfers between devices, direct_per_device(): sent.append(lax.ppermute(message, 'src', pairs))  6.09 us
    ppermute x3, waiting for transfers between devices, direct_per_device(): sent.append(lax.ppermute(message, 'src', pairs))  4.91 us
    pallas_call x1, Pallas kernels, direct_per_device(): pl.pallas_call(lambda *refs: prepare(slots, size * shards, *refs), out_sh...  1.84 us
    unnamed x6, local copies, waits for them, and re-layouts  0.61 us
  transfers between devices with their start and end apart: 3, of which 3 were waited for; matrix products, arithmetic and copies ran while one was open for 0% of the time, Pallas kernels for 0%

profile of v1, /device:TPU:0, one launch (start us, length us, event | category | flops | bytes accessed | tf_op | source)
XLA Modules:
  0.0 28.8 jit_solution(7179539059311235971)
XLA Ops:
  0.0 1.8 %prepare.1 = (f32[16,512]{1,0:T(8,128)}, f32[8,512]{1,0:T(8,128)}) custom-call(f32[12,512]{1,0:T(8,128)} %refs_4_.1, f32[1,512]{1,0:T(1,128)} %bitcast.3, f32[1,512]{1,0:T(1,128)} %bitcast.4, s32[1,512]{1,0:T(1,128)} %bitcast.5), custom_call_target="tpu_custom_call" | custom-call | tf_op jit(solution)/shard_map/prepare/pallas_call | solution.py:275
  1.8 5.1 %collective-permute-start.2 = (f32[16,512]{1,0:T(8,128)}, f32[16,512]{1,0:T(8,128)S(1)}, u32[]{:S(2)}, u32[]{:S(2)}) collective-permute-start(f32[16,512]{1,0:T(8,128)} %get-tuple-element.7.refs_0_), channel_id=1, source_target_pairs={{0,12},{4,0},{8,4},{12,8},{1,13},{5,1},{9,5},{13,9},{2,14},{6,2},{... | collective-permute-start | bytes 98312 | tf_op jit(solution)/shard_map/ppermute | solution.py:288
  6.9 0.0 collective-permute-start.1
  6.9 1.0 %collective-permute-start = (f32[16,512]{1,0:T(8,128)}, f32[16,512]{1,0:T(8,128)S(1)}, u32[]{:S(2)}, u32[]{:S(2)}) collective-permute-start(f32[16,512]{1,0:T(8,128)} %get-tuple-element.7.refs_0_), channel_id=1, source_target_pairs={{0,4},{4,8},{8,12},{12,0},{1,5},{5,9},{9,13},{13,1},{2,6},{6,10},{... | collective-permute-start | bytes 98312 | tf_op jit(solution)/shard_map/ppermute | solution.py:288
  7.9 0.9 %collective-permute-done.2.refs_3_ = f32[16,512]{1,0:T(8,128)S(1)} collective-permute-done((f32[16,512]{1,0:T(8,128)}, f32[16,512]{1,0:T(8,128)S(1)}, u32[]{:S(2)}, u32[]{:S(2)}) %collective-permute-start.2) | collective-permute-done | bytes 32800 | tf_op jit(solution)/shard_map/ppermute | solution.py:288
  8.8 0.0 copy-start
  8.8 3.1 %collective-permute-done.1.refs_2_ = f32[16,512]{1,0:T(8,128)S(1)} collective-permute-done((f32[16,512]{1,0:T(8,128)}, f32[16,512]{1,0:T(8,128)S(1)}, u32[]{:S(2)}, u32[]{:S(2)}) %collective-permute-start.1) | collective-permute-done | bytes 32800 | tf_op jit(solution)/shard_map/ppermute | solution.py:288
  11.9 0.0 copy-start.1
  11.9 0.9 %collective-permute-done.refs_1_ = f32[16,512]{1,0:T(8,128)S(1)} collective-permute-done((f32[16,512]{1,0:T(8,128)}, f32[16,512]{1,0:T(8,128)S(1)}, u32[]{:S(2)}, u32[]{:S(2)}) %collective-permute-start) | collective-permute-done | bytes 32800 | tf_op jit(solution)/shard_map/ppermute | solution.py:288
  12.8 0.0 copy-start.2
  12.8 0.0 copy-done
  12.8 0.0 copy-done.1
  12.8 0.6 %copy-done.2 = f32[16,512]{1,0:T(8,128)} copy-done((f32[16,512]{1,0:T(8,128)}, f32[16,512]{1,0:T(8,128)S(1)}, u32[]{:S(2)}) %copy-start.2) | copy-done | bytes 32792
  13.4 15.3 %advance_stars.1 = f32[12,512]{1,0:T(8,128)} custom-call(f32[16,512]{1,0:T(8,128)} %get-tuple-element.7.refs_0_, f32[16,512]{1,0:T(8,128)} %copy-done.2, f32[16,512]{1,0:T(8,128)} %copy-done.1, f32[16,512]{1,0:T(8,128)} %copy-done, f32[12,512]{1,0:T(8,128)} %refs_4_.1, f32[8,512]{1,0:T(8,128)} %get-tuple-element.8.refs_5_), custom_call_target="tpu_custom_call" | custom-call | tf_op jit(solution)/shard_map/advance_stars/pallas_call | solution.py:289
Async XLA Ops:
  1.8 7.0 %collective-permute-start.2 = (f32[16,512]{1,0:T(8,128)}, f32[16,512]{1,0:T(8,128)S(1)}, u32[]{:S(2)}, u32[]{:S(2)}) collective-permute-start(f32[16,512]{1,0:T(8,128)} %get-tuple-element.7.refs_0_), channel_id=1, source_target_pairs={{0,12},{4,0},{8,4},{12,8},{1,13},{5,1},{9,5},{13,9},{2,14},{6,2},{... | collective-permute-start | bytes 98312 | tf_op jit(solution)/shard_map/ppermute | solution.py:288
  6.9 5.0 %collective-permute-start.1 = (f32[16,512]{1,0:T(8,128)}, f32[16,512]{1,0:T(8,128)S(1)}, u32[]{:S(2)}, u32[]{:S(2)}) collective-permute-start(f32[16,512]{1,0:T(8,128)} %get-tuple-element.7.refs_0_), channel_id=1, source_target_pairs={{0,8},{4,12},{8,0},{12,4},{1,9},{5,13},{9,1},{13,5},{2,10},{6,14},... | collective-permute-start | bytes 98312 | tf_op jit(solution)/shard_map/ppermute | solution.py:288
  6.9 5.9 %collective-permute-start = (f32[16,512]{1,0:T(8,128)}, f32[16,512]{1,0:T(8,128)S(1)}, u32[]{:S(2)}, u32[]{:S(2)}) collective-permute-start(f32[16,512]{1,0:T(8,128)} %get-tuple-element.7.refs_0_), channel_id=1, source_target_pairs={{0,4},{4,8},{8,12},{12,0},{1,5},{5,9},{9,13},{13,1},{2,6},{6,10},{... | collective-permute-start | bytes 98312 | tf_op jit(solution)/shard_map/ppermute | solution.py:288
  8.8 4.0 %copy-start = (f32[16,512]{1,0:T(8,128)}, f32[16,512]{1,0:T(8,128)S(1)}, u32[]{:S(2)}) copy-start(f32[16,512]{1,0:T(8,128)S(1)} %collective-permute-done.2.refs_3_) | copy-start | bytes 98308
  11.9 0.9 %copy-start.1 = (f32[16,512]{1,0:T(8,128)}, f32[16,512]{1,0:T(8,128)S(1)}, u32[]{:S(2)}) copy-start(f32[16,512]{1,0:T(8,128)S(1)} %collective-permute-done.1.refs_2_) | copy-start | bytes 98308
  12.8 0.6 %copy-start.2 = (f32[16,512]{1,0:T(8,128)}, f32[16,512]{1,0:T(8,128)S(1)}, u32[]{:S(2)}) copy-start(f32[16,512]{1,0:T(8,128)S(1)} %collective-permute-done.refs_1_) | copy-start | bytes 98308

commit v2 on v1

--- a/solution.py
+++ b/solution.py
@@ -190,7 +190,7 @@
     tx, ty, tz, tu, tv, tw = target
     dx, dy, dz = sx - tx, sy - ty, sz - tz
     du, dv, dw = su - tu, sv - tv, sw - tw
-    inverse = lax.rsqrt(dx * dx + dy * dy + dz * dz + soften_sq)
+    inverse = lax.rsqrt(dx * dx + dy * dy + (dz * dz + soften_sq))
     inv_sq = inverse * inverse
     pull = weight * inverse * inv_sq
     radial = (dx * du + dy * dv + dz * dw) * (inv_sq * 3.0)
@@ -205,60 +205,92 @@
     )
 
 
-def pair_sums(columns_ref, targets, unroll):
-    count = columns_ref.shape[0] // 8
-    lanes = targets[0].shape[1]
-    spread = [
-        [jnp.broadcast_to(t[r : r + 1], (8, lanes)) for r in range(6)] for t in targets
-    ]
-
-    def body(step, sums):
-        for inner in range(unroll):
-            group = columns_ref[pl.ds((step * unroll + inner) * 8, 8), :]
-            source = [jnp.broadcast_to(group[:, r : r + 1], (8, lanes)) for r in range(7)]
-            sums = tuple(pair_terms(source, t, s) for t, s in zip(spread, sums))
-        return sums
-
-    zero = jnp.zeros((8, lanes), jnp.float32)
-    sums = lax.fori_loop(0, count // unroll, body, tuple((zero,) * 6 for _ in targets))
-    return [jnp.concatenate([jnp.sum(q, axis=0, keepdims=True) for q in s], axis=0) for s in sums]
+def spread_sources(rows, spread_ref, first):
+    for c in range(rows.shape[1] // 128):
+        for r in range(7):
+            spread_ref[r, 8 * (first + c) : 8 * (first + c + 1), :] = jnp.broadcast_to(
+                rows[r : r + 1, 128 * c : 128 * (c + 1)], (8, 128)
+            )
+
+
+def spread_targets(rows, spread_ref, first):
+    columns = jnp.transpose(rows)
+    count = columns.shape[0]
+    for r in range(6):
+        spread_ref[r, first : first + count, :] = jnp.broadcast_to(
+            columns[:, r : r + 1], (count, 128)
+        )
+
+
+def pair_sums(sources_ref, targets_ref, partial_ref, sums_ref, chunks, count, together):
+    def reduce(place):
+        for g in range(together):
+            for q in range(6):
+                part = partial_ref[(g * 6 + q) * 8 : (g * 6 + q + 1) * 8, :]
+                sums_ref[pl.ds(place + 8 * g, 8), q : q + 1] = jnp.sum(part, axis=1, keepdims=True)
+
+    def body(step, unused):
+        base = pl.multiple_of(step * (8 * together), 8)
+        reduce(base)
+        for g in range(together):
+            target = [targets_ref[r, pl.ds(base + 8 * g, 8), :] for r in range(6)]
+            sums = (jnp.zeros((8, 128), jnp.float32),) * 6
+            for c in range(chunks):
+                source = [sources_ref[r, 8 * c : 8 * (c + 1), :] for r in range(7)]
+                sums = pair_terms(source, target, sums)
+            for q in range(6):
+                partial_ref[(g * 6 + q) * 8 : (g * 6 + q + 1) * 8, :] = sums[q]
+        return unused
+
+    lax.fori_loop(0, count // (8 * together), body, 0)
+    reduce(count)
 
 
 def advance_stars(slots, shards, *refs):
     sent = refs[:shards]
-    state_ref, place_ref, out_ref, columns_ref = refs[shards:]
+    state_ref, place_ref, out_ref, sources_ref, targets_ref, partial_ref, sums_ref = refs[shards:]
     size = state_ref.shape[1]
     across = size // slots
+    chunks = size // 128
+    together = 4
+    lead = 8 * together
     for d in range(shards):
-        columns_ref[d * size : (d + 1) * size, :] = jnp.transpose(sent[d][0:8, :])
-    targets = [sent[d][0:6, 0:slots] for d in range(shards)]
-    forces = pair_sums(columns_ref, targets, 8)
+        spread_sources(sent[d][0:8, :], sources_ref, d * chunks)
+        spread_targets(sent[d][0:8, 0:slots], targets_ref, d * slots)
+    partial_ref[...] = jnp.zeros_like(partial_ref)
+    pair_sums(
+        sources_ref, targets_ref, partial_ref, sums_ref, shards * chunks, shards * slots, together
+    )
     own = None
     for d in range(shards):
+        forces = jnp.transpose(sums_ref[lead + d * slots : lead + (d + 1) * slots, :])
         first = [
             sent[d][14 + k // across : 15 + k // across, slots * (k % across) : slots * (k % across + 1)]
             for k in range(6)
         ]
         first = jnp.concatenate(first, axis=0)
-        acceleration, jerk = forces[d][0:3], forces[d][3:6]
         position, velocity = corrected(
-            first[0:3], first[3:6], targets[d][0:3], targets[d][3:6], acceleration, jerk
-        )
-        ahead, speed = advance(position, velocity, acceleration, jerk, fine_step)
+            first[0:3], first[3:6], sent[d][0:3, 0:slots], sent[d][3:6, 0:slots], forces[0:3], forces[3:6]
+        )
+        ahead, speed = advance(position, velocity, forces[0:3], forces[3:6], fine_step)
         active = sent[d][7:8, 0:slots] > 0.5
         still = sent[d][8:14, 0:slots]
         again = jnp.where(active, jnp.concatenate([ahead, speed], axis=0), still)
         if d == 0:
-            own = again
+            own = jnp.concatenate([again, jnp.zeros((2, slots), jnp.float32)], axis=0)
+            before = forces
         later = jnp.concatenate([again, sent[d][8:14, slots:size]], axis=1)
-        later = jnp.concatenate([later, sent[d][6:8, :]], axis=0)
-        columns_ref[d * size : (d + 1) * size, :] = jnp.transpose(later)
-    second = pair_sums(columns_ref, [own], 16)[0]
+        spread_sources(
+            jnp.concatenate([later, sent[d][6:8, :]], axis=0), sources_ref, d * chunks
+        )
+    spread_targets(own, targets_ref, 0)
+    pair_sums(sources_ref, targets_ref, partial_ref, sums_ref, shards * chunks, slots, together)
+    second = jnp.transpose(sums_ref[lead : lead + slots, :])
     position, velocity = corrected(
-        forces[0][0:3], forces[0][3:6], own[0:3], own[3:6], second[0:3], second[3:6]
+        before[0:3], before[3:6], own[0:3], own[3:6], second[0:3], second[3:6]
     )
     new_rows = jnp.concatenate(
-        [position, velocity, second, jnp.zeros((4, slots), jnp.float32)], axis=0
+        [position, velocity, second[0:6], jnp.zeros((4, slots), jnp.float32)], axis=0
     )
     slot = lax.broadcasted_iota(jnp.int32, (slots, size), 0).astype(jnp.float32)
     chosen = jnp.where(slot == place_ref[0:1, :], 1.0, 0.0).astype(jnp.bfloat16)
@@ -280,18 +312,26 @@
         ),
         in_specs=[whole] * 4,
         out_specs=(whole, whole),
+        compiler_params=pltpu.CompilerParams(vmem_limit_bytes=16 * 2**20),
         name="prepare",
     )(star_state, masses.reshape(1, size), phases.reshape(1, size), levels.reshape(1, size))
-    sent = [message]
-    for shift in range(1, shards):
+    sent = []
+    for shift in range(shards - 1, 0, -1):
         pairs = [(d, (d + shift) % shards) for d in range(shards)]
-        sent.append(lax.ppermute(message, "src", pairs))
+        sent.insert(0, lax.ppermute(message, "src", pairs))
+    sent.insert(0, message)
     return pl.pallas_call(
         lambda *refs: advance_stars(slots, shards, *refs),
         out_shape=jax.ShapeDtypeStruct((12, size), jnp.float32),
         in_specs=[whole] * (shards + 2),
         out_specs=whole,
-        scratch_shapes=[pltpu.VMEM((shards * size, 8), jnp.float32)],
+        scratch_shapes=[
+            pltpu.VMEM((7, shards * size // 16, 128), jnp.float32),
+            pltpu.VMEM((6, shards * slots, 128), jnp.float32),
+            pltpu.VMEM((24 * 8, 128), jnp.float32),
+            pltpu.VMEM((shards * slots + 32, 8), jnp.float32),
+        ],
+        compiler_params=pltpu.CompilerParams(vmem_limit_bytes=16 * 2**20),
         name="advance_stars",
     )(*sent, star_state, place)
 

time: 29 us -> 22.7 us (0.78)
  Pallas kernels: 17.2 us -> 9.46 us
  local copies, waits for them, and re-layouts: 0.61 us -> 2.13 us
    pallas_call x1, Pallas kernels: 15.3 us -> 9.04 us  [direct_per_device(): pl.pallas_call(lambda *refs: advance_stars(slots, shards, *refs), out_sha...]
    unnamed x6 -> x8, local copies, waits for them, and re-layouts: 0.61 us -> 2.13 us
    pallas_call x1, Pallas kernels: 1.84 us -> 0.42 us  [direct_per_device(): pl.pallas_call(lambda *refs: prepare(slots, size * shards, *refs), out_sh...]
where the time goes in v2:
time: 22.7 us; the launch traced here: 22.5 us
  Pallas kernels  9.46 us (42%)
  starting transfers between devices  6.15 us (27%)
  waiting for transfers between devices  4.7 us (21%)
  local copies, waits for them, and re-layouts  2.13 us (9%)
    pallas_call x1, Pallas kernels, direct_per_device(): pl.pallas_call(lambda *refs: advance_stars(slots, shards, *refs), out_sha...  9.04 us
    ppermute x3, starting transfers between devices, direct_per_device(): sent.insert(0, lax.ppermute(message, 'src', pairs))  6.15 us
    ppermute x3, waiting for transfers between devices, direct_per_device(): sent.insert(0, lax.ppermute(message, 'src', pairs))  4.7 us
    unnamed x8, local copies, waits for them, and re-layouts  2.13 us
  transfers between devices with their start and end apart: 3, of which 3 were waited for; matrix products, arithmetic and copies ran while one was open for 0% of the time, Pallas kernels for 0%

profile of v2, /device:TPU:0, one launch (start us, length us, event | category | flops | bytes accessed | tf_op | source)
XLA Modules:
  0.0 22.5 jit_solution(12744870791018537729)
XLA Ops:
  0.0 0.0 copy-start.2
  0.0 0.0 copy-start.1
  0.0 0.7 %copy-done.2 = f32[512]{0:T(512)S(1)} copy-done((f32[512]{0:T(512)S(1)}, f32[512]{0:T(512)}, u32[]{:S(2)}) %copy-start.2) | copy-done | bytes 2072
  0.7 0.0 copy-done.1
  0.7 0.0 copy-start
  0.7 0.8 %copy-done = f32[12,512]{1,0:T(8,128)S(1)} copy-done((f32[12,512]{1,0:T(8,128)S(1)}, f32[12,512]{1,0:T(8,128)}, u32[]{:S(2)}) %copy-start) | copy-done | bytes 24600
  1.5 0.0 copy-start.3
  1.5 0.7 %copy-done.3 = s32[512]{0:T(512)S(1)} copy-done((s32[512]{0:T(512)S(1)}, s32[512]{0:T(512)}, u32[]{:S(2)}) %copy-start.3) | copy-done | bytes 2072
  2.1 0.4 %prepare.1 = (f32[16,512]{1,0:T(8,128)S(1)}, f32[8,512]{1,0:T(8,128)S(1)}) custom-call(f32[12,512]{1,0:T(8,128)S(1)} %copy-done, f32[1,512]{1,0:T(1,128)S(1)} %bitcast.3, f32[1,512]{1,0:T(1,128)S(1)} %bitcast.4, s32[1,512]{1,0:T(1,128)S(1)} %bitcast.5), custom_call_target="tpu_custom_call" | custom-call | tf_op jit(solution)/shard_map/prepare/pallas_call | solution.py:307
  2.6 5.1 %collective-permute-start.2 = (f32[16,512]{1,0:T(8,128)S(1)}, f32[16,512]{1,0:T(8,128)S(1)}, u32[]{:S(2)}, u32[]{:S(2)}) collective-permute-start(f32[16,512]{1,0:T(8,128)S(1)} %get-tuple-element.7.refs_0_), channel_id=1, source_target_pairs={{0,12},{4,0},{8,4},{12,8},{1,13},{5,1},{9,5},{13,9},{2,14},{6,2},{... | collective-permute-start | bytes 98312 | tf_op jit(solution)/shard_map/ppermute | solution.py:321
  7.7 0.0 collective-permute-start.1
  7.7 1.0 %collective-permute-start = (f32[16,512]{1,0:T(8,128)S(1)}, f32[16,512]{1,0:T(8,128)S(1)}, u32[]{:S(2)}, u32[]{:S(2)}) collective-permute-start(f32[16,512]{1,0:T(8,128)S(1)} %get-tuple-element.7.refs_0_), channel_id=1, source_target_pairs={{0,4},{4,8},{8,12},{12,0},{1,5},{5,9},{9,13},{13,1},{2,6},{6,10},{... | collective-permute-start | bytes 98312 | tf_op jit(solution)/shard_map/ppermute | solution.py:321
  8.7 0.6 %collective-permute-done.2.refs_3_ = f32[16,512]{1,0:T(8,128)S(1)} collective-permute-done((f32[16,512]{1,0:T(8,128)S(1)}, f32[16,512]{1,0:T(8,128)S(1)}, u32[]{:S(2)}, u32[]{:S(2)}) %collective-permute-start.2) | collective-permute-done | bytes 32800 | tf_op jit(solution)/shard_map/ppermute | solution.py:321
  9.3 3.2 %collective-permute-done.1.refs_2_ = f32[16,512]{1,0:T(8,128)S(1)} collective-permute-done((f32[16,512]{1,0:T(8,128)S(1)}, f32[16,512]{1,0:T(8,128)S(1)}, u32[]{:S(2)}, u32[]{:S(2)}) %collective-permute-start.1) | collective-permute-done | bytes 32800 | tf_op jit(solution)/shard_map/ppermute | solution.py:321
  12.5 0.9 %collective-permute-done.refs_1_ = f32[16,512]{1,0:T(8,128)S(1)} collective-permute-done((f32[16,512]{1,0:T(8,128)S(1)}, f32[16,512]{1,0:T(8,128)S(1)}, u32[]{:S(2)}, u32[]{:S(2)}) %collective-permute-start) | collective-permute-done | bytes 32800 | tf_op jit(solution)/shard_map/ppermute | solution.py:321
  13.4 9.0 %advance_stars.1 = f32[12,512]{1,0:T(8,128)} custom-call(f32[16,512]{1,0:T(8,128)S(1)} %get-tuple-element.7.refs_0_, f32[16,512]{1,0:T(8,128)S(1)} %collective-permute-done.refs_1_, f32[16,512]{1,0:T(8,128)S(1)} %collective-permute-done.1.refs_2_, f32[16,512]{1,0:T(8,128)S(1)} %collective-permute-done.2.refs_3_, f32[12,512]{1,0:T(8,128)S(1)} %copy-done, ...), custom_call_target="tpu_custom_call" | custom-call | tf_op jit(solution)/shard_map/advance_stars/pallas_call | solution.py:323
Async XLA Ops:
  0.0 0.7 %copy-start.2 = (f32[512]{0:T(512)S(1)}, f32[512]{0:T(512)}, u32[]{:S(2)}) copy-start(f32[512]{0:T(512)} %param.8) | copy-start | bytes 6148
  0.0 0.7 %copy-start.1 = (f32[512]{0:T(512)S(1)}, f32[512]{0:T(512)}, u32[]{:S(2)}) copy-start(f32[512]{0:T(512)} %param.7) | copy-start | bytes 6148
  0.7 0.8 %copy-start = (f32[12,512]{1,0:T(8,128)S(1)}, f32[12,512]{1,0:T(8,128)}, u32[]{:S(2)}) copy-start(f32[12,512]{1,0:T(8,128)} %refs_4_.1) | copy-start | bytes 73732
  1.5 0.7 %copy-start.3 = (s32[512]{0:T(512)S(1)}, s32[512]{0:T(512)}, u32[]{:S(2)}) copy-start(s32[512]{0:T(512)} %param.9) | copy-start | bytes 6148
  2.6 6.7 %collective-permute-start.2 = (f32[16,512]{1,0:T(8,128)S(1)}, f32[16,512]{1,0:T(8,128)S(1)}, u32[]{:S(2)}, u32[]{:S(2)}) collective-permute-start(f32[16,512]{1,0:T(8,128)S(1)} %get-tuple-element.7.refs_0_), channel_id=1, source_target_pairs={{0,12},{4,0},{8,4},{12,8},{1,13},{5,1},{9,5},{13,9},{2,14},{6,2},{... | collective-permute-start | bytes 98312 | tf_op jit(solution)/shard_map/ppermute | solution.py:321
  7.7 4.8 %collective-permute-start.1 = (f32[16,512]{1,0:T(8,128)S(1)}, f32[16,512]{1,0:T(8,128)S(1)}, u32[]{:S(2)}, u32[]{:S(2)}) collective-permute-start(f32[16,512]{1,0:T(8,128)S(1)} %get-tuple-element.7.refs_0_), channel_id=1, source_target_pairs={{0,8},{4,12},{8,0},{12,4},{1,9},{5,13},{9,1},{13,5},{2,10},{6,14},... | collective-permute-start | bytes 98312 | tf_op jit(solution)/shard_map/ppermute | solution.py:321
  7.7 5.7 %collective-permute-start = (f32[16,512]{1,0:T(8,128)S(1)}, f32[16,512]{1,0:T(8,128)S(1)}, u32[]{:S(2)}, u32[]{:S(2)}) collective-permute-start(f32[16,512]{1,0:T(8,128)S(1)} %get-tuple-element.7.refs_0_), channel_id=1, source_target_pairs={{0,4},{4,8},{8,12},{12,0},{1,5},{5,9},{9,13},{13,1},{2,6},{6,10},{... | collective-permute-start | bytes 98312 | tf_op jit(solution)/shard_map/ppermute | solution.py:321

commit v3 on v2

--- a/solution.py
+++ b/solution.py
@@ -128,7 +128,17 @@
     return ahead, speed
 
 
-def prepare(slots, total_stars, state_ref, mass_ref, phase_ref, level_ref, out_ref, place_ref):
+def prepare(slots, total_stars, *refs):
+    out_ref, place_ref = refs[4:6]
+    copies = [
+        pltpu.make_async_copy(far, near, refs[10].at[k])
+        for k, (far, near) in enumerate(zip(refs[0:4], refs[6:10]))
+    ]
+    for copy in copies:
+        copy.start()
+    for copy in copies:
+        copy.wait()
+    state_ref, mass_ref, phase_ref, level_ref = refs[6:10]
     size = state_ref.shape[1]
     level = level_ref[...]
     active = level == LEVELS - 1
@@ -247,7 +257,7 @@
 
 
 def advance_stars(slots, shards, *refs):
-    sent = refs[:shards]
+    sent = (refs[0],) + refs[shards - 1 : 0 : -1]
     state_ref, place_ref, out_ref, sources_ref, targets_ref, partial_ref, sums_ref = refs[shards:]
     size = state_ref.shape[1]
     across = size // slots
@@ -310,16 +320,27 @@
             jax.ShapeDtypeStruct((16, size), jnp.float32),
             jax.ShapeDtypeStruct((8, size), jnp.float32),
         ),
-        in_specs=[whole] * 4,
+        in_specs=[pl.BlockSpec(memory_space=pltpu.HBM)] * 4,
         out_specs=(whole, whole),
+        scratch_shapes=[
+            pltpu.VMEM((12, size), jnp.float32),
+            pltpu.VMEM((1, size), jnp.float32),
+            pltpu.VMEM((1, size), jnp.float32),
+            pltpu.VMEM((1, size), jnp.int32),
+            pltpu.SemaphoreType.DMA((4,)),
+        ],
         compiler_params=pltpu.CompilerParams(vmem_limit_bytes=16 * 2**20),
         name="prepare",
-    )(star_state, masses.reshape(1, size), phases.reshape(1, size), levels.reshape(1, size))
-    sent = []
+    )(
+        *(
+            pltpu.with_memory_space_constraint(x, pltpu.HBM)
+            for x in (star_state, masses.reshape(1, size), phases.reshape(1, size), levels.reshape(1, size))
+        )
+    )
+    sent = [message]
     for shift in range(shards - 1, 0, -1):
         pairs = [(d, (d + shift) % shards) for d in range(shards)]
-        sent.insert(0, lax.ppermute(message, "src", pairs))
-    sent.insert(0, message)
+        sent.append(lax.ppermute(message, "src", pairs))
     return pl.pallas_call(
         lambda *refs: advance_stars(slots, shards, *refs),
         out_shape=jax.ShapeDtypeStruct((12, size), jnp.float32),

time: 22.7 us -> 20.2 us (0.89)
  waiting for transfers between devices: 4.7 us -> 2.56 us
  local copies, waits for them, and re-layouts: 2.13 us -> 0.01 us
  Pallas kernels: 9.46 us -> 10.4 us
  starting transfers between devices: 6.15 us -> 7.04 us
    ppermute x3, waiting for transfers between devices: 4.7 us -> 2.56 us  [direct_per_device(): sent.append(lax.ppermute(message, 'src', pairs))]
    unnamed x8 -> x2, local copies, waits for them, and re-layouts: 2.13 us -> 0.01 us
    ppermute x3, starting transfers between devices: 6.15 us -> 7.04 us  [direct_per_device(): sent.append(lax.ppermute(message, 'src', pairs))]
    pallas_call x1, Pallas kernels: 0.42 us -> 1.32 us  [direct_per_device(): pl.pallas_call(lambda *refs: prepare(slots, size * shards, *refs), out_sh...]
  transfers between devices with their start and end apart: 3 -> 3, of which waited for: 3 -> 2; matrix products, arithmetic and copies ran while one was open for 0% -> 0% of each run, Pallas kernels for 0% -> 0%
where the time goes in v3:
time: 20.2 us; the launch traced here: 20 us
  Pallas kernels  10.4 us (51%)
  starting transfers between devices  7.04 us (35%)
  waiting for transfers between devices  2.56 us (13%)
    pallas_call x1, Pallas kernels, direct_per_device(): pl.pallas_call(lambda *refs: advance_stars(slots, shards, *refs), out_sha...  9.04 us
    ppermute x3, starting transfers between devices, direct_per_device(): sent.append(lax.ppermute(message, 'src', pairs))  7.04 us
    ppermute x3, waiting for transfers between devices, direct_per_device(): sent.append(lax.ppermute(message, 'src', pairs))  2.56 us
    pallas_call x1, Pallas kernels, direct_per_device(): pl.pallas_call(lambda *refs: prepare(slots, size * shards, *refs), out_sh...  1.32 us
  transfers between devices with their start and end apart: 3, of which 2 were waited for; matrix products, arithmetic and copies ran while one was open for 0% of the time, Pallas kernels for 0%

profile of v3, /device:TPU:0, one launch (start us, length us, event | category | flops | bytes accessed | tf_op | source)
XLA Modules:
  0.0 20.0 jit_solution(12118802522033371792)
XLA Ops:
  0.0 0.0 copy-start
  0.0 1.3 %prepare.1 = (f32[16,512]{1,0:T(8,128)S(1)}, f32[8,512]{1,0:T(8,128)S(1)}) custom-call(f32[12,512]{1,0:T(8,128)} %refs_4_.1, f32[1,512]{1,0:T(1,128)} %bitcast.3, f32[1,512]{1,0:T(1,128)} %bitcast.4, s32[1,512]{1,0:T(1,128)} %bitcast.5), custom_call_target="tpu_custom_call" | custom-call | tf_op jit(solution)/shard_map/prepare/pallas_call | solution.py:317
  1.3 3.1 %collective-permute-start.2 = (f32[16,512]{1,0:T(8,128)S(1)}, f32[16,512]{1,0:T(8,128)S(1)}, u32[]{:S(2)}, u32[]{:S(2)}) collective-permute-start(f32[16,512]{1,0:T(8,128)S(1)} %get-tuple-element.7.refs_0_), channel_id=1, source_target_pairs={{0,4},{4,8},{8,12},{12,0},{1,5},{5,9},{9,13},{13,1},{2,6},{6,10},{... | collective-permute-start | bytes 98312 | tf_op jit(solution)/shard_map/ppermute | solution.py:343
  4.4 2.6 %collective-permute-start.1 = (f32[16,512]{1,0:T(8,128)S(1)}, f32[16,512]{1,0:T(8,128)S(1)}, u32[]{:S(2)}, u32[]{:S(2)}) collective-permute-start(f32[16,512]{1,0:T(8,128)S(1)} %get-tuple-element.7.refs_0_), channel_id=1, source_target_pairs={{0,8},{4,12},{8,0},{12,4},{1,9},{5,13},{9,1},{13,5},{2,10},{6,14},... | collective-permute-start | bytes 98312 | tf_op jit(solution)/shard_map/ppermute | solution.py:343
  7.0 1.3 %collective-permute-start = (f32[16,512]{1,0:T(8,128)S(1)}, f32[16,512]{1,0:T(8,128)S(1)}, u32[]{:S(2)}, u32[]{:S(2)}) collective-permute-start(f32[16,512]{1,0:T(8,128)S(1)} %get-tuple-element.7.refs_0_), channel_id=1, source_target_pairs={{0,12},{4,0},{8,4},{12,8},{1,13},{5,1},{9,5},{13,9},{2,14},{6,2},{... | collective-permute-start | bytes 98312 | tf_op jit(solution)/shard_map/ppermute | solution.py:343
  8.4 0.0 collective-permute-done.2.refs_3_
  8.4 1.2 %collective-permute-done.1.refs_2_ = f32[16,512]{1,0:T(8,128)S(1)} collective-permute-done((f32[16,512]{1,0:T(8,128)S(1)}, f32[16,512]{1,0:T(8,128)S(1)}, u32[]{:S(2)}, u32[]{:S(2)}) %collective-permute-start.1) | collective-permute-done | bytes 32800 | tf_op jit(solution)/shard_map/ppermute | solution.py:343
  9.6 1.3 %collective-permute-done.refs_1_ = f32[16,512]{1,0:T(8,128)S(1)} collective-permute-done((f32[16,512]{1,0:T(8,128)S(1)}, f32[16,512]{1,0:T(8,128)S(1)}, u32[]{:S(2)}, u32[]{:S(2)}) %collective-permute-start) | collective-permute-done | bytes 32800 | tf_op jit(solution)/shard_map/ppermute | solution.py:343
  10.9 0.0 copy-done
  10.9 9.0 %advance_stars.1 = f32[12,512]{1,0:T(8,128)} custom-call(f32[16,512]{1,0:T(8,128)S(1)} %get-tuple-element.7.refs_0_, f32[16,512]{1,0:T(8,128)S(1)} %collective-permute-done.refs_1_, f32[16,512]{1,0:T(8,128)S(1)} %collective-permute-done.1.refs_2_, f32[16,512]{1,0:T(8,128)S(1)} %collective-permute-done.2.refs_3_, f32[12,512]{1,0:T(8,128)S(1)} %copy-done, ...), custom_call_target="tpu_custom_call" | custom-call | tf_op jit(solution)/shard_map/advance_stars/pallas_call | solution.py:344
Async XLA Ops:
  0.0 10.9 %copy-start = (f32[12,512]{1,0:T(8,128)S(1)}, f32[12,512]{1,0:T(8,128)}, u32[]{:S(2)}) copy-start(f32[12,512]{1,0:T(8,128)} %refs_4_.1) | copy-start | bytes 73732
  1.3 7.0 %collective-permute-start.2 = (f32[16,512]{1,0:T(8,128)S(1)}, f32[16,512]{1,0:T(8,128)S(1)}, u32[]{:S(2)}, u32[]{:S(2)}) collective-permute-start(f32[16,512]{1,0:T(8,128)S(1)} %get-tuple-element.7.refs_0_), channel_id=1, source_target_pairs={{0,4},{4,8},{8,12},{12,0},{1,5},{5,9},{9,13},{13,1},{2,6},{6,10},{... | collective-permute-start | bytes 98312 | tf_op jit(solution)/shard_map/ppermute | solution.py:343
  4.4 5.2 %collective-permute-start.1 = (f32[16,512]{1,0:T(8,128)S(1)}, f32[16,512]{1,0:T(8,128)S(1)}, u32[]{:S(2)}, u32[]{:S(2)}) collective-permute-start(f32[16,512]{1,0:T(8,128)S(1)} %get-tuple-element.7.refs_0_), channel_id=1, source_target_pairs={{0,8},{4,12},{8,0},{12,4},{1,9},{5,13},{9,1},{13,5},{2,10},{6,14},... | collective-permute-start | bytes 98312 | tf_op jit(solution)/shard_map/ppermute | solution.py:343
  7.0 3.9 %collective-permute-start = (f32[16,512]{1,0:T(8,128)S(1)}, f32[16,512]{1,0:T(8,128)S(1)}, u32[]{:S(2)}, u32[]{:S(2)}) collective-permute-start(f32[16,512]{1,0:T(8,128)S(1)} %get-tuple-element.7.refs_0_), channel_id=1, source_target_pairs={{0,12},{4,0},{8,4},{12,8},{1,13},{5,1},{9,5},{13,9},{2,14},{6,2},{... | collective-permute-start | bytes 98312 | tf_op jit(solution)/shard_map/ppermute | solution.py:343

commit v4 on v3

--- a/solution.py
+++ b/solution.py
@@ -1,3 +1,5 @@
+import functools
+
 import jax
 import jax.numpy as jnp
 from jax import lax
@@ -223,81 +225,136 @@
             )
 
 
-def spread_targets(rows, spread_ref, first):
+def spread_targets(rows, spread_ref):
     columns = jnp.transpose(rows)
-    count = columns.shape[0]
     for r in range(6):
-        spread_ref[r, first : first + count, :] = jnp.broadcast_to(
-            columns[:, r : r + 1], (count, 128)
-        )
-
-
-def pair_sums(sources_ref, targets_ref, partial_ref, sums_ref, chunks, count, together):
+        spread_ref[r] = jnp.broadcast_to(columns[:, r : r + 1], (columns.shape[0], 128))
+
+
+def run_pairs(groups, slots, together, finish, partial_ref, sums_ref):
+    lead = 8 * together
+
     def reduce(place):
         for g in range(together):
-            for q in range(6):
-                part = partial_ref[(g * 6 + q) * 8 : (g * 6 + q + 1) * 8, :]
-                sums_ref[pl.ds(place + 8 * g, 8), q : q + 1] = jnp.sum(part, axis=1, keepdims=True)
+            for j in range(len(groups)):
+                for q in range(6):
+                    row = ((g * len(groups) + j) * 6 + q) * 8
+                    sums_ref[pl.ds(j * (slots + lead) + place + 8 * g, 8), q : q + 1] = jnp.sum(
+                        partial_ref[row : row + 8, :], axis=1, keepdims=True
+                    )
 
     def body(step, unused):
-        base = pl.multiple_of(step * (8 * together), 8)
-        reduce(base)
+        base = pl.multiple_of(step * lead, 8)
+        if finish:
+            reduce(base)
         for g in range(together):
-            target = [targets_ref[r, pl.ds(base + 8 * g, 8), :] for r in range(6)]
-            sums = (jnp.zeros((8, 128), jnp.float32),) * 6
-            for c in range(chunks):
-                source = [sources_ref[r, 8 * c : 8 * (c + 1), :] for r in range(7)]
-                sums = pair_terms(source, target, sums)
-            for q in range(6):
-                partial_ref[(g * 6 + q) * 8 : (g * 6 + q + 1) * 8, :] = sums[q]
+            here = pl.ds(base + 8 * g, 8)
+            for j, (target_ref, before_ref, sources, after_ref) in enumerate(groups):
+                target = [target_ref[r, here, :] for r in range(6)]
+                if before_ref is None:
+                    sums = (jnp.zeros((8, 128), jnp.float32),) * 6
+                else:
+                    sums = tuple(before_ref[q, here, :] for q in range(6))
+                for source_ref in sources:
+                    for c in range(source_ref.shape[1] // 8):
+                        source = [source_ref[r, 8 * c : 8 * (c + 1), :] for r in range(7)]
+                        sums = pair_terms(source, target, sums)
+                for q in range(6):
+                    if finish:
+                        row = ((g * len(groups) + j) * 6 + q) * 8
+                        partial_ref[row : row + 8, :] = sums[q]
+                    else:
+                        after_ref[q, here, :] = sums[q]
         return unused
 
-    lax.fori_loop(0, count // (8 * together), body, 0)
-    reduce(count)
-
-
-def advance_stars(slots, shards, *refs):
-    sent = (refs[0],) + refs[shards - 1 : 0 : -1]
-    state_ref, place_ref, out_ref, sources_ref, targets_ref, partial_ref, sums_ref = refs[shards:]
+    if finish:
+        used = together * len(groups) * 48
+        partial_ref[0:used, :] = jnp.zeros((used, 128), jnp.float32)
+    lax.fori_loop(0, slots // lead, body, 0)
+    if not finish:
+        return None
+    reduce(slots)
+    return [
+        jnp.transpose(sums_ref[j * (slots + lead) + lead : (j + 1) * (slots + lead), :])
+        for j in range(len(groups))
+    ]
+
+
+def pair_groups(sent, sources, targets, before, after, slots):
+    for d in range(len(before), len(targets)):
+        fresh = sent[d - len(before)]
+        spread_sources(fresh[0:8, :], sources[d], 0)
+        spread_targets(fresh[0:8, 0:slots], targets[d])
+    groups = []
+    for d in range(len(targets)):
+        if d < len(before):
+            groups.append((targets[d], before[d], sources[len(before) :], after[d]))
+        else:
+            groups.append((targets[d], None, sources, after[d]))
+    return groups
+
+
+def meet(slots, known, fresh, together, *refs):
+    sent, refs = refs[:fresh], refs[fresh:]
+    every = known + fresh
+    old_sources, old_targets, before = refs[:known], refs[known : 2 * known], refs[2 * known : 3 * known]
+    refs = refs[3 * known :]
+    new_sources, new_targets, after = refs[:fresh], refs[fresh : 2 * fresh], refs[2 * fresh :]
+    groups = pair_groups(
+        sent, old_sources + new_sources, old_targets + new_targets, before, after, slots
+    )
+    run_pairs(groups, slots, together, False, None, None)
+
+
+def finish(slots, known, fresh, together, *refs):
+    every = known + fresh
+    sent, refs = refs[:every], refs[every:]
+    old_sources, old_targets, before = refs[:known], refs[known : 2 * known], refs[2 * known : 3 * known]
+    state_ref, place_ref, out_ref = refs[3 * known : 3 * known + 3]
+    refs = refs[3 * known + 3 :]
+    new_sources, new_targets = refs[:fresh], refs[fresh : 2 * fresh]
+    later_ref, partial_ref, sums_ref = refs[2 * fresh :]
+    groups = pair_groups(
+        sent[known:],
+        old_sources + new_sources,
+        old_targets + new_targets,
+        before,
+        (None,) * every,
+        slots,
+    )
     size = state_ref.shape[1]
     across = size // slots
     chunks = size // 128
-    together = 4
-    lead = 8 * together
-    for d in range(shards):
-        spread_sources(sent[d][0:8, :], sources_ref, d * chunks)
-        spread_targets(sent[d][0:8, 0:slots], targets_ref, d * slots)
-    partial_ref[...] = jnp.zeros_like(partial_ref)
-    pair_sums(
-        sources_ref, targets_ref, partial_ref, sums_ref, shards * chunks, shards * slots, together
-    )
-    own = None
-    for d in range(shards):
-        forces = jnp.transpose(sums_ref[lead + d * slots : lead + (d + 1) * slots, :])
+    forces = run_pairs(groups, slots, together, True, partial_ref, sums_ref)
+    for d in range(every):
         first = [
             sent[d][14 + k // across : 15 + k // across, slots * (k % across) : slots * (k % across + 1)]
             for k in range(6)
         ]
         first = jnp.concatenate(first, axis=0)
         position, velocity = corrected(
-            first[0:3], first[3:6], sent[d][0:3, 0:slots], sent[d][3:6, 0:slots], forces[0:3], forces[3:6]
-        )
-        ahead, speed = advance(position, velocity, forces[0:3], forces[3:6], fine_step)
+            first[0:3],
+            first[3:6],
+            sent[d][0:3, 0:slots],
+            sent[d][3:6, 0:slots],
+            forces[d][0:3],
+            forces[d][3:6],
+        )
+        ahead, speed = advance(position, velocity, forces[d][0:3], forces[d][3:6], fine_step)
         active = sent[d][7:8, 0:slots] > 0.5
         still = sent[d][8:14, 0:slots]
         again = jnp.where(active, jnp.concatenate([ahead, speed], axis=0), still)
         if d == 0:
             own = jnp.concatenate([again, jnp.zeros((2, slots), jnp.float32)], axis=0)
-            before = forces
         later = jnp.concatenate([again, sent[d][8:14, slots:size]], axis=1)
-        spread_sources(
-            jnp.concatenate([later, sent[d][6:8, :]], axis=0), sources_ref, d * chunks
-        )
-    spread_targets(own, targets_ref, 0)
-    pair_sums(sources_ref, targets_ref, partial_ref, sums_ref, shards * chunks, slots, together)
-    second = jnp.transpose(sums_ref[lead : lead + slots, :])
+        spread_sources(jnp.concatenate([later, sent[d][6:8, :]], axis=0), later_ref, d * chunks)
+    target_ref = new_targets[0]
+    spread_targets(own, target_ref)
+    second = run_pairs(
+        [(target_ref, None, (later_ref,), None)], slots, 4, True, partial_ref, sums_ref
+    )[0]
     position, velocity = corrected(
-        before[0:3], before[3:6], own[0:3], own[3:6], second[0:3], second[3:6]
+        forces[0][0:3], forces[0][3:6], own[0:3], own[3:6], second[0:3], second[3:6]
     )
     new_rows = jnp.concatenate(
         [position, velocity, second[0:6], jnp.zeros((4, slots), jnp.float32)], axis=0
@@ -338,23 +395,47 @@
         )
     )
     sent = [message]
-    for shift in range(shards - 1, 0, -1):
+    for shift in range(1, shards):
         pairs = [(d, (d + shift) % shards) for d in range(shards)]
         sent.append(lax.ppermute(message, "src", pairs))
+
+    limit = pltpu.CompilerParams(vmem_limit_bytes=16 * 2**20)
+    source_shape = jax.ShapeDtypeStruct((7, size // 16, 128), jnp.float32)
+    target_shape = jax.ShapeDtypeStruct((6, slots, 128), jnp.float32)
+    sources, targets, sums = [], [], []
+    known = 0
+    stages = [min(2, shards - 1)] + [1] * (shards - 3)
+    for fresh in stages:
+        every = known + fresh
+        outs = pl.pallas_call(
+            functools.partial(meet, slots, known, fresh, 2),
+            out_shape=[source_shape] * fresh + [target_shape] * (fresh + every),
+            in_specs=[whole] * (fresh + 3 * known),
+            out_specs=[whole] * (2 * fresh + every),
+            compiler_params=limit,
+            name=f"meet_{every}",
+        )(*sent[known:every], *sources, *targets, *sums)
+        sources += outs[:fresh]
+        targets += outs[fresh : 2 * fresh]
+        sums = list(outs[2 * fresh :])
+        known = every
+    together = 2
+    rows = max(together * shards, 4) * 48
     return pl.pallas_call(
-        lambda *refs: advance_stars(slots, shards, *refs),
+        functools.partial(finish, slots, known, shards - known, together),
         out_shape=jax.ShapeDtypeStruct((12, size), jnp.float32),
-        in_specs=[whole] * (shards + 2),
+        in_specs=[whole] * (shards + 3 * known + 2),
         out_specs=whole,
-        scratch_shapes=[
+        scratch_shapes=[pltpu.VMEM(source_shape.shape, jnp.float32)] * (shards - known)
+        + [pltpu.VMEM(target_shape.shape, jnp.float32)] * (shards - known)
+        + [
             pltpu.VMEM((7, shards * size // 16, 128), jnp.float32),
-            pltpu.VMEM((6, shards * slots, 128), jnp.float32),
-            pltpu.VMEM((24 * 8, 128), jnp.float32),
-            pltpu.VMEM((shards * slots + 32, 8), jnp.float32),
+            pltpu.VMEM((rows, 128), jnp.float32),
+            pltpu.VMEM((shards * (slots + 32), 8), jnp.float32),
         ],
-        compiler_params=pltpu.CompilerParams(vmem_limit_bytes=16 * 2**20),
-        name="advance_stars",
-    )(*sent, star_state, place)
+        compiler_params=limit,
+        name="finish",
+    )(*sent, *sources, *targets, *sums, star_state, place)
 
 
 def solution(mesh):
@@ -367,7 +448,7 @@
         P(("groups", "src", "act")),
     )
     out_specs = P(None, ("groups", "src"))
-    few = mesh.shape["src"] <= MAX_DIRECT
+    few = 3 <= mesh.shape["src"] <= MAX_DIRECT
     return jax.shard_map(
         direct_per_device if few else gather_per_device,
         mesh=mesh,

time: 20.2 us -> 18.3 us (0.906)
  waiting for transfers between devices: 2.56 us -> 0.01 us
  Pallas kernels: 10.4 us -> 11 us
    ppermute x3, waiting for transfers between devices: 2.56 us -> 0.01 us  [direct_per_device(): sent.append(lax.ppermute(message, 'src', pairs))]
    pallas_call x1 -> x3, Pallas kernels: 9.04 us -> 9.81 us  [the longest x1 5.86 us: direct_per_device(): pl.pallas_call(functools.partial(finish, slots, known, shards - known, to...]
  transfers between devices with their start and end apart: 3 -> 3, of which waited for: 2 -> 0; matrix products, arithmetic and copies ran while one was open for 0% -> 0% of each run, Pallas kernels for 0% -> 22%
where the time goes in v4:
time: 18.3 us; the launch traced here: 18.2 us
  Pallas kernels  11 us (60%)
  starting transfers between devices  7.04 us (38%)
    ppermute x3, starting transfers between devices, direct_per_device(): sent.append(lax.ppermute(message, 'src', pairs))  7.04 us
    pallas_call x1, Pallas kernels, direct_per_device(): pl.pallas_call(functools.partial(finish, slots, known, shards - known, to...  5.86 us
    pallas_call x2, Pallas kernels, direct_per_device(): pl.pallas_call(functools.partial(meet, slots, known, fresh, 2), out_shape...  3.95 us
    pallas_call x1, Pallas kernels, direct_per_device(): pl.pallas_call(lambda *refs: prepare(slots, size * shards, *refs), out_sh...  1.24 us
  transfers between devices with their start and end apart: 3, of which 0 were waited for; matrix products, arithmetic and copies ran while one was open for 0% of the time, Pallas kernels for 22%

profile of v4, /device:TPU:0, one launch (start us, length us, event | category | flops | bytes accessed | tf_op | source)
XLA Modules:
  0.0 18.2 jit_solution(10364003488416252804)
XLA Ops:
  0.0 1.2 %prepare.1 = (f32[16,512]{1,0:T(8,128)S(1)}, f32[8,512]{1,0:T(8,128)S(1)}) custom-call(f32[12,512]{1,0:T(8,128)} %refs_13_.1, f32[1,512]{1,0:T(1,128)} %bitcast.3, f32[1,512]{1,0:T(1,128)} %bitcast.4, s32[1,512]{1,0:T(1,128)} %bitcast.5), custom_call_target="tpu_custom_call" | custom-call | tf_op jit(solution)/shard_map/prepare/pallas_call | solution.py:374
  1.2 3.1 %collective-permute-start = (f32[16,512]{1,0:T(8,128)S(1)}, f32[16,512]{1,0:T(8,128)S(1)}, u32[]{:S(2)}, u32[]{:S(2)}) collective-permute-start(f32[16,512]{1,0:T(8,128)S(1)} %get-tuple-element.18.refs_0_), channel_id=1, source_target_pairs={{0,4},{4,8},{8,12},{12,0},{1,5},{5,9},{9,13},{13,1},{2,6},{6,10},{... | collective-permute-start | bytes 98312 | tf_op jit(solution)/shard_map/ppermute | solution.py:400
  4.4 2.6 %collective-permute-start.1 = (f32[16,512]{1,0:T(8,128)S(1)}, f32[16,512]{1,0:T(8,128)S(1)}, u32[]{:S(2)}, u32[]{:S(2)}) collective-permute-start(f32[16,512]{1,0:T(8,128)S(1)} %get-tuple-element.18.refs_0_), channel_id=1, source_target_pairs={{0,8},{4,12},{8,0},{12,4},{1,9},{5,13},{9,1},{13,5},{2,10},{6,14},... | collective-permute-start | bytes 98312 | tf_op jit(solution)/shard_map/ppermute | solution.py:400
  6.9 1.3 %collective-permute-start.2 = (f32[16,512]{1,0:T(8,128)S(1)}, f32[16,512]{1,0:T(8,128)S(1)}, u32[]{:S(2)}, u32[]{:S(2)}) collective-permute-start(f32[16,512]{1,0:T(8,128)S(1)} %get-tuple-element.18.refs_0_), channel_id=1, source_target_pairs={{0,12},{4,0},{8,4},{12,8},{1,13},{5,1},{9,5},{13,9},{2,14},{6,2},{... | collective-permute-start | bytes 98312 | tf_op jit(solution)/shard_map/ppermute | solution.py:400
  8.3 0.0 collective-permute-done.refs_1_
  8.3 1.8 %meet_2.1 = (f32[7,32,128]{2,1,0:T(8,128)S(1)}, f32[7,32,128]{2,1,0:T(8,128)S(1)}, f32[6,128,128]{2,1,0:T(8,128)S(1)}, f32[6,128,128]{2,1,0:T(8,128)S(1)}, f32[6...) custom-call(f32[16,512]{1,0:T(8,128)S(1)} %get-tuple-element.18.refs_0_, f32[16,512]{1,0:T(8,128)S(1)} %collective-permute-done.refs_1_), custom_call_target="tpu_custom_call" | custom-call | tf_op jit(solution)/shard_map/meet_2/pallas_call | solution.py:410
  10.1 0.0 collective-permute-done.1.refs_0_.refs_2_
  10.1 0.0 copy-start
  10.1 2.1 %meet_3.1 = (f32[7,32,128]{2,1,0:T(8,128)S(1)}, f32[6,128,128]{2,1,0:T(8,128)S(1)}, f32[6,128,128]{2,1,0:T(8,128)S(1)}, f32[6,128,128]{2,1,0:T(8,128)S(1)}, f32[6,128,128]{2,1,0:T(8,128)S(1)}) custom-call(f32[16,512]{1,0:T(8,128)S(1)} %collective-permute-done.1.refs_0_.refs_2_, f32[7,32,128]{2,1,0:T(8,128)S(1)} %get-tuple-element.19.refs_1_.refs_4_, ...), custom_call_target="tpu_custom_call" | custom-call | tf_op jit(solution)/shard_map/meet_3/pallas_call | solution.py:410
  12.3 0.0 collective-permute-done.2.refs_3_
  12.3 0.0 copy-done
  12.3 5.9 %finish.1 = f32[12,512]{1,0:T(8,128)} custom-call(f32[16,512]{1,0:T(8,128)S(1)} %get-tuple-element.18.refs_0_, f32[16,512]{1,0:T(8,128)S(1)} %collective-permute-done.refs_1_, f32[16,512]{1,0:T(8,128)S(1)} %collective-permute-done.1.refs_0_.refs_2_, f32[16,512]{1,0:T(8,128)S(1)} %collective-permute-done.2.refs_3_, ...), custom_call_target="tpu_custom_call" | custom-call | tf_op jit(solution)/shard_map/finish/pallas_call | solution.py:424
Async XLA Ops:
  1.2 7.0 %collective-permute-start = (f32[16,512]{1,0:T(8,128)S(1)}, f32[16,512]{1,0:T(8,128)S(1)}, u32[]{:S(2)}, u32[]{:S(2)}) collective-permute-start(f32[16,512]{1,0:T(8,128)S(1)} %get-tuple-element.18.refs_0_), channel_id=1, source_target_pairs={{0,4},{4,8},{8,12},{12,0},{1,5},{5,9},{9,13},{13,1},{2,6},{6,10},{... | collective-permute-start | bytes 98312 | tf_op jit(solution)/shard_map/ppermute | solution.py:400
  4.4 5.8 %collective-permute-start.1 = (f32[16,512]{1,0:T(8,128)S(1)}, f32[16,512]{1,0:T(8,128)S(1)}, u32[]{:S(2)}, u32[]{:S(2)}) collective-permute-start(f32[16,512]{1,0:T(8,128)S(1)} %get-tuple-element.18.refs_0_), channel_id=1, source_target_pairs={{0,8},{4,12},{8,0},{12,4},{1,9},{5,13},{9,1},{13,5},{2,10},{6,14},... | collective-permute-start | bytes 98312 | tf_op jit(solution)/shard_map/ppermute | solution.py:400
  6.9 5.3 %collective-permute-start.2 = (f32[16,512]{1,0:T(8,128)S(1)}, f32[16,512]{1,0:T(8,128)S(1)}, u32[]{:S(2)}, u32[]{:S(2)}) collective-permute-start(f32[16,512]{1,0:T(8,128)S(1)} %get-tuple-element.18.refs_0_), channel_id=1, source_target_pairs={{0,12},{4,0},{8,4},{12,8},{1,13},{5,1},{9,5},{13,9},{2,14},{6,2},{... | collective-permute-start | bytes 98312 | tf_op jit(solution)/shard_map/ppermute | solution.py:400
  10.1 2.2 %copy-start = (f32[12,512]{1,0:T(8,128)S(1)}, f32[12,512]{1,0:T(8,128)}, u32[]{:S(2)}) copy-start(f32[12,512]{1,0:T(8,128)} %refs_13_.1) | copy-start | bytes 73732

commit v5 on v4

--- a/solution.py
+++ b/solution.py
@@ -231,7 +231,7 @@
         spread_ref[r] = jnp.broadcast_to(columns[:, r : r + 1], (columns.shape[0], 128))
 
 
-def run_pairs(groups, slots, together, finish, partial_ref, sums_ref):
+def run_pairs(groups, slots, start, count, together, finish, partial_ref, sums_ref):
     lead = 8 * together
 
     def reduce(place):
@@ -244,7 +244,7 @@
                     )
 
     def body(step, unused):
-        base = pl.multiple_of(step * lead, 8)
+        base = pl.multiple_of(start + step * lead, 8)
         if finish:
             reduce(base)
         for g in range(together):
@@ -270,10 +270,12 @@
     if finish:
         used = together * len(groups) * 48
         partial_ref[0:used, :] = jnp.zeros((used, 128), jnp.float32)
-    lax.fori_loop(0, slots // lead, body, 0)
+        if count < slots:
+            sums_ref[...] = jnp.zeros_like(sums_ref)
+    lax.fori_loop(0, count // lead, body, 0)
     if not finish:
         return None
-    reduce(slots)
+    reduce(pl.multiple_of(start + count, 8))
     return [
         jnp.transpose(sums_ref[j * (slots + lead) + lead : (j + 1) * (slots + lead), :])
         for j in range(len(groups))
@@ -294,39 +296,48 @@
     return groups
 
 
-def meet(slots, known, fresh, together, *refs):
+def my_slots(slots, split):
+    if not split:
+        return 0, slots
+    half = slots // 2
+    return pl.multiple_of(lax.rem(lax.axis_index("act"), 2) * half, 8), half
+
+
+def meet(slots, split, known, fresh, last, together, *refs):
+    every = known + fresh
     sent, refs = refs[:fresh], refs[fresh:]
-    every = known + fresh
     old_sources, old_targets, before = refs[:known], refs[known : 2 * known], refs[2 * known : 3 * known]
     refs = refs[3 * known :]
-    new_sources, new_targets, after = refs[:fresh], refs[fresh : 2 * fresh], refs[2 * fresh :]
+    start, count = my_slots(slots, split)
+    if last:
+        forces_ref, refs = refs[0], refs[1:]
+        after = (None,) * every
+        partial_ref, sums_ref = refs[2 * fresh :]
+    else:
+        after = refs[2 * fresh :]
+        partial_ref, sums_ref = None, None
+    new_sources, new_targets = refs[:fresh], refs[fresh : 2 * fresh]
     groups = pair_groups(
         sent, old_sources + new_sources, old_targets + new_targets, before, after, slots
     )
-    run_pairs(groups, slots, together, False, None, None)
-
-
-def finish(slots, known, fresh, together, *refs):
-    every = known + fresh
-    sent, refs = refs[:every], refs[every:]
-    old_sources, old_targets, before = refs[:known], refs[known : 2 * known], refs[2 * known : 3 * known]
-    state_ref, place_ref, out_ref = refs[3 * known : 3 * known + 3]
-    refs = refs[3 * known + 3 :]
-    new_sources, new_targets = refs[:fresh], refs[fresh : 2 * fresh]
-    later_ref, partial_ref, sums_ref = refs[2 * fresh :]
-    groups = pair_groups(
-        sent[known:],
-        old_sources + new_sources,
-        old_targets + new_targets,
-        before,
-        (None,) * every,
-        slots,
-    )
+    forces = run_pairs(groups, slots, start, count, together, last, partial_ref, sums_ref)
+    if last:
+        for d in range(every):
+            forces_ref[:, d * slots : (d + 1) * slots] = forces[d]
+
+
+def finish(slots, shards, parts, *refs):
+    sent, refs = refs[:shards], refs[shards:]
+    shares, refs = refs[:parts], refs[parts:]
+    state_ref, place_ref, out_ref, later_ref, target_ref, partial_ref, sums_ref = refs
     size = state_ref.shape[1]
     across = size // slots
     chunks = size // 128
-    forces = run_pairs(groups, slots, together, True, partial_ref, sums_ref)
-    for d in range(every):
+    forces = []
+    for d in range(shards):
+        share = [s[:, d * slots : (d + 1) * slots] for s in shares]
+        forces.append(share[0] + share[1] if parts == 2 else share[0])
+    for d in range(shards):
         first = [
             sent[d][14 + k // across : 15 + k // across, slots * (k % across) : slots * (k % across + 1)]
             for k in range(6)
@@ -348,10 +359,9 @@
             own = jnp.concatenate([again, jnp.zeros((2, slots), jnp.float32)], axis=0)
         later = jnp.concatenate([again, sent[d][8:14, slots:size]], axis=1)
         spread_sources(jnp.concatenate([later, sent[d][6:8, :]], axis=0), later_ref, d * chunks)
-    target_ref = new_targets[0]
     spread_targets(own, target_ref)
     second = run_pairs(
-        [(target_ref, None, (later_ref,), None)], slots, 4, True, partial_ref, sums_ref
+        [(target_ref, None, (later_ref,), None)], slots, 0, slots, 4, True, partial_ref, sums_ref
     )[0]
     position, velocity = corrected(
         forces[0][0:3], forces[0][3:6], own[0:3], own[3:6], second[0:3], second[3:6]
@@ -400,42 +410,61 @@
         sent.append(lax.ppermute(message, "src", pairs))
 
     limit = pltpu.CompilerParams(vmem_limit_bytes=16 * 2**20)
+    owners = lax.axis_size("act")
+    split = owners % 2 == 0
     source_shape = jax.ShapeDtypeStruct((7, size // 16, 128), jnp.float32)
     target_shape = jax.ShapeDtypeStruct((6, slots, 128), jnp.float32)
+    together = 2
     sources, targets, sums = [], [], []
     known = 0
-    stages = [min(2, shards - 1)] + [1] * (shards - 3)
-    for fresh in stages:
+    for fresh in [2] + [1] * (shards - 2):
         every = known + fresh
+        last = every == shards
+        kept = [source_shape] * fresh + [target_shape] * fresh
         outs = pl.pallas_call(
-            functools.partial(meet, slots, known, fresh, 2),
-            out_shape=[source_shape] * fresh + [target_shape] * (fresh + every),
+            functools.partial(meet, slots, split, known, fresh, last, together),
+            out_shape=(
+                jax.ShapeDtypeStruct((8, shards * slots), jnp.float32)
+                if last
+                else kept + [target_shape] * every
+            ),
             in_specs=[whole] * (fresh + 3 * known),
-            out_specs=[whole] * (2 * fresh + every),
+            out_specs=whole if last else [whole] * (2 * fresh + every),
+            scratch_shapes=(
+                [pltpu.VMEM(k.shape, k.dtype) for k in kept]
+                + [
+                    pltpu.VMEM((together * shards * 48, 128), jnp.float32),
+                    pltpu.VMEM((shards * (slots + 8 * together), 8), jnp.float32),
+                ]
+                if last
+                else []
+            ),
             compiler_params=limit,
             name=f"meet_{every}",
         )(*sent[known:every], *sources, *targets, *sums)
+        if last:
+            break
         sources += outs[:fresh]
         targets += outs[fresh : 2 * fresh]
         sums = list(outs[2 * fresh :])
         known = every
-    together = 2
-    rows = max(together * shards, 4) * 48
+    shares = [outs]
+    if split:
+        shares.append(lax.ppermute(outs, "act", [(i, i ^ 1) for i in range(owners)]))
     return pl.pallas_call(
-        functools.partial(finish, slots, known, shards - known, together),
+        functools.partial(finish, slots, shards, len(shares)),
         out_shape=jax.ShapeDtypeStruct((12, size), jnp.float32),
-        in_specs=[whole] * (shards + 3 * known + 2),
+        in_specs=[whole] * (shards + len(shares) + 2),
         out_specs=whole,
-        scratch_shapes=[pltpu.VMEM(source_shape.shape, jnp.float32)] * (shards - known)
-        + [pltpu.VMEM(target_shape.shape, jnp.float32)] * (shards - known)
-        + [
+        scratch_shapes=[
             pltpu.VMEM((7, shards * size // 16, 128), jnp.float32),
-            pltpu.VMEM((rows, 128), jnp.float32),
-            pltpu.VMEM((shards * (slots + 32), 8), jnp.float32),
+            pltpu.VMEM(target_shape.shape, jnp.float32),
+            pltpu.VMEM((4 * 48, 128), jnp.float32),
+            pltpu.VMEM((slots + 32, 8), jnp.float32),
         ],
         compiler_params=limit,
         name="finish",
-    )(*sent, *sources, *targets, *sums, star_state, place)
+    )(*sent, *shares, star_state, place)
 
 
 def solution(mesh):
@@ -448,7 +477,7 @@
         P(("groups", "src", "act")),
     )
     out_specs = P(None, ("groups", "src"))
-    few = 3 <= mesh.shape["src"] <= MAX_DIRECT
+    few = 2 <= mesh.shape["src"] <= MAX_DIRECT
     return jax.shard_map(
         direct_per_device if few else gather_per_device,
         mesh=mesh,

time: 18.3 us -> 16.8 us (0.918)
  Pallas kernels: 11 us -> 8.02 us
  waiting for transfers between devices: 0.01 us -> 1.43 us
    pallas_call x3 -> x4, Pallas kernels: 9.81 us -> 6.78 us  [the longest x3 4.16 us: direct_per_device(): pl.pallas_call(functools.partial(meet, slots, split, known, fresh, last,...]
    ppermute x0 -> x1, waiting for transfers between devices: none -> 1.17 us  [direct_per_device(): lax.ppermute(outs, 'act', [(i, i ^ 1) for i in range(owners)])]
    ppermute x3, waiting for transfers between devices: 0.01 us -> 0.26 us  [direct_per_device(): sent.append(lax.ppermute(message, 'src', pairs))]
  transfers between devices with their start and end apart: 3 -> 4, of which waited for: 0 -> 3; matrix products, arithmetic and copies ran while one was open for 0% -> 0% of each run, Pallas kernels for 22% -> 14%
where the time goes in v5:
time: 16.8 us; the launch traced here: 16.6 us
  Pallas kernels  8.02 us (48%)
  starting transfers between devices  7.1 us (42%)
  waiting for transfers between devices  1.43 us (9%)
    ppermute x3, starting transfers between devices, direct_per_device(): sent.append(lax.ppermute(message, 'src', pairs))  7.04 us
    pallas_call x3, Pallas kernels, direct_per_device(): pl.pallas_call(functools.partial(meet, slots, split, known, fresh, last,...  4.16 us
    pallas_call x1, Pallas kernels, direct_per_device(): pl.pallas_call(functools.partial(finish, slots, shards, len(shares)), out...  2.62 us
    pallas_call x1, Pallas kernels, direct_per_device(): pl.pallas_call(lambda *refs: prepare(slots, size * shards, *refs), out_sh...  1.24 us
    ppermute x1, waiting for transfers between devices, direct_per_device(): lax.ppermute(outs, 'act', [(i, i ^ 1) for i in range(owners)])  1.17 us
  transfers between devices with their start and end apart: 4, of which 3 were waited for; matrix products, arithmetic and copies ran while one was open for 0% of the time, Pallas kernels for 14%

profile of v5, /device:TPU:0, one launch (start us, length us, event | category | flops | bytes accessed | tf_op | source)
XLA Modules:
  0.0 16.6 jit_solution(13419129797155404742)
XLA Ops:
  0.0 1.2 %prepare.1 = (f32[16,512]{1,0:T(8,128)S(1)}, f32[8,512]{1,0:T(8,128)S(1)}) custom-call(f32[12,512]{1,0:T(8,128)} %refs_6_.1, f32[1,512]{1,0:T(1,128)} %bitcast.3, f32[1,512]{1,0:T(1,128)} %bitcast.4, s32[1,512]{1,0:T(1,128)} %bitcast.5), custom_call_target="tpu_custom_call" | custom-call | tf_op jit(solution)/shard_map/prepare/pallas_call | solution.py:384
  1.2 3.1 %collective-permute-start = (f32[16,512]{1,0:T(8,128)S(1)}, f32[16,512]{1,0:T(8,128)S(1)}, u32[]{:S(2)}, u32[]{:S(2)}) collective-permute-start(f32[16,512]{1,0:T(8,128)S(1)} %get-tuple-element.18.refs_0_), channel_id=1, source_target_pairs={{0,4},{4,8},{8,12},{12,0},{1,5},{5,9},{9,13},{13,1},{2,6},{6,10},{... | collective-permute-start | bytes 98312 | tf_op jit(solution)/shard_map/ppermute | solution.py:410
  4.4 2.6 %collective-permute-start.1 = (f32[16,512]{1,0:T(8,128)S(1)}, f32[16,512]{1,0:T(8,128)S(1)}, u32[]{:S(2)}, u32[]{:S(2)}) collective-permute-start(f32[16,512]{1,0:T(8,128)S(1)} %get-tuple-element.18.refs_0_), channel_id=1, source_target_pairs={{0,8},{4,12},{8,0},{12,4},{1,9},{5,13},{9,1},{13,5},{2,10},{6,14},... | collective-permute-start | bytes 98312 | tf_op jit(solution)/shard_map/ppermute | solution.py:410
  6.9 1.3 %collective-permute-start.2 = (f32[16,512]{1,0:T(8,128)S(1)}, f32[16,512]{1,0:T(8,128)S(1)}, u32[]{:S(2)}, u32[]{:S(2)}) collective-permute-start(f32[16,512]{1,0:T(8,128)S(1)} %get-tuple-element.18.refs_0_), channel_id=1, source_target_pairs={{0,12},{4,0},{8,4},{12,8},{1,13},{5,1},{9,5},{13,9},{2,14},{6,2},{... | collective-permute-start | bytes 98312 | tf_op jit(solution)/shard_map/ppermute | solution.py:410
  8.3 0.0 collective-permute-done.refs_1_
  8.3 1.1 %meet_2.1 = (f32[7,32,128]{2,1,0:T(8,128)S(1)}, f32[7,32,128]{2,1,0:T(8,128)S(1)}, f32[6,128,128]{2,1,0:T(8,128)S(1)}, f32[6,128,128]{2,1,0:T(8,128)S(1)}, f32[6...) custom-call(f32[16,512]{1,0:T(8,128)S(1)} %get-tuple-element.18.refs_0_, f32[16,512]{1,0:T(8,128)S(1)} %collective-permute-done.refs_1_), custom_call_target="tpu_custom_call" | custom-call | tf_op jit(solution)/shard_map/meet_2/pallas_call | solution.py:424
  9.4 0.1 collective-permute-done.1.refs_0_.refs_2_
  9.5 1.2 %meet_3.1 = (f32[7,32,128]{2,1,0:T(8,128)S(1)}, f32[6,128,128]{2,1,0:T(8,128)S(1)}, f32[6,128,128]{2,1,0:T(8,128)S(1)}, f32[6,128,128]{2,1,0:T(8,128)S(1)}, f32[6,128,128]{2,1,0:T(8,128)S(1)}) custom-call(f32[16,512]{1,0:T(8,128)S(1)} %collective-permute-done.1.refs_0_.refs_2_, f32[7,32,128]{2,1,0:T(8,128)S(1)} %get-tuple-element.19.refs_1_, ...), custom_call_target="tpu_custom_call" | custom-call | tf_op jit(solution)/shard_map/meet_3/pallas_call | solution.py:424
  10.7 0.1 collective-permute-done.2.refs_0_.refs_3_
  10.9 0.0 copy-start
  10.9 1.9 %meet_4.1.refs_4_ = f32[8,512]{1,0:T(8,128)S(1)} custom-call(f32[16,512]{1,0:T(8,128)S(1)} %collective-permute-done.2.refs_0_.refs_3_, f32[7,32,128]{2,1,0:T(8,128)S(1)} %get-tuple-element.19.refs_1_, f32[7,32,128]{2,1,0:T(8,128)S(1)} %get-tuple-element.20.refs_2_, f32[7,32,128]{2,1,0:T(8,128)S(1)} %get-tuple-element.25.refs_3_, ...), custom_call_target="tpu_custom_call" | custom-call | tf_op jit(solution)/shard_map/meet_4/pallas_call | solution.py:424
  12.7 0.1 collective-permute-start.3
  12.8 1.2 %collective-permute-done.3.refs_5_ = f32[8,512]{1,0:T(8,128)S(1)} collective-permute-done((f32[8,512]{1,0:T(8,128)S(1)}, f32[8,512]{1,0:T(8,128)S(1)}, u32[]{:S(2)}, u32[]{:S(2)}) %collective-permute-start.3) | collective-permute-done | bytes 16416 | tf_op jit(solution)/shard_map/ppermute | solution.py:453
  14.0 0.0 copy-done
  14.0 2.6 %finish.1 = f32[12,512]{1,0:T(8,128)} custom-call(f32[16,512]{1,0:T(8,128)S(1)} %get-tuple-element.18.refs_0_, f32[16,512]{1,0:T(8,128)S(1)} %collective-permute-done.refs_1_, f32[16,512]{1,0:T(8,128)S(1)} %collective-permute-done.1.refs_0_.refs_2_, f32[16,512]{1,0:T(8,128)S(1)} %collective-permute-done.2.refs_0_.refs_3_, f32[8,512]{1,0:T(8,128)S(1)} %meet_4.1.refs_4_, ...), custom_call_target="tpu_custom_call" | custom-call | tf_op jit(solution)/shard_map/finish/pallas_call | solution.py:454
Async XLA Ops:
  1.2 7.0 %collective-permute-start = (f32[16,512]{1,0:T(8,128)S(1)}, f32[16,512]{1,0:T(8,128)S(1)}, u32[]{:S(2)}, u32[]{:S(2)}) collective-permute-start(f32[16,512]{1,0:T(8,128)S(1)} %get-tuple-element.18.refs_0_), channel_id=1, source_target_pairs={{0,4},{4,8},{8,12},{12,0},{1,5},{5,9},{9,13},{13,1},{2,6},{6,10},{... | collective-permute-start | bytes 98312 | tf_op jit(solution)/shard_map/ppermute | solution.py:410
  4.4 5.2 %collective-permute-start.1 = (f32[16,512]{1,0:T(8,128)S(1)}, f32[16,512]{1,0:T(8,128)S(1)}, u32[]{:S(2)}, u32[]{:S(2)}) collective-permute-start(f32[16,512]{1,0:T(8,128)S(1)} %get-tuple-element.18.refs_0_), channel_id=1, source_target_pairs={{0,8},{4,12},{8,0},{12,4},{1,9},{5,13},{9,1},{13,5},{2,10},{6,14},... | collective-permute-start | bytes 98312 | tf_op jit(solution)/shard_map/ppermute | solution.py:410
  6.9 3.9 %collective-permute-start.2 = (f32[16,512]{1,0:T(8,128)S(1)}, f32[16,512]{1,0:T(8,128)S(1)}, u32[]{:S(2)}, u32[]{:S(2)}) collective-permute-start(f32[16,512]{1,0:T(8,128)S(1)} %get-tuple-element.18.refs_0_), channel_id=1, source_target_pairs={{0,12},{4,0},{8,4},{12,8},{1,13},{5,1},{9,5},{13,9},{2,14},{6,2},{... | collective-permute-start | bytes 98312 | tf_op jit(solution)/shard_map/ppermute | solution.py:410
  10.9 3.1 %copy-start = (f32[12,512]{1,0:T(8,128)S(1)}, f32[12,512]{1,0:T(8,128)}, u32[]{:S(2)}) copy-start(f32[12,512]{1,0:T(8,128)} %refs_6_.1) | copy-start | bytes 73732
  12.7 1.2 %collective-permute-start.3 = (f32[8,512]{1,0:T(8,128)S(1)}, f32[8,512]{1,0:T(8,128)S(1)}, u32[]{:S(2)}, u32[]{:S(2)}) collective-permute-start(f32[8,512]{1,0:T(8,128)S(1)} %meet_4.1.refs_4_), channel_id=1, source_target_pairs={{0,1},{1,0},{2,3},{3,2},{4,5},{5,4},{6,7},{7,6},{8,9},{9,8},{10,11... | collective-permute-start | bytes 49160 | tf_op jit(solution)/shard_map/ppermute | solution.py:453

commit v6 on v5

--- a/solution.py
+++ b/solution.py
@@ -225,10 +225,12 @@
             )
 
 
-def spread_targets(rows, spread_ref):
+def spread_targets(rows, spread_ref, start, count):
     columns = jnp.transpose(rows)
     for r in range(6):
-        spread_ref[r] = jnp.broadcast_to(columns[:, r : r + 1], (columns.shape[0], 128))
+        spread_ref[r, start : start + count, :] = jnp.broadcast_to(
+            columns[start : start + count, r : r + 1], (count, 128)
+        )
 
 
 def run_pairs(groups, slots, start, count, together, finish, partial_ref, sums_ref):
@@ -249,8 +251,15 @@
             reduce(base)
         for g in range(together):
             here = pl.ds(base + 8 * g, 8)
-            for j, (target_ref, before_ref, sources, after_ref) in enumerate(groups):
-                target = [target_ref[r, here, :] for r in range(6)]
+            for j, (target_ref, columns_ref, before_ref, sources, after_ref) in enumerate(groups):
+                if columns_ref is None:
+                    target = [target_ref[r, here, :] for r in range(6)]
+                else:
+                    columns = columns_ref[here, :]
+                    target = [jnp.broadcast_to(columns[:, r : r + 1], (8, 128)) for r in range(6)]
+                    if target_ref is not None:
+                        for r in range(6):
+                            target_ref[r, here, :] = target[r]
                 if before_ref is None:
                     sums = (jnp.zeros((8, 128), jnp.float32),) * 6
                 else:
@@ -282,48 +291,50 @@
     ]
 
 
-def pair_groups(sent, sources, targets, before, after, slots):
-    for d in range(len(before), len(targets)):
-        fresh = sent[d - len(before)]
-        spread_sources(fresh[0:8, :], sources[d], 0)
-        spread_targets(fresh[0:8, 0:slots], targets[d])
-    groups = []
-    for d in range(len(targets)):
-        if d < len(before):
-            groups.append((targets[d], before[d], sources[len(before) :], after[d]))
-        else:
-            groups.append((targets[d], None, sources, after[d]))
-    return groups
-
-
-def my_slots(slots, split):
-    if not split:
-        return 0, slots
-    half = slots // 2
-    return pl.multiple_of(lax.rem(lax.axis_index("act"), 2) * half, 8), half
-
-
-def meet(slots, split, known, fresh, last, together, *refs):
+def meet(slots, shares, known, fresh, last, together, *refs):
     every = known + fresh
     sent, refs = refs[:fresh], refs[fresh:]
     old_sources, old_targets, before = refs[:known], refs[known : 2 * known], refs[2 * known : 3 * known]
     refs = refs[3 * known :]
-    start, count = my_slots(slots, split)
+    forces_ref = columns_ref = partial_ref = sums_ref = None
     if last:
         forces_ref, refs = refs[0], refs[1:]
+        new_sources, refs = refs[:fresh], refs[fresh:]
+        new_targets = (None,) * fresh
         after = (None,) * every
-        partial_ref, sums_ref = refs[2 * fresh :]
+        columns_ref, partial_ref, sums_ref = refs
     else:
-        after = refs[2 * fresh :]
-        partial_ref, sums_ref = None, None
-    new_sources, new_targets = refs[:fresh], refs[fresh : 2 * fresh]
-    groups = pair_groups(
-        sent, old_sources + new_sources, old_targets + new_targets, before, after, slots
-    )
-    forces = run_pairs(groups, slots, start, count, together, last, partial_ref, sums_ref)
-    if last:
-        for d in range(every):
-            forces_ref[:, d * slots : (d + 1) * slots] = forces[d]
+        new_sources, new_targets, after = refs[:fresh], refs[fresh : 2 * fresh], refs[2 * fresh : 2 * fresh + every]
+        columns_ref = refs[2 * fresh + every]
+    sources = old_sources + new_sources
+
+    def run(start, count):
+        groups = []
+        for d in range(known):
+            groups.append((old_targets[d], None, before[d], new_sources, after[d]))
+        for d in range(fresh):
+            spread_sources(sent[d][0:8, :], new_sources[d], 0)
+            in_loop = None
+            if known:
+                in_loop = columns_ref
+                columns_ref[...] = jnp.transpose(sent[d][0:8, 0:slots])
+            else:
+                spread_targets(sent[d][0:8, 0:slots], new_targets[d], start, count)
+            groups.append((new_targets[d], in_loop, None, sources, after[known + d]))
+        forces = run_pairs(groups, slots, start, count, together, last, partial_ref, sums_ref)
+        if last:
+            for d in range(every):
+                forces_ref[:, d * slots : (d + 1) * slots] = forces[d]
+
+    if len(shares) == 1:
+        run(0, slots)
+        return
+    member = lax.rem(lax.axis_index("act"), len(shares))
+    for m in range(len(shares)):
+
+        @pl.when(member == m)
+        def _():
+            run(sum(shares[:m]), shares[m])
 
 
 def finish(slots, shards, parts, *refs):
@@ -359,9 +370,9 @@
             own = jnp.concatenate([again, jnp.zeros((2, slots), jnp.float32)], axis=0)
         later = jnp.concatenate([again, sent[d][8:14, slots:size]], axis=1)
         spread_sources(jnp.concatenate([later, sent[d][6:8, :]], axis=0), later_ref, d * chunks)
-    spread_targets(own, target_ref)
+    spread_targets(own, target_ref, 0, slots)
     second = run_pairs(
-        [(target_ref, None, (later_ref,), None)], slots, 0, slots, 4, True, partial_ref, sums_ref
+        [(target_ref, None, None, (later_ref,), None)], slots, 0, slots, 4, True, partial_ref, sums_ref
     )[0]
     position, velocity = corrected(
         forces[0][0:3], forces[0][3:6], own[0:3], own[3:6], second[0:3], second[3:6]
@@ -411,7 +422,10 @@
 
     limit = pltpu.CompilerParams(vmem_limit_bytes=16 * 2**20)
     owners = lax.axis_size("act")
-    split = owners % 2 == 0
+    shares = (slots,)
+    if owners % 2 == 0:
+        first_share = slots * 3 // 8 // 16 * 16
+        shares = (first_share, slots - first_share)
     source_shape = jax.ShapeDtypeStruct((7, size // 16, 128), jnp.float32)
     target_shape = jax.ShapeDtypeStruct((6, slots, 128), jnp.float32)
     together = 2
@@ -422,7 +436,7 @@
         last = every == shards
         kept = [source_shape] * fresh + [target_shape] * fresh
         outs = pl.pallas_call(
-            functools.partial(meet, slots, split, known, fresh, last, together),
+            functools.partial(meet, slots, shares, known, fresh, last, together),
             out_shape=(
                 jax.ShapeDtypeStruct((8, shards * slots), jnp.float32)
                 if last
@@ -431,13 +445,14 @@
             in_specs=[whole] * (fresh + 3 * known),
             out_specs=whole if last else [whole] * (2 * fresh + every),
             scratch_shapes=(
-                [pltpu.VMEM(k.shape, k.dtype) for k in kept]
-                + [
+                [
+                    pltpu.VMEM(source_shape.shape, jnp.float32),
+                    pltpu.VMEM((slots, 8), jnp.float32),
                     pltpu.VMEM((together * shards * 48, 128), jnp.float32),
                     pltpu.VMEM((shards * (slots + 8 * together), 8), jnp.float32),
                 ]
                 if last
-                else []
+                else [pltpu.VMEM((slots, 8), jnp.float32)]
             ),
             compiler_params=limit,
             name=f"meet_{every}",
@@ -448,13 +463,13 @@
         targets += outs[fresh : 2 * fresh]
         sums = list(outs[2 * fresh :])
         known = every
-    shares = [outs]
-    if split:
-        shares.append(lax.ppermute(outs, "act", [(i, i ^ 1) for i in range(owners)]))
+    parts = [outs]
+    if len(shares) == 2:
+        parts.append(lax.ppermute(outs, "act", [(i, i ^ 1) for i in range(owners)]))
     return pl.pallas_call(
-        functools.partial(finish, slots, shards, len(shares)),
+        functools.partial(finish, slots, shards, len(parts)),
         out_shape=jax.ShapeDtypeStruct((12, size), jnp.float32),
-        in_specs=[whole] * (shards + len(shares) + 2),
+        in_specs=[whole] * (shards + len(parts) + 2),
         out_specs=whole,
         scratch_shapes=[
             pltpu.VMEM((7, shards * size // 16, 128), jnp.float32),
@@ -464,7 +479,7 @@
         ],
         compiler_params=limit,
         name="finish",
-    )(*sent, *shares, star_state, place)
+    )(*sent, *parts, star_state, place)
 
 
 def solution(mesh):
@@ -477,7 +492,7 @@
         P(("groups", "src", "act")),
     )
     out_specs = P(None, ("groups", "src"))
-    few = 2 <= mesh.shape["src"] <= MAX_DIRECT
+    few = 3 <= mesh.shape["src"] <= MAX_DIRECT
     return jax.shard_map(
         direct_per_device if few else gather_per_device,
         mesh=mesh,

time: 16.8 us -> 16.3 us (0.970)
  Pallas kernels: 8.02 us -> 6.82 us
  waiting for transfers between devices: 1.43 us -> 2.13 us
    pallas_call x4, Pallas kernels: 6.78 us -> 5.58 us  [the longest x3 2.96 us: direct_per_device(): pl.pallas_call(functools.partial(meet, slots, shares, known, fresh, last,...]
    ppermute x3, waiting for transfers between devices: 0.26 us -> 0.96 us  [direct_per_device(): sent.append(lax.ppermute(message, 'src', pairs))]
  transfers between devices with their start and end apart: 4 -> 4, of which waited for: 3 -> 3; matrix products, arithmetic and copies ran while one was open for 0% -> 0% of each run, Pallas kernels for 14% -> 10%
where the time goes in v6:
time: 16.3 us; the launch traced here: 16.1 us
  starting transfers between devices  7.1 us (44%)
  Pallas kernels  6.82 us (42%)
  waiting for transfers between devices  2.13 us (13%)
    ppermute x3, starting transfers between devices, direct_per_device(): sent.append(lax.ppermute(message, 'src', pairs))  7.04 us
    pallas_call x3, Pallas kernels, direct_per_device(): pl.pallas_call(functools.partial(meet, slots, shares, known, fresh, last,...  2.96 us
    pallas_call x1, Pallas kernels, direct_per_device(): pl.pallas_call(functools.partial(finish, slots, shards, len(parts)), out_...  2.62 us
    pallas_call x1, Pallas kernels, direct_per_device(): pl.pallas_call(lambda *refs: prepare(slots, size * shards, *refs), out_sh...  1.24 us
    ppermute x1, waiting for transfers between devices, direct_per_device(): parts.append(lax.ppermute(outs, 'act', [(i, i ^ 1) for i in range(owners)]))  1.17 us
    ppermute x3, waiting for transfers between devices, direct_per_device(): sent.append(lax.ppermute(message, 'src', pairs))  0.96 us
  transfers between devices with their start and end apart: 4, of which 3 were waited for; matrix products, arithmetic and copies ran while one was open for 0% of the time, Pallas kernels for 10%

profile of v6, /device:TPU:0, one launch (start us, length us, event | category | flops | bytes accessed | tf_op | source)
XLA Modules:
  0.0 16.1 jit_solution(8536483126585833614)
XLA Ops:
  0.0 1.2 %prepare.1 = (f32[16,512]{1,0:T(8,128)S(1)}, f32[8,512]{1,0:T(8,128)S(1)}) custom-call(f32[12,512]{1,0:T(8,128)} %refs_6_.1, f32[1,512]{1,0:T(1,128)} %bitcast.3, f32[1,512]{1,0:T(1,128)} %bitcast.4, s32[1,512]{1,0:T(1,128)} %bitcast.5), custom_call_target="tpu_custom_call" | custom-call | tf_op jit(solution)/shard_map/prepare/pallas_call | solution.py:395
  1.2 3.1 %collective-permute-start = (f32[16,512]{1,0:T(8,128)S(1)}, f32[16,512]{1,0:T(8,128)S(1)}, u32[]{:S(2)}, u32[]{:S(2)}) collective-permute-start(f32[16,512]{1,0:T(8,128)S(1)} %get-tuple-element.18.refs_0_), channel_id=1, source_target_pairs={{0,4},{4,8},{8,12},{12,0},{1,5},{5,9},{9,13},{13,1},{2,6},{6,10},{... | collective-permute-start | bytes 98312 | tf_op jit(solution)/shard_map/ppermute | solution.py:421
  4.4 2.6 %collective-permute-start.1 = (f32[16,512]{1,0:T(8,128)S(1)}, f32[16,512]{1,0:T(8,128)S(1)}, u32[]{:S(2)}, u32[]{:S(2)}) collective-permute-start(f32[16,512]{1,0:T(8,128)S(1)} %get-tuple-element.18.refs_0_), channel_id=1, source_target_pairs={{0,8},{4,12},{8,0},{12,4},{1,9},{5,13},{9,1},{13,5},{2,10},{6,14},... | collective-permute-start | bytes 98312 | tf_op jit(solution)/shard_map/ppermute | solution.py:421
  6.9 1.3 %collective-permute-start.2 = (f32[16,512]{1,0:T(8,128)S(1)}, f32[16,512]{1,0:T(8,128)S(1)}, u32[]{:S(2)}, u32[]{:S(2)}) collective-permute-start(f32[16,512]{1,0:T(8,128)S(1)} %get-tuple-element.18.refs_0_), channel_id=1, source_target_pairs={{0,12},{4,0},{8,4},{12,8},{1,13},{5,1},{9,5},{13,9},{2,14},{6,2},{... | collective-permute-start | bytes 98312 | tf_op jit(solution)/shard_map/ppermute | solution.py:421
  8.3 0.0 collective-permute-done.refs_1_
  8.3 0.8 %meet_2.1 = (f32[7,32,128]{2,1,0:T(8,128)S(1)}, f32[7,32,128]{2,1,0:T(8,128)S(1)}, f32[6,128,128]{2,1,0:T(8,128)S(1)}, f32[6,128,128]{2,1,0:T(8,128)S(1)}, f32[6...) custom-call(f32[16,512]{1,0:T(8,128)S(1)} %get-tuple-element.18.refs_0_, f32[16,512]{1,0:T(8,128)S(1)} %collective-permute-done.refs_1_), custom_call_target="tpu_custom_call" | custom-call | tf_op jit(solution)/shard_map/meet_2/pallas_call | solution.py:438
  9.1 0.4 %collective-permute-done.1.refs_0_.refs_2_ = f32[16,512]{1,0:T(8,128)S(1)} collective-permute-done((f32[16,512]{1,0:T(8,128)S(1)}, f32[16,512]{1,0:T(8,128)S(1)}, u32[]{:S(2)}, u32[]{:S(2)}) %collective-permute-start.1) | collective-permute-done | bytes 32800 | tf_op jit(solution)/shard_map/ppermute | solution.py:421
  9.5 0.8 %meet_3.1 = (f32[7,32,128]{2,1,0:T(8,128)S(1)}, f32[6,128,128]{2,1,0:T(8,128)S(1)}, f32[6,128,128]{2,1,0:T(8,128)S(1)}, f32[6,128,128]{2,1,0:T(8,128)S(1)}, f32[6,128,128]{2,1,0:T(8,128)S(1)}) custom-call(f32[16,512]{1,0:T(8,128)S(1)} %collective-permute-done.1.refs_0_.refs_2_, f32[7,32,128]{2,1,0:T(8,128)S(1)} %get-tuple-element.19.refs_1_, ...), custom_call_target="tpu_custom_call" | custom-call | tf_op jit(solution)/shard_map/meet_3/pallas_call | solution.py:438
  10.3 0.5 %collective-permute-done.2.refs_0_.refs_3_ = f32[16,512]{1,0:T(8,128)S(1)} collective-permute-done((f32[16,512]{1,0:T(8,128)S(1)}, f32[16,512]{1,0:T(8,128)S(1)}, u32[]{:S(2)}, u32[]{:S(2)}) %collective-permute-start.2) | collective-permute-done | bytes 32800 | tf_op jit(solution)/shard_map/ppermute | solution.py:421
  10.9 0.0 copy-start
  10.9 1.4 %meet_4.1.refs_4_ = f32[8,512]{1,0:T(8,128)S(1)} custom-call(f32[16,512]{1,0:T(8,128)S(1)} %collective-permute-done.2.refs_0_.refs_3_, f32[7,32,128]{2,1,0:T(8,128)S(1)} %get-tuple-element.19.refs_1_, f32[7,32,128]{2,1,0:T(8,128)S(1)} %get-tuple-element.20.refs_2_, f32[7,32,128]{2,1,0:T(8,128)S(1)} %get-tuple-element.25.refs_3_, ...), custom_call_target="tpu_custom_call" | custom-call | tf_op jit(solution)/shard_map/meet_4/pallas_call | solution.py:438
  12.2 0.1 collective-permute-start.3
  12.3 1.2 %collective-permute-done.3.refs_5_ = f32[8,512]{1,0:T(8,128)S(1)} collective-permute-done((f32[8,512]{1,0:T(8,128)S(1)}, f32[8,512]{1,0:T(8,128)S(1)}, u32[]{:S(2)}, u32[]{:S(2)}) %collective-permute-start.3) | collective-permute-done | bytes 16416 | tf_op jit(solution)/shard_map/ppermute | solution.py:468
  13.5 0.0 copy-done
  13.5 2.6 %finish.1 = f32[12,512]{1,0:T(8,128)} custom-call(f32[16,512]{1,0:T(8,128)S(1)} %get-tuple-element.18.refs_0_, f32[16,512]{1,0:T(8,128)S(1)} %collective-permute-done.refs_1_, f32[16,512]{1,0:T(8,128)S(1)} %collective-permute-done.1.refs_0_.refs_2_, f32[16,512]{1,0:T(8,128)S(1)} %collective-permute-done.2.refs_0_.refs_3_, f32[8,512]{1,0:T(8,128)S(1)} %meet_4.1.refs_4_, ...), custom_call_target="tpu_custom_call" | custom-call | tf_op jit(solution)/shard_map/finish/pallas_call | solution.py:469
Async XLA Ops:
  1.2 7.0 %collective-permute-start = (f32[16,512]{1,0:T(8,128)S(1)}, f32[16,512]{1,0:T(8,128)S(1)}, u32[]{:S(2)}, u32[]{:S(2)}) collective-permute-start(f32[16,512]{1,0:T(8,128)S(1)} %get-tuple-element.18.refs_0_), channel_id=1, source_target_pairs={{0,4},{4,8},{8,12},{12,0},{1,5},{5,9},{9,13},{13,1},{2,6},{6,10},{... | collective-permute-start | bytes 98312 | tf_op jit(solution)/shard_map/ppermute | solution.py:421
  4.4 5.2 %collective-permute-start.1 = (f32[16,512]{1,0:T(8,128)S(1)}, f32[16,512]{1,0:T(8,128)S(1)}, u32[]{:S(2)}, u32[]{:S(2)}) collective-permute-start(f32[16,512]{1,0:T(8,128)S(1)} %get-tuple-element.18.refs_0_), channel_id=1, source_target_pairs={{0,8},{4,12},{8,0},{12,4},{1,9},{5,13},{9,1},{13,5},{2,10},{6,14},... | collective-permute-start | bytes 98312 | tf_op jit(solution)/shard_map/ppermute | solution.py:421
  6.9 3.9 %collective-permute-start.2 = (f32[16,512]{1,0:T(8,128)S(1)}, f32[16,512]{1,0:T(8,128)S(1)}, u32[]{:S(2)}, u32[]{:S(2)}) collective-permute-start(f32[16,512]{1,0:T(8,128)S(1)} %get-tuple-element.18.refs_0_), channel_id=1, source_target_pairs={{0,12},{4,0},{8,4},{12,8},{1,13},{5,1},{9,5},{13,9},{2,14},{6,2},{... | collective-permute-start | bytes 98312 | tf_op jit(solution)/shard_map/ppermute | solution.py:421
  10.9 2.6 %copy-start = (f32[12,512]{1,0:T(8,128)S(1)}, f32[12,512]{1,0:T(8,128)}, u32[]{:S(2)}) copy-start(f32[12,512]{1,0:T(8,128)} %refs_6_.1) | copy-start | bytes 73732
  12.2 1.2 %collective-permute-start.3 = (f32[8,512]{1,0:T(8,128)S(1)}, f32[8,512]{1,0:T(8,128)S(1)}, u32[]{:S(2)}, u32[]{:S(2)}) collective-permute-start(f32[8,512]{1,0:T(8,128)S(1)} %meet_4.1.refs_4_), channel_id=1, source_target_pairs={{0,1},{1,0},{2,3},{3,2},{4,5},{5,4},{6,7},{7,6},{8,9},{9,8},{10,11... | collective-permute-start | bytes 49160 | tf_op jit(solution)/shard_map/ppermute | solution.py:468

commit v7 on v6

--- a/solution.py
+++ b/solution.py
@@ -291,40 +291,47 @@
     ]
 
 
-def meet(slots, shares, known, fresh, last, together, *refs):
+def meet(slots, shares, known, fresh, last, *refs):
     every = known + fresh
     sent, refs = refs[:fresh], refs[fresh:]
     old_sources, old_targets, before = refs[:known], refs[known : 2 * known], refs[2 * known : 3 * known]
     refs = refs[3 * known :]
-    forces_ref = columns_ref = partial_ref = sums_ref = None
+    own_ref = forces_ref = own_partial = own_sums = partial_ref = sums_ref = None
     if last:
-        forces_ref, refs = refs[0], refs[1:]
+        own_ref, forces_ref, refs = refs[0], refs[1], refs[2:]
         new_sources, refs = refs[:fresh], refs[fresh:]
         new_targets = (None,) * fresh
         after = (None,) * every
-        columns_ref, partial_ref, sums_ref = refs
+        columns_ref, own_partial, own_sums, partial_ref, sums_ref = refs
     else:
         new_sources, new_targets, after = refs[:fresh], refs[fresh : 2 * fresh], refs[2 * fresh : 2 * fresh + every]
         columns_ref = refs[2 * fresh + every]
     sources = old_sources + new_sources
 
+    for d in range(fresh):
+        spread_sources(sent[d][0:8, :], new_sources[d], 0)
+        if known + d > 0:
+            columns_ref[...] = jnp.transpose(sent[d][0:8, 0:slots])
+    if known == 0:
+        spread_targets(sent[0][0:8, 0:slots], new_targets[0], 0, slots)
+        own = (new_targets[0], None, None, sources, after[0])
+    else:
+        own = (old_targets[0], None, before[0], new_sources, after[0])
+    own = run_pairs([own], slots, 0, slots, 4 if known == 0 else 8, last, own_partial, own_sums)
+    if last:
+        own_ref[...] = own[0]
+
     def run(start, count):
         groups = []
-        for d in range(known):
+        for d in range(1, known):
             groups.append((old_targets[d], None, before[d], new_sources, after[d]))
-        for d in range(fresh):
-            spread_sources(sent[d][0:8, :], new_sources[d], 0)
-            in_loop = None
-            if known:
-                in_loop = columns_ref
-                columns_ref[...] = jnp.transpose(sent[d][0:8, 0:slots])
-            else:
-                spread_targets(sent[d][0:8, 0:slots], new_targets[d], start, count)
-            groups.append((new_targets[d], in_loop, None, sources, after[known + d]))
+        for d in range(max(known, 1), every):
+            groups.append((new_targets[d - known], columns_ref, None, sources, after[d]))
+        together = 4 if known == 0 else 2
         forces = run_pairs(groups, slots, start, count, together, last, partial_ref, sums_ref)
         if last:
-            for d in range(every):
-                forces_ref[:, d * slots : (d + 1) * slots] = forces[d]
+            for d in range(1, every):
+                forces_ref[:, (d - 1) * slots : d * slots] = forces[d - 1]
 
     if len(shares) == 1:
         run(0, slots)
@@ -337,45 +344,71 @@
             run(sum(shares[:m]), shares[m])
 
 
+def first_step(slots, sent, forces):
+    size = sent.shape[1]
+    across = size // slots
+    old = [
+        sent[14 + k // across : 15 + k // across, slots * (k % across) : slots * (k % across + 1)]
+        for k in range(6)
+    ]
+    old = jnp.concatenate(old, axis=0)
+    position, velocity = corrected(
+        old[0:3], old[3:6], sent[0:3, 0:slots], sent[3:6, 0:slots], forces[0:3], forces[3:6]
+    )
+    ahead, speed = advance(position, velocity, forces[0:3], forces[3:6], fine_step)
+    active = sent[7:8, 0:slots] > 0.5
+    return jnp.where(active, jnp.concatenate([ahead, speed], axis=0), sent[8:14, 0:slots])
+
+
+def meet_still(slots, shards, *refs):
+    sent, refs = refs[:shards], refs[shards:]
+    own_ref, again_ref, target_ref, after_ref, still_ref = refs
+    size = sent[0].shape[1]
+    chunks = size // 128
+    first = slots // 128
+    again = first_step(slots, sent[0], own_ref[...])
+    again = jnp.concatenate([again, jnp.zeros((2, slots), jnp.float32)], axis=0)
+    again_ref[...] = again
+    for d in range(shards):
+        rows = jnp.concatenate([sent[d][8:14, slots:size], sent[d][6:8, slots:size]], axis=0)
+        spread_sources(rows, still_ref, d * (chunks - first))
+    spread_targets(again, target_ref, 0, slots)
+    run_pairs(
+        [(target_ref, None, None, (still_ref,), after_ref)], slots, 0, slots, 4, False, None, None
+    )
+
+
 def finish(slots, shards, parts, *refs):
     sent, refs = refs[:shards], refs[shards:]
     shares, refs = refs[:parts], refs[parts:]
-    state_ref, place_ref, out_ref, later_ref, target_ref, partial_ref, sums_ref = refs
+    own_ref, again_ref, target_ref, before_ref, state_ref, place_ref, out_ref = refs[:7]
+    later_ref, partial_ref, sums_ref = refs[7:]
     size = state_ref.shape[1]
-    across = size // slots
-    chunks = size // 128
-    forces = []
+    first = slots // 128
+    own = again_ref[...]
     for d in range(shards):
-        share = [s[:, d * slots : (d + 1) * slots] for s in shares]
-        forces.append(share[0] + share[1] if parts == 2 else share[0])
-    for d in range(shards):
-        first = [
-            sent[d][14 + k // across : 15 + k // across, slots * (k % across) : slots * (k % across + 1)]
-            for k in range(6)
-        ]
-        first = jnp.concatenate(first, axis=0)
-        position, velocity = corrected(
-            first[0:3],
-            first[3:6],
-            sent[d][0:3, 0:slots],
-            sent[d][3:6, 0:slots],
-            forces[d][0:3],
-            forces[d][3:6],
-        )
-        ahead, speed = advance(position, velocity, forces[d][0:3], forces[d][3:6], fine_step)
-        active = sent[d][7:8, 0:slots] > 0.5
-        still = sent[d][8:14, 0:slots]
-        again = jnp.where(active, jnp.concatenate([ahead, speed], axis=0), still)
         if d == 0:
-            own = jnp.concatenate([again, jnp.zeros((2, slots), jnp.float32)], axis=0)
-        later = jnp.concatenate([again, sent[d][8:14, slots:size]], axis=1)
-        spread_sources(jnp.concatenate([later, sent[d][6:8, :]], axis=0), later_ref, d * chunks)
-    spread_targets(own, target_ref, 0, slots)
+            again = own[0:6]
+        else:
+            share = [s[:, (d - 1) * slots : d * slots] for s in shares]
+            again = first_step(
+                slots, sent[d], share[0] + share[1] if parts == 2 else share[0]
+            )
+        rows = jnp.concatenate([again, sent[d][6:8, 0:slots]], axis=0)
+        spread_sources(rows, later_ref, d * first)
     second = run_pairs(
-        [(target_ref, None, None, (later_ref,), None)], slots, 0, slots, 4, True, partial_ref, sums_ref
+        [(target_ref, None, before_ref, (later_ref,), None)],
+        slots,
+        0,
+        slots,
+        8,
+        True,
+        partial_ref,
+        sums_ref,
     )[0]
+    before = own_ref[...]
     position, velocity = corrected(
-        forces[0][0:3], forces[0][3:6], own[0:3], own[3:6], second[0:3], second[3:6]
+        before[0:3], before[3:6], own[0:3], own[3:6], second[0:3], second[3:6]
     )
     new_rows = jnp.concatenate(
         [position, velocity, second[0:6], jnp.zeros((4, slots), jnp.float32)], axis=0
@@ -424,36 +457,36 @@
     owners = lax.axis_size("act")
     shares = (slots,)
     if owners % 2 == 0:
-        first_share = slots * 3 // 8 // 16 * 16
+        first_share = slots // 4 // 32 * 32
         shares = (first_share, slots - first_share)
     source_shape = jax.ShapeDtypeStruct((7, size // 16, 128), jnp.float32)
     target_shape = jax.ShapeDtypeStruct((6, slots, 128), jnp.float32)
-    together = 2
+    own_shape = jax.ShapeDtypeStruct((8, slots), jnp.float32)
+    columns = pltpu.VMEM((slots, 8), jnp.float32)
     sources, targets, sums = [], [], []
     known = 0
     for fresh in [2] + [1] * (shards - 2):
         every = known + fresh
         last = every == shards
-        kept = [source_shape] * fresh + [target_shape] * fresh
+        if last:
+            out_shape = (own_shape, jax.ShapeDtypeStruct((8, (shards - 1) * slots), jnp.float32))
+            scratch = [
+                pltpu.VMEM(source_shape.shape, jnp.float32),
+                columns,
+                pltpu.VMEM((8 * 48, 128), jnp.float32),
+                pltpu.VMEM((slots + 64, 8), jnp.float32),
+                pltpu.VMEM((2 * (shards - 1) * 48, 128), jnp.float32),
+                pltpu.VMEM(((shards - 1) * (slots + 16), 8), jnp.float32),
+            ]
+        else:
+            out_shape = [source_shape] * fresh + [target_shape] * (fresh + every)
+            scratch = [columns]
         outs = pl.pallas_call(
-            functools.partial(meet, slots, shares, known, fresh, last, together),
-            out_shape=(
-                jax.ShapeDtypeStruct((8, shards * slots), jnp.float32)
-                if last
-                else kept + [target_shape] * every
-            ),
+            functools.partial(meet, slots, shares, known, fresh, last),
+            out_shape=out_shape,
             in_specs=[whole] * (fresh + 3 * known),
-            out_specs=whole if last else [whole] * (2 * fresh + every),
-            scratch_shapes=(
-                [
-                    pltpu.VMEM(source_shape.shape, jnp.float32),
-                    pltpu.VMEM((slots, 8), jnp.float32),
-                    pltpu.VMEM((together * shards * 48, 128), jnp.float32),
-                    pltpu.VMEM((shards * (slots + 8 * together), 8), jnp.float32),
-                ]
-                if last
-                else [pltpu.VMEM((slots, 8), jnp.float32)]
-            ),
+            out_specs=(whole, whole) if last else [whole] * (2 * fresh + every),
+            scratch_shapes=scratch,
             compiler_params=limit,
             name=f"meet_{every}",
         )(*sent[known:every], *sources, *targets, *sums)
@@ -463,23 +496,33 @@
         targets += outs[fresh : 2 * fresh]
         sums = list(outs[2 * fresh :])
         known = every
-    parts = [outs]
+    own, part = outs
+    parts = [part]
     if len(shares) == 2:
-        parts.append(lax.ppermute(outs, "act", [(i, i ^ 1) for i in range(owners)]))
+        parts.append(lax.ppermute(part, "act", [(i, i ^ 1) for i in range(owners)]))
+    first = slots // 128
+    again, target, still = pl.pallas_call(
+        functools.partial(meet_still, slots, shards),
+        out_shape=(own_shape, target_shape, target_shape),
+        in_specs=[whole] * (shards + 1),
+        out_specs=(whole,) * 3,
+        scratch_shapes=[pltpu.VMEM((7, shards * (size // 128 - first) * 8, 128), jnp.float32)],
+        compiler_params=limit,
+        name="meet_still",
+    )(*sent, own)
     return pl.pallas_call(
         functools.partial(finish, slots, shards, len(parts)),
         out_shape=jax.ShapeDtypeStruct((12, size), jnp.float32),
-        in_specs=[whole] * (shards + len(parts) + 2),
+        in_specs=[whole] * (shards + len(parts) + 6),
         out_specs=whole,
         scratch_shapes=[
-            pltpu.VMEM((7, shards * size // 16, 128), jnp.float32),
-            pltpu.VMEM(target_shape.shape, jnp.float32),
-            pltpu.VMEM((4 * 48, 128), jnp.float32),
-            pltpu.VMEM((slots + 32, 8), jnp.float32),
+            pltpu.VMEM((7, shards * first * 8, 128), jnp.float32),
+            pltpu.VMEM((8 * 48, 128), jnp.float32),
+            pltpu.VMEM((slots + 64, 8), jnp.float32),
         ],
         compiler_params=limit,
         name="finish",
-    )(*sent, *parts, star_state, place)
+    )(*sent, *parts, own, again, target, still, star_state, place)
 
 
 def solution(mesh):

time: 16.3 us -> 16.8 us (1.031)
  waiting for transfers between devices: 2.13 us -> 0.28 us
  starting transfers between devices: 7.1 us -> 8.5 us
  Pallas kernels: 6.82 us -> 7.78 us
    pallas_call x3 -> x4, Pallas kernels: 2.96 us -> 5.15 us  [the longest x3 3.76 us: direct_per_device(): pl.pallas_call(functools.partial(meet, slots, shares, known, fresh, last)...]
    ppermute x1, starting transfers between devices: 0.06 us -> 1.46 us  [direct_per_device(): parts.append(lax.ppermute(part, 'act', [(i, i ^ 1) for i in range(owners)]))]
    pallas_call x1, Pallas kernels: 2.62 us -> 1.38 us  [direct_per_device(): pl.pallas_call(functools.partial(finish, slots, shards, len(parts)), out_...]
    ppermute x1, waiting for transfers between devices: 1.17 us -> 0.01 us  [direct_per_device(): parts.append(lax.ppermute(part, 'act', [(i, i ^ 1) for i in range(owners)]))]
    ppermute x3, waiting for transfers between devices: 0.96 us -> 0.28 us  [direct_per_device(): sent.append(lax.ppermute(message, 'src', pairs))]
  transfers between devices with their start and end apart: 4 -> 4, of which waited for: 3 -> 1; matrix products, arithmetic and copies ran while one was open for 0% -> 0% of each run, Pallas kernels for 10% -> 22%
where the time goes in v7:
time: 16.8 us; the launch traced here: 16.6 us
  starting transfers between devices  8.5 us (51%)
  Pallas kernels  7.78 us (46%)
  waiting for transfers between devices  0.28 us (2%)
    ppermute x3, starting transfers between devices, direct_per_device(): sent.append(lax.ppermute(message, 'src', pairs))  7.04 us
    pallas_call x3, Pallas kernels, direct_per_device(): pl.pallas_call(functools.partial(meet, slots, shares, known, fresh, last)...  3.76 us
    ppermute x1, starting transfers between devices, direct_per_device(): parts.append(lax.ppermute(part, 'act', [(i, i ^ 1) for i in range(owners)]))  1.46 us
    pallas_call x1, Pallas kernels, direct_per_device(): pl.pallas_call(functools.partial(meet_still, slots, shards), out_shape=(o...  1.39 us
    pallas_call x1, Pallas kernels, direct_per_device(): pl.pallas_call(functools.partial(finish, slots, shards, len(parts)), out_...  1.38 us
    pallas_call x1, Pallas kernels, direct_per_device(): pl.pallas_call(lambda *refs: prepare(slots, size * shards, *refs), out_sh...  1.24 us
  transfers between devices with their start and end apart: 4, of which 1 were waited for; matrix products, arithmetic and copies ran while one was open for 0% of the time, Pallas kernels for 22%

profile of v7, /device:TPU:0, one launch (start us, length us, event | category | flops | bytes accessed | tf_op | source)
XLA Modules:
  0.0 16.6 jit_solution(10441270885363318994)
XLA Ops:
  0.0 1.2 %prepare.1 = (f32[16,512]{1,0:T(8,128)S(1)}, f32[8,512]{1,0:T(8,128)S(1)}) custom-call(f32[12,512]{1,0:T(8,128)} %refs_10_.1, f32[1,512]{1,0:T(1,128)} %bitcast.3, f32[1,512]{1,0:T(1,128)} %bitcast.4, s32[1,512]{1,0:T(1,128)} %bitcast.5), custom_call_target="tpu_custom_call" | custom-call | tf_op jit(solution)/shard_map/prepare/pallas_call | solution.py:428
  1.2 3.1 %collective-permute-start = (f32[16,512]{1,0:T(8,128)S(1)}, f32[16,512]{1,0:T(8,128)S(1)}, u32[]{:S(2)}, u32[]{:S(2)}) collective-permute-start(f32[16,512]{1,0:T(8,128)S(1)} %get-tuple-element.23.refs_0_), channel_id=1, source_target_pairs={{0,4},{4,8},{8,12},{12,0},{1,5},{5,9},{9,13},{13,1},{2,6},{6,10},{... | collective-permute-start | bytes 98312 | tf_op jit(solution)/shard_map/ppermute | solution.py:454
  4.4 2.6 %collective-permute-start.1 = (f32[16,512]{1,0:T(8,128)S(1)}, f32[16,512]{1,0:T(8,128)S(1)}, u32[]{:S(2)}, u32[]{:S(2)}) collective-permute-start(f32[16,512]{1,0:T(8,128)S(1)} %get-tuple-element.23.refs_0_), channel_id=1, source_target_pairs={{0,8},{4,12},{8,0},{12,4},{1,9},{5,13},{9,1},{13,5},{2,10},{6,14},... | collective-permute-start | bytes 98312 | tf_op jit(solution)/shard_map/ppermute | solution.py:454
  6.9 1.3 %collective-permute-start.2 = (f32[16,512]{1,0:T(8,128)S(1)}, f32[16,512]{1,0:T(8,128)S(1)}, u32[]{:S(2)}, u32[]{:S(2)}) collective-permute-start(f32[16,512]{1,0:T(8,128)S(1)} %get-tuple-element.23.refs_0_), channel_id=1, source_target_pairs={{0,12},{4,0},{8,4},{12,8},{1,13},{5,1},{9,5},{13,9},{2,14},{6,2},{... | collective-permute-start | bytes 98312 | tf_op jit(solution)/shard_map/ppermute | solution.py:454
  8.3 0.0 collective-permute-done.refs_1_
  8.3 1.3 %meet_2.1 = (f32[7,32,128]{2,1,0:T(8,128)S(1)}, f32[7,32,128]{2,1,0:T(8,128)S(1)}, f32[6,128,128]{2,1,0:T(8,128)S(1)}, f32[6,128,128]{2,1,0:T(8,128)S(1)}, f32[6...) custom-call(f32[16,512]{1,0:T(8,128)S(1)} %get-tuple-element.23.refs_0_, f32[16,512]{1,0:T(8,128)S(1)} %collective-permute-done.refs_1_), custom_call_target="tpu_custom_call" | custom-call | tf_op jit(solution)/shard_map/meet_2/pallas_call | solution.py:484
  9.6 0.0 collective-permute-done.1.refs_0_.refs_2_
  9.7 0.9 %meet_3.1 = (f32[7,32,128]{2,1,0:T(8,128)S(1)}, f32[6,128,128]{2,1,0:T(8,128)S(1)}, f32[6,128,128]{2,1,0:T(8,128)S(1)}, f32[6,128,128]{2,1,0:T(8,128)S(1)}, f32[6,128,128]{2,1,0:T(8,128)S(1)}) custom-call(f32[16,512]{1,0:T(8,128)S(1)} %collective-permute-done.1.refs_0_.refs_2_, f32[7,32,128]{2,1,0:T(8,128)S(1)} %get-tuple-element.24.refs_1_, ...), custom_call_target="tpu_custom_call" | custom-call | tf_op jit(solution)/shard_map/meet_3/pallas_call | solution.py:484
  10.6 0.3 %collective-permute-done.2.refs_0_.refs_3_ = f32[16,512]{1,0:T(8,128)S(1)} collective-permute-done((f32[16,512]{1,0:T(8,128)S(1)}, f32[16,512]{1,0:T(8,128)S(1)}, u32[]{:S(2)}, u32[]{:S(2)}) %collective-permute-start.2) | collective-permute-done | bytes 32800 | tf_op jit(solution)/shard_map/ppermute | solution.py:454
  10.9 1.5 %meet_4.1 = (f32[8,128]{1,0:T(8,128)S(1)}, f32[8,384]{1,0:T(8,128)S(1)}) custom-call(f32[16,512]{1,0:T(8,128)S(1)} %collective-permute-done.2.refs_0_.refs_3_, f32[7,32,128]{2,1,0:T(8,128)S(1)} %get-tuple-element.24.refs_1_, f32[7,32,128]{2,1,0:T(8,128)S(1)} %get-tuple-element.25.refs_2_, f32[7,32,128]{2,1,0:T(8,128)S(1)} %get-tuple-element.30.refs_3_, ...), custom_call_target="tpu_custom_call" | custom-call | tf_op jit(solution)/shard_map/meet_4/pallas_call | solution.py:484
  12.4 1.5 %collective-permute-start.3 = (f32[8,384]{1,0:T(8,128)S(1)}, f32[8,384]{1,0:T(8,128)S(1)}, u32[]{:S(2)}, u32[]{:S(2)}) collective-permute-start(f32[8,384]{1,0:T(8,128)S(1)} %get-tuple-element.35.refs_4_), channel_id=1, source_target_pairs={{0,1},{1,0},{2,3},{3,2},{4,5},{5,4},{6,7},{7,6},{8,9},{9,8},{10,11... | collective-permute-start | bytes 36872 | tf_op jit(solution)/shard_map/ppermute | solution.py:502
  13.8 0.0 copy-start
  13.8 1.4 %meet_still.1 = (f32[8,128]{1,0:T(8,128)S(1)}, f32[6,128,128]{2,1,0:T(8,128)S(1)}, f32[6,128,128]{2,1,0:T(8,128)S(1)}) custom-call(f32[16,512]{1,0:T(8,128)S(1)} %get-tuple-element.23.refs_0_, f32[16,512]{1,0:T(8,128)S(1)} %collective-permute-done.refs_1_, f32[16,512]{1,0:T(8,128)S(1)} %collective-permute-done.1.refs_0_.refs_2_, ...), custom_call_target="tpu_custom_call" | custom-call | tf_op jit(solution)/shard_map/meet_still/pallas_call | solution.py:504
  15.2 0.0 collective-permute-done.3.refs_5_
  15.2 0.0 copy-done
  15.2 1.4 %finish.1 = f32[12,512]{1,0:T(8,128)} custom-call(f32[16,512]{1,0:T(8,128)S(1)} %get-tuple-element.23.refs_0_, f32[16,512]{1,0:T(8,128)S(1)} %collective-permute-done.refs_1_, f32[16,512]{1,0:T(8,128)S(1)} %collective-permute-done.1.refs_0_.refs_2_, f32[16,512]{1,0:T(8,128)S(1)} %collective-permute-done.2.refs_0_.refs_3_, ...), custom_call_target="tpu_custom_call" | custom-call | tf_op jit(solution)/shard_map/finish/pallas_call | solution.py:513
Async XLA Ops:
  1.2 7.0 %collective-permute-start = (f32[16,512]{1,0:T(8,128)S(1)}, f32[16,512]{1,0:T(8,128)S(1)}, u32[]{:S(2)}, u32[]{:S(2)}) collective-permute-start(f32[16,512]{1,0:T(8,128)S(1)} %get-tuple-element.23.refs_0_), channel_id=1, source_target_pairs={{0,4},{4,8},{8,12},{12,0},{1,5},{5,9},{9,13},{13,1},{2,6},{6,10},{... | collective-permute-start | bytes 98312 | tf_op jit(solution)/shard_map/ppermute | solution.py:454
  4.4 5.3 %collective-permute-start.1 = (f32[16,512]{1,0:T(8,128)S(1)}, f32[16,512]{1,0:T(8,128)S(1)}, u32[]{:S(2)}, u32[]{:S(2)}) collective-permute-start(f32[16,512]{1,0:T(8,128)S(1)} %get-tuple-element.23.refs_0_), channel_id=1, source_target_pairs={{0,8},{4,12},{8,0},{12,4},{1,9},{5,13},{9,1},{13,5},{2,10},{6,14},... | collective-permute-start | bytes 98312 | tf_op jit(solution)/shard_map/ppermute | solution.py:454
  6.9 3.9 %collective-permute-start.2 = (f32[16,512]{1,0:T(8,128)S(1)}, f32[16,512]{1,0:T(8,128)S(1)}, u32[]{:S(2)}, u32[]{:S(2)}) collective-permute-start(f32[16,512]{1,0:T(8,128)S(1)} %get-tuple-element.23.refs_0_), channel_id=1, source_target_pairs={{0,12},{4,0},{8,4},{12,8},{1,13},{5,1},{9,5},{13,9},{2,14},{6,2},{... | collective-permute-start | bytes 98312 | tf_op jit(solution)/shard_map/ppermute | solution.py:454
  12.4 2.9 %collective-permute-start.3 = (f32[8,384]{1,0:T(8,128)S(1)}, f32[8,384]{1,0:T(8,128)S(1)}, u32[]{:S(2)}, u32[]{:S(2)}) collective-permute-start(f32[8,384]{1,0:T(8,128)S(1)} %get-tuple-element.35.refs_4_), channel_id=1, source_target_pairs={{0,1},{1,0},{2,3},{3,2},{4,5},{5,4},{6,7},{7,6},{8,9},{9,8},{10,11... | collective-permute-start | bytes 36872 | tf_op jit(solution)/shard_map/ppermute | solution.py:502
  13.8 1.4 %copy-start = (f32[12,512]{1,0:T(8,128)S(1)}, f32[12,512]{1,0:T(8,128)}, u32[]{:S(2)}) copy-start(f32[12,512]{1,0:T(8,128)} %refs_10_.1) | copy-start | bytes 73732

commit v8 on v7

--- a/solution.py
+++ b/solution.py
@@ -235,21 +235,19 @@
 
 def run_pairs(groups, slots, start, count, together, finish, partial_ref, sums_ref):
     lead = 8 * together
-
-    def reduce(place):
-        for g in range(together):
+    stride = slots + lead
+
+    def reduce(place, many):
+        for g in range(many):
             for j in range(len(groups)):
                 for q in range(6):
                     row = ((g * len(groups) + j) * 6 + q) * 8
-                    sums_ref[pl.ds(j * (slots + lead) + place + 8 * g, 8), q : q + 1] = jnp.sum(
+                    sums_ref[pl.ds(j * stride + place + 8 * g, 8), q : q + 1] = jnp.sum(
                         partial_ref[row : row + 8, :], axis=1, keepdims=True
                     )
 
-    def body(step, unused):
-        base = pl.multiple_of(start + step * lead, 8)
-        if finish:
-            reduce(base)
-        for g in range(together):
+    def block(base, many):
+        for g in range(many):
             here = pl.ds(base + 8 * g, 8)
             for j, (target_ref, columns_ref, before_ref, sources, after_ref) in enumerate(groups):
                 if columns_ref is None:
@@ -274,6 +272,12 @@
                         partial_ref[row : row + 8, :] = sums[q]
                     else:
                         after_ref[q, here, :] = sums[q]
+
+    def body(step, unused):
+        base = pl.multiple_of(start + step * lead, 8)
+        if finish:
+            reduce(base, together)
+        block(base, together)
         return unused
 
     if finish:
@@ -281,12 +285,20 @@
         partial_ref[0:used, :] = jnp.zeros((used, 128), jnp.float32)
         if count < slots:
             sums_ref[...] = jnp.zeros_like(sums_ref)
-    lax.fori_loop(0, count // lead, body, 0)
+    steps = count // lead
+    lax.fori_loop(0, steps, body, 0)
+    rest = (count - steps * lead) // 8
+    end = start + steps * lead
+    if finish:
+        reduce(end, together)
+    if rest:
+        block(end, rest)
+        if finish:
+            reduce(end + lead, rest)
     if not finish:
         return None
-    reduce(pl.multiple_of(start + count, 8))
     return [
-        jnp.transpose(sums_ref[j * (slots + lead) + lead : (j + 1) * (slots + lead), :])
+        jnp.transpose(sums_ref[j * stride + lead : (j + 1) * stride, :])
         for j in range(len(groups))
     ]
 
@@ -457,7 +469,7 @@
     owners = lax.axis_size("act")
     shares = (slots,)
     if owners % 2 == 0:
-        first_share = slots // 4 // 32 * 32
+        first_share = slots * 7 // 16 // 8 * 8
         shares = (first_share, slots - first_share)
     source_shape = jax.ShapeDtypeStruct((7, size // 16, 128), jnp.float32)
     target_shape = jax.ShapeDtypeStruct((6, slots, 128), jnp.float32)

time: 16.8 us -> 16.2 us (0.964)
  starting transfers between devices: 8.5 us -> 7.11 us
  Pallas kernels: 7.78 us -> 8.76 us
  waiting for transfers between devices: 0.28 us -> 0.01 us
    ppermute x1, starting transfers between devices: 1.46 us -> 0.07 us  [direct_per_device(): parts.append(lax.ppermute(part, 'act', [(i, i ^ 1) for i in range(owners)]))]
    pallas_call x3, Pallas kernels: 3.76 us -> 4.74 us  [direct_per_device(): pl.pallas_call(functools.partial(meet, slots, shares, known, fresh, last)...]
    ppermute x3, waiting for transfers between devices: 0.28 us -> 0.01 us  [direct_per_device(): sent.append(lax.ppermute(message, 'src', pairs))]
  transfers between devices with their start and end apart: 4 -> 4, of which waited for: 1 -> 0; matrix products, arithmetic and copies ran while one was open for 0% -> 0% of each run, Pallas kernels for 22% -> 26%
where the time goes in v8:
time: 16.2 us; the launch traced here: 16 us
  Pallas kernels  8.76 us (54%)
  starting transfers between devices  7.11 us (44%)
    ppermute x3, starting transfers between devices, direct_per_device(): sent.append(lax.ppermute(message, 'src', pairs))  7.04 us
    pallas_call x3, Pallas kernels, direct_per_device(): pl.pallas_call(functools.partial(meet, slots, shares, known, fresh, last)...  4.74 us
    pallas_call x1, Pallas kernels, direct_per_device(): pl.pallas_call(functools.partial(meet_still, slots, shards), out_shape=(o...  1.4 us
    pallas_call x1, Pallas kernels, direct_per_device(): pl.pallas_call(functools.partial(finish, slots, shards, len(parts)), out_...  1.38 us
    pallas_call x1, Pallas kernels, direct_per_device(): pl.pallas_call(lambda *refs: prepare(slots, size * shards, *refs), out_sh...  1.24 us
  transfers between devices with their start and end apart: 4, of which 0 were waited for; matrix products, arithmetic and copies ran while one was open for 0% of the time, Pallas kernels for 26%

profile of v8, /device:TPU:0, one launch (start us, length us, event | category | flops | bytes accessed | tf_op | source)
XLA Modules:
  0.0 16.0 jit_solution(771245376021406750)
XLA Ops:
  0.0 1.2 %prepare.1 = (f32[16,512]{1,0:T(8,128)S(1)}, f32[8,512]{1,0:T(8,128)S(1)}) custom-call(f32[12,512]{1,0:T(8,128)} %refs_10_.1, f32[1,512]{1,0:T(1,128)} %bitcast.3, f32[1,512]{1,0:T(1,128)} %bitcast.4, s32[1,512]{1,0:T(1,128)} %bitcast.5), custom_call_target="tpu_custom_call" | custom-call | tf_op jit(solution)/shard_map/prepare/pallas_call | solution.py:440
  1.2 3.1 %collective-permute-start = (f32[16,512]{1,0:T(8,128)S(1)}, f32[16,512]{1,0:T(8,128)S(1)}, u32[]{:S(2)}, u32[]{:S(2)}) collective-permute-start(f32[16,512]{1,0:T(8,128)S(1)} %get-tuple-element.23.refs_0_), channel_id=1, source_target_pairs={{0,4},{4,8},{8,12},{12,0},{1,5},{5,9},{9,13},{13,1},{2,6},{6,10},{... | collective-permute-start | bytes 98312 | tf_op jit(solution)/shard_map/ppermute | solution.py:466
  4.4 2.6 %collective-permute-start.1 = (f32[16,512]{1,0:T(8,128)S(1)}, f32[16,512]{1,0:T(8,128)S(1)}, u32[]{:S(2)}, u32[]{:S(2)}) collective-permute-start(f32[16,512]{1,0:T(8,128)S(1)} %get-tuple-element.23.refs_0_), channel_id=1, source_target_pairs={{0,8},{4,12},{8,0},{12,4},{1,9},{5,13},{9,1},{13,5},{2,10},{6,14},... | collective-permute-start | bytes 98312 | tf_op jit(solution)/shard_map/ppermute | solution.py:466
  6.9 1.3 %collective-permute-start.2 = (f32[16,512]{1,0:T(8,128)S(1)}, f32[16,512]{1,0:T(8,128)S(1)}, u32[]{:S(2)}, u32[]{:S(2)}) collective-permute-start(f32[16,512]{1,0:T(8,128)S(1)} %get-tuple-element.23.refs_0_), channel_id=1, source_target_pairs={{0,12},{4,0},{8,4},{12,8},{1,13},{5,1},{9,5},{13,9},{2,14},{6,2},{... | collective-permute-start | bytes 98312 | tf_op jit(solution)/shard_map/ppermute | solution.py:466
  8.3 0.0 collective-permute-done.refs_1_
  8.3 1.5 %meet_2.1 = (f32[7,32,128]{2,1,0:T(8,128)S(1)}, f32[7,32,128]{2,1,0:T(8,128)S(1)}, f32[6,128,128]{2,1,0:T(8,128)S(1)}, f32[6,128,128]{2,1,0:T(8,128)S(1)}, f32[6...) custom-call(f32[16,512]{1,0:T(8,128)S(1)} %get-tuple-element.23.refs_0_, f32[16,512]{1,0:T(8,128)S(1)} %collective-permute-done.refs_1_), custom_call_target="tpu_custom_call" | custom-call | tf_op jit(solution)/shard_map/meet_2/pallas_call | solution.py:496
  9.8 0.0 collective-permute-done.1.refs_0_.refs_2_
  9.8 1.3 %meet_3.1 = (f32[7,32,128]{2,1,0:T(8,128)S(1)}, f32[6,128,128]{2,1,0:T(8,128)S(1)}, f32[6,128,128]{2,1,0:T(8,128)S(1)}, f32[6,128,128]{2,1,0:T(8,128)S(1)}, f32[6,128,128]{2,1,0:T(8,128)S(1)}) custom-call(f32[16,512]{1,0:T(8,128)S(1)} %collective-permute-done.1.refs_0_.refs_2_, f32[7,32,128]{2,1,0:T(8,128)S(1)} %get-tuple-element.24.refs_1_, ...), custom_call_target="tpu_custom_call" | custom-call | tf_op jit(solution)/shard_map/meet_3/pallas_call | solution.py:496
  11.1 0.0 collective-permute-done.2.refs_0_.refs_3_
  11.1 1.9 %meet_4.1 = (f32[8,128]{1,0:T(8,128)S(1)}, f32[8,384]{1,0:T(8,128)S(1)}) custom-call(f32[16,512]{1,0:T(8,128)S(1)} %collective-permute-done.2.refs_0_.refs_3_, f32[7,32,128]{2,1,0:T(8,128)S(1)} %get-tuple-element.24.refs_1_, f32[7,32,128]{2,1,0:T(8,128)S(1)} %get-tuple-element.25.refs_2_, f32[7,32,128]{2,1,0:T(8,128)S(1)} %get-tuple-element.30.refs_3_, ...), custom_call_target="tpu_custom_call" | custom-call | tf_op jit(solution)/shard_map/meet_4/pallas_call | solution.py:496
  13.1 0.1 collective-permute-start.3
  13.2 0.0 copy-start
  13.2 1.4 %meet_still.1 = (f32[8,128]{1,0:T(8,128)S(1)}, f32[6,128,128]{2,1,0:T(8,128)S(1)}, f32[6,128,128]{2,1,0:T(8,128)S(1)}) custom-call(f32[16,512]{1,0:T(8,128)S(1)} %get-tuple-element.23.refs_0_, f32[16,512]{1,0:T(8,128)S(1)} %collective-permute-done.refs_1_, f32[16,512]{1,0:T(8,128)S(1)} %collective-permute-done.1.refs_0_.refs_2_, ...), custom_call_target="tpu_custom_call" | custom-call | tf_op jit(solution)/shard_map/meet_still/pallas_call | solution.py:516
  14.6 0.0 collective-permute-done.3.refs_5_
  14.6 0.0 copy-done
  14.6 1.4 %finish.1 = f32[12,512]{1,0:T(8,128)} custom-call(f32[16,512]{1,0:T(8,128)S(1)} %get-tuple-element.23.refs_0_, f32[16,512]{1,0:T(8,128)S(1)} %collective-permute-done.refs_1_, f32[16,512]{1,0:T(8,128)S(1)} %collective-permute-done.1.refs_0_.refs_2_, f32[16,512]{1,0:T(8,128)S(1)} %collective-permute-done.2.refs_0_.refs_3_, ...), custom_call_target="tpu_custom_call" | custom-call | tf_op jit(solution)/shard_map/finish/pallas_call | solution.py:525
Async XLA Ops:
  1.2 7.0 %collective-permute-start = (f32[16,512]{1,0:T(8,128)S(1)}, f32[16,512]{1,0:T(8,128)S(1)}, u32[]{:S(2)}, u32[]{:S(2)}) collective-permute-start(f32[16,512]{1,0:T(8,128)S(1)} %get-tuple-element.23.refs_0_), channel_id=1, source_target_pairs={{0,4},{4,8},{8,12},{12,0},{1,5},{5,9},{9,13},{13,1},{2,6},{6,10},{... | collective-permute-start | bytes 98312 | tf_op jit(solution)/shard_map/ppermute | solution.py:466
  4.4 5.5 %collective-permute-start.1 = (f32[16,512]{1,0:T(8,128)S(1)}, f32[16,512]{1,0:T(8,128)S(1)}, u32[]{:S(2)}, u32[]{:S(2)}) collective-permute-start(f32[16,512]{1,0:T(8,128)S(1)} %get-tuple-element.23.refs_0_), channel_id=1, source_target_pairs={{0,8},{4,12},{8,0},{12,4},{1,9},{5,13},{9,1},{13,5},{2,10},{6,14},... | collective-permute-start | bytes 98312 | tf_op jit(solution)/shard_map/ppermute | solution.py:466
  6.9 4.2 %collective-permute-start.2 = (f32[16,512]{1,0:T(8,128)S(1)}, f32[16,512]{1,0:T(8,128)S(1)}, u32[]{:S(2)}, u32[]{:S(2)}) collective-permute-start(f32[16,512]{1,0:T(8,128)S(1)} %get-tuple-element.23.refs_0_), channel_id=1, source_target_pairs={{0,12},{4,0},{8,4},{12,8},{1,13},{5,1},{9,5},{13,9},{2,14},{6,2},{... | collective-permute-start | bytes 98312 | tf_op jit(solution)/shard_map/ppermute | solution.py:466
  13.1 1.5 %collective-permute-start.3 = (f32[8,384]{1,0:T(8,128)S(1)}, f32[8,384]{1,0:T(8,128)S(1)}, u32[]{:S(2)}, u32[]{:S(2)}) collective-permute-start(f32[8,384]{1,0:T(8,128)S(1)} %get-tuple-element.35.refs_4_), channel_id=1, source_target_pairs={{0,1},{1,0},{2,3},{3,2},{4,5},{5,4},{6,7},{7,6},{8,9},{9,8},{10,11... | collective-permute-start | bytes 36872 | tf_op jit(solution)/shard_map/ppermute | solution.py:514
  13.2 1.4 %copy-start = (f32[12,512]{1,0:T(8,128)S(1)}, f32[12,512]{1,0:T(8,128)}, u32[]{:S(2)}) copy-start(f32[12,512]{1,0:T(8,128)} %refs_10_.1) | copy-start | bytes 73732

commit v9 on v8

--- a/solution.py
+++ b/solution.py
@@ -469,7 +469,7 @@
     owners = lax.axis_size("act")
     shares = (slots,)
     if owners % 2 == 0:
-        first_share = slots * 7 // 16 // 8 * 8
+        first_share = slots * 3 // 8 // 16 * 16
         shares = (first_share, slots - first_share)
     source_shape = jax.ShapeDtypeStruct((7, size // 16, 128), jnp.float32)
     target_shape = jax.ShapeDtypeStruct((6, slots, 128), jnp.float32)

time: 16.2 us -> 16.1 us (level)
  starting transfers between devices: 7.11 us -> 7.48 us
  Pallas kernels: 8.76 us -> 8.41 us
    ppermute x1, starting transfers between devices: 0.07 us -> 0.43 us  [direct_per_device(): parts.append(lax.ppermute(part, 'act', [(i, i ^ 1) for i in range(owners)]))]
    pallas_call x3, Pallas kernels: 4.74 us -> 4.39 us  [direct_per_device(): pl.pallas_call(functools.partial(meet, slots, shares, known, fresh, last)...]
  transfers between devices with their start and end apart: 4 -> 4, of which waited for: 0 -> 0; matrix products, arithmetic and copies ran while one was open for 0% -> 0% of each run, Pallas kernels for 26% -> 25%
where the time goes in v9:
time: 16.1 us; the launch traced here: 16 us
  Pallas kernels  8.41 us (52%)
  starting transfers between devices  7.48 us (46%)
    ppermute x3, starting transfers between devices, direct_per_device(): sent.append(lax.ppermute(message, 'src', pairs))  7.04 us
    pallas_call x3, Pallas kernels, direct_per_device(): pl.pallas_call(functools.partial(meet, slots, shares, known, fresh, last)...  4.39 us
    pallas_call x1, Pallas kernels, direct_per_device(): pl.pallas_call(functools.partial(meet_still, slots, shards), out_shape=(o...  1.39 us
    pallas_call x1, Pallas kernels, direct_per_device(): pl.pallas_call(functools.partial(finish, slots, shards, len(parts)), out_...  1.38 us
    pallas_call x1, Pallas kernels, direct_per_device(): pl.pallas_call(lambda *refs: prepare(slots, size * shards, *refs), out_sh...  1.24 us
    ppermute x1, starting transfers between devices, direct_per_device(): parts.append(lax.ppermute(part, 'act', [(i, i ^ 1) for i in range(owners)]))  0.43 us
  transfers between devices with their start and end apart: 4, of which 0 were waited for; matrix products, arithmetic and copies ran while one was open for 0% of the time, Pallas kernels for 25%

profile of v9, /device:TPU:0, one launch (start us, length us, event | category | flops | bytes accessed | tf_op | source)
XLA Modules:
  0.0 16.0 jit_solution(2587217526925954512)
XLA Ops:
  0.0 1.2 %prepare.1 = (f32[16,512]{1,0:T(8,128)S(1)}, f32[8,512]{1,0:T(8,128)S(1)}) custom-call(f32[12,512]{1,0:T(8,128)} %refs_10_.1, f32[1,512]{1,0:T(1,128)} %bitcast.3, f32[1,512]{1,0:T(1,128)} %bitcast.4, s32[1,512]{1,0:T(1,128)} %bitcast.5), custom_call_target="tpu_custom_call" | custom-call | tf_op jit(solution)/shard_map/prepare/pallas_call | solution.py:440
  1.2 3.1 %collective-permute-start = (f32[16,512]{1,0:T(8,128)S(1)}, f32[16,512]{1,0:T(8,128)S(1)}, u32[]{:S(2)}, u32[]{:S(2)}) collective-permute-start(f32[16,512]{1,0:T(8,128)S(1)} %get-tuple-element.23.refs_0_), channel_id=1, source_target_pairs={{0,4},{4,8},{8,12},{12,0},{1,5},{5,9},{9,13},{13,1},{2,6},{6,10},{... | collective-permute-start | bytes 98312 | tf_op jit(solution)/shard_map/ppermute | solution.py:466
  4.4 2.6 %collective-permute-start.1 = (f32[16,512]{1,0:T(8,128)S(1)}, f32[16,512]{1,0:T(8,128)S(1)}, u32[]{:S(2)}, u32[]{:S(2)}) collective-permute-start(f32[16,512]{1,0:T(8,128)S(1)} %get-tuple-element.23.refs_0_), channel_id=1, source_target_pairs={{0,8},{4,12},{8,0},{12,4},{1,9},{5,13},{9,1},{13,5},{2,10},{6,14},... | collective-permute-start | bytes 98312 | tf_op jit(solution)/shard_map/ppermute | solution.py:466
  6.9 1.3 %collective-permute-start.2 = (f32[16,512]{1,0:T(8,128)S(1)}, f32[16,512]{1,0:T(8,128)S(1)}, u32[]{:S(2)}, u32[]{:S(2)}) collective-permute-start(f32[16,512]{1,0:T(8,128)S(1)} %get-tuple-element.23.refs_0_), channel_id=1, source_target_pairs={{0,12},{4,0},{8,4},{12,8},{1,13},{5,1},{9,5},{13,9},{2,14},{6,2},{... | collective-permute-start | bytes 98312 | tf_op jit(solution)/shard_map/ppermute | solution.py:466
  8.3 0.0 collective-permute-done.refs_1_
  8.3 1.4 %meet_2.1 = (f32[7,32,128]{2,1,0:T(8,128)S(1)}, f32[7,32,128]{2,1,0:T(8,128)S(1)}, f32[6,128,128]{2,1,0:T(8,128)S(1)}, f32[6,128,128]{2,1,0:T(8,128)S(1)}, f32[6...) custom-call(f32[16,512]{1,0:T(8,128)S(1)} %get-tuple-element.23.refs_0_, f32[16,512]{1,0:T(8,128)S(1)} %collective-permute-done.refs_1_), custom_call_target="tpu_custom_call" | custom-call | tf_op jit(solution)/shard_map/meet_2/pallas_call | solution.py:496
  9.8 0.0 collective-permute-done.1.refs_0_.refs_2_
  9.8 1.1 %meet_3.1 = (f32[7,32,128]{2,1,0:T(8,128)S(1)}, f32[6,128,128]{2,1,0:T(8,128)S(1)}, f32[6,128,128]{2,1,0:T(8,128)S(1)}, f32[6,128,128]{2,1,0:T(8,128)S(1)}, f32[6,128,128]{2,1,0:T(8,128)S(1)}) custom-call(f32[16,512]{1,0:T(8,128)S(1)} %collective-permute-done.1.refs_0_.refs_2_, f32[7,32,128]{2,1,0:T(8,128)S(1)} %get-tuple-element.24.refs_1_, ...), custom_call_target="tpu_custom_call" | custom-call | tf_op jit(solution)/shard_map/meet_3/pallas_call | solution.py:496
  10.9 0.0 collective-permute-done.2.refs_0_.refs_3_
  10.9 1.8 %meet_4.1 = (f32[8,128]{1,0:T(8,128)S(1)}, f32[8,384]{1,0:T(8,128)S(1)}) custom-call(f32[16,512]{1,0:T(8,128)S(1)} %collective-permute-done.2.refs_0_.refs_3_, f32[7,32,128]{2,1,0:T(8,128)S(1)} %get-tuple-element.24.refs_1_, f32[7,32,128]{2,1,0:T(8,128)S(1)} %get-tuple-element.25.refs_2_, f32[7,32,128]{2,1,0:T(8,128)S(1)} %get-tuple-element.30.refs_3_, ...), custom_call_target="tpu_custom_call" | custom-call | tf_op jit(solution)/shard_map/meet_4/pallas_call | solution.py:496
  12.7 0.4 %collective-permute-start.3 = (f32[8,384]{1,0:T(8,128)S(1)}, f32[8,384]{1,0:T(8,128)S(1)}, u32[]{:S(2)}, u32[]{:S(2)}) collective-permute-start(f32[8,384]{1,0:T(8,128)S(1)} %get-tuple-element.35.refs_4_), channel_id=1, source_target_pairs={{0,1},{1,0},{2,3},{3,2},{4,5},{5,4},{6,7},{7,6},{8,9},{9,8},{10,11... | collective-permute-start | bytes 36872 | tf_op jit(solution)/shard_map/ppermute | solution.py:514
  13.2 0.0 copy-start
  13.2 1.4 %meet_still.1 = (f32[8,128]{1,0:T(8,128)S(1)}, f32[6,128,128]{2,1,0:T(8,128)S(1)}, f32[6,128,128]{2,1,0:T(8,128)S(1)}) custom-call(f32[16,512]{1,0:T(8,128)S(1)} %get-tuple-element.23.refs_0_, f32[16,512]{1,0:T(8,128)S(1)} %collective-permute-done.refs_1_, f32[16,512]{1,0:T(8,128)S(1)} %collective-permute-done.1.refs_0_.refs_2_, ...), custom_call_target="tpu_custom_call" | custom-call | tf_op jit(solution)/shard_map/meet_still/pallas_call | solution.py:516
  14.6 0.0 collective-permute-done.3.refs_5_
  14.6 0.0 copy-done
  14.6 1.4 %finish.1 = f32[12,512]{1,0:T(8,128)} custom-call(f32[16,512]{1,0:T(8,128)S(1)} %get-tuple-element.23.refs_0_, f32[16,512]{1,0:T(8,128)S(1)} %collective-permute-done.refs_1_, f32[16,512]{1,0:T(8,128)S(1)} %collective-permute-done.1.refs_0_.refs_2_, f32[16,512]{1,0:T(8,128)S(1)} %collective-permute-done.2.refs_0_.refs_3_, ...), custom_call_target="tpu_custom_call" | custom-call | tf_op jit(solution)/shard_map/finish/pallas_call | solution.py:525
Async XLA Ops:
  1.2 7.0 %collective-permute-start = (f32[16,512]{1,0:T(8,128)S(1)}, f32[16,512]{1,0:T(8,128)S(1)}, u32[]{:S(2)}, u32[]{:S(2)}) collective-permute-start(f32[16,512]{1,0:T(8,128)S(1)} %get-tuple-element.23.refs_0_), channel_id=1, source_target_pairs={{0,4},{4,8},{8,12},{12,0},{1,5},{5,9},{9,13},{13,1},{2,6},{6,10},{... | collective-permute-start | bytes 98312 | tf_op jit(solution)/shard_map/ppermute | solution.py:466
  4.4 5.4 %collective-permute-start.1 = (f32[16,512]{1,0:T(8,128)S(1)}, f32[16,512]{1,0:T(8,128)S(1)}, u32[]{:S(2)}, u32[]{:S(2)}) collective-permute-start(f32[16,512]{1,0:T(8,128)S(1)} %get-tuple-element.23.refs_0_), channel_id=1, source_target_pairs={{0,8},{4,12},{8,0},{12,4},{1,9},{5,13},{9,1},{13,5},{2,10},{6,14},... | collective-permute-start | bytes 98312 | tf_op jit(solution)/shard_map/ppermute | solution.py:466
  6.9 4.0 %collective-permute-start.2 = (f32[16,512]{1,0:T(8,128)S(1)}, f32[16,512]{1,0:T(8,128)S(1)}, u32[]{:S(2)}, u32[]{:S(2)}) collective-permute-start(f32[16,512]{1,0:T(8,128)S(1)} %get-tuple-element.23.refs_0_), channel_id=1, source_target_pairs={{0,12},{4,0},{8,4},{12,8},{1,13},{5,1},{9,5},{13,9},{2,14},{6,2},{... | collective-permute-start | bytes 98312 | tf_op jit(solution)/shard_map/ppermute | solution.py:466
  12.7 1.8 %collective-permute-start.3 = (f32[8,384]{1,0:T(8,128)S(1)}, f32[8,384]{1,0:T(8,128)S(1)}, u32[]{:S(2)}, u32[]{:S(2)}) collective-permute-start(f32[8,384]{1,0:T(8,128)S(1)} %get-tuple-element.35.refs_4_), channel_id=1, source_target_pairs={{0,1},{1,0},{2,3},{3,2},{4,5},{5,4},{6,7},{7,6},{8,9},{9,8},{10,11... | collective-permute-start | bytes 36872 | tf_op jit(solution)/shard_map/ppermute | solution.py:514
  13.2 1.4 %copy-start = (f32[12,512]{1,0:T(8,128)S(1)}, f32[12,512]{1,0:T(8,128)}, u32[]{:S(2)}) copy-start(f32[12,512]{1,0:T(8,128)} %refs_10_.1) | copy-start | bytes 73732

commit v10 on v9

--- a/solution.py
+++ b/solution.py
@@ -6,6 +6,7 @@
 from jax.experimental import pallas as pl
 from jax.experimental.pallas import tpu as pltpu
 from jax.sharding import PartitionSpec as P
+
 
 LEVELS = 5
 STEPS = 2
@@ -56,7 +57,7 @@
         return (running + pair_block(targets, portion), None)
 
     init = jnp.zeros((6, targets.shape[1]), jnp.float32)
-    running, unused = lax.scan(accumulate, init, blocks)
+    running, _ = lax.scan(accumulate, init, blocks)
     return running
 
 
@@ -303,57 +304,70 @@
     ]
 
 
-def meet(slots, shares, known, fresh, last, *refs):
+def on_member(shares, run):
+    if len(shares) == 1:
+        run(0, shares[0])
+        return
+    member = lax.rem(lax.axis_index("act"), len(shares))
+    for m in range(len(shares)):
+
+        @pl.when(member == m)
+        def _():
+            run(sum(shares[:m]), shares[m])
+
+
+def meet(slots, shares, known, fresh, *refs):
     every = known + fresh
     sent, refs = refs[:fresh], refs[fresh:]
     old_sources, old_targets, before = refs[:known], refs[known : 2 * known], refs[2 * known : 3 * known]
     refs = refs[3 * known :]
-    own_ref = forces_ref = own_partial = own_sums = partial_ref = sums_ref = None
-    if last:
-        own_ref, forces_ref, refs = refs[0], refs[1], refs[2:]
-        new_sources, refs = refs[:fresh], refs[fresh:]
-        new_targets = (None,) * fresh
-        after = (None,) * every
-        columns_ref, own_partial, own_sums, partial_ref, sums_ref = refs
-    else:
-        new_sources, new_targets, after = refs[:fresh], refs[fresh : 2 * fresh], refs[2 * fresh : 2 * fresh + every]
-        columns_ref = refs[2 * fresh + every]
+    new_sources, new_targets, after = refs[:fresh], refs[fresh : 2 * fresh], refs[2 * fresh : 2 * fresh + every]
+    columns_ref = refs[2 * fresh + every]
     sources = old_sources + new_sources
-
-    for d in range(fresh):
-        spread_sources(sent[d][0:8, :], new_sources[d], 0)
-        if known + d > 0:
-            columns_ref[...] = jnp.transpose(sent[d][0:8, 0:slots])
-    if known == 0:
-        spread_targets(sent[0][0:8, 0:slots], new_targets[0], 0, slots)
-        own = (new_targets[0], None, None, sources, after[0])
-    else:
-        own = (old_targets[0], None, before[0], new_sources, after[0])
-    own = run_pairs([own], slots, 0, slots, 4 if known == 0 else 8, last, own_partial, own_sums)
-    if last:
-        own_ref[...] = own[0]
 
     def run(start, count):
         groups = []
-        for d in range(1, known):
+        for d in range(known):
             groups.append((old_targets[d], None, before[d], new_sources, after[d]))
-        for d in range(max(known, 1), every):
-            groups.append((new_targets[d - known], columns_ref, None, sources, after[d]))
-        together = 4 if known == 0 else 2
-        forces = run_pairs(groups, slots, start, count, together, last, partial_ref, sums_ref)
-        if last:
-            for d in range(1, every):
-                forces_ref[:, (d - 1) * slots : d * slots] = forces[d - 1]
-
-    if len(shares) == 1:
-        run(0, slots)
-        return
-    member = lax.rem(lax.axis_index("act"), len(shares))
-    for m in range(len(shares)):
-
-        @pl.when(member == m)
-        def _():
-            run(sum(shares[:m]), shares[m])
+        for d in range(fresh):
+            spread_sources(sent[d][0:8, :], new_sources[d], 0)
+            in_loop = None
+            if known:
+                in_loop = columns_ref
+                columns_ref[...] = jnp.transpose(sent[d][0:8, 0:slots])
+            else:
+                spread_targets(sent[d][0:8, 0:slots], new_targets[d], start, count)
+            groups.append((new_targets[d], in_loop, None, sources, after[known + d]))
+        run_pairs(groups, slots, start, count, 2, False, None, None)
+
+    on_member(shares, run)
+
+
+def meet_own(slots, shares, sent_ref, target_ref, before_ref, source_ref, own_ref, *scratch):
+    spread_sources(sent_ref[0:8, :], source_ref, 0)
+
+    def run(start, count):
+        group = (target_ref, None, before_ref, (source_ref,), None)
+        own_ref[...] = run_pairs(
+            [group], slots, start, count, count // 8, True, scratch[0], scratch[1]
+        )[0]
+
+    on_member(shares, run)
+
+
+def meet_rest(slots, shares, known, sent_ref, source_ref, *refs):
+    sources, targets, before = refs[:known], refs[known : 2 * known - 1], refs[2 * known - 1 : 3 * known - 2]
+    forces_ref, columns_ref, partial_ref, sums_ref = refs[3 * known - 2 :]
+    columns_ref[...] = jnp.transpose(sent_ref[0:8, 0:slots])
+
+    def run(start, count):
+        groups = [(t, None, b, (source_ref,), None) for t, b in zip(targets, before)]
+        groups.append((None, columns_ref, None, sources + (source_ref,), None))
+        forces = run_pairs(groups, slots, start, count, 2, True, partial_ref, sums_ref)
+        for d in range(known):
+            forces_ref[:, d * slots : (d + 1) * slots] = forces[d]
+
+    on_member(shares, run)
 
 
 def first_step(slots, sent, forces):
@@ -372,9 +386,11 @@
     return jnp.where(active, jnp.concatenate([ahead, speed], axis=0), sent[8:14, 0:slots])
 
 
-def meet_still(slots, shards, *refs):
+def meet_still(slots, shards, parts, *refs):
     sent, refs = refs[:shards], refs[shards:]
+    shares, refs = refs[:parts], refs[parts:]
     own_ref, again_ref, target_ref, after_ref, still_ref = refs
+    own_ref[...] = shares[0][...] + shares[1][...] if parts == 2 else shares[0][...]
     size = sent[0].shape[1]
     chunks = size // 128
     first = slots // 128
@@ -471,70 +487,74 @@
     if owners % 2 == 0:
         first_share = slots * 3 // 8 // 16 * 16
         shares = (first_share, slots - first_share)
+    parts = len(shares)
+
+    def with_other(part):
+        if parts == 1:
+            return [part]
+        return [part, lax.ppermute(part, "act", [(i, i ^ 1) for i in range(owners)])]
+
+    def call(body, operands, out_shape, scratch=(), pairs=0):
+        cost = pl.CostEstimate(flops=41 * pairs, bytes_accessed=0, transcendentals=pairs)
+        return pl.pallas_call(
+            body,
+            out_shape=out_shape,
+            in_specs=[whole] * len(operands),
+            out_specs=jax.tree.map(lambda _: whole, out_shape),
+            scratch_shapes=list(scratch),
+            compiler_params=limit,
+            cost_estimate=cost if pairs else None,
+        )(*operands)
+
+    def rows(shape):
+        return pltpu.VMEM(shape, jnp.float32)
+
     source_shape = jax.ShapeDtypeStruct((7, size // 16, 128), jnp.float32)
     target_shape = jax.ShapeDtypeStruct((6, slots, 128), jnp.float32)
     own_shape = jax.ShapeDtypeStruct((8, slots), jnp.float32)
-    columns = pltpu.VMEM((slots, 8), jnp.float32)
     sources, targets, sums = [], [], []
     known = 0
-    for fresh in [2] + [1] * (shards - 2):
+    for fresh in [2] + [1] * (shards - 3):
         every = known + fresh
-        last = every == shards
-        if last:
-            out_shape = (own_shape, jax.ShapeDtypeStruct((8, (shards - 1) * slots), jnp.float32))
-            scratch = [
-                pltpu.VMEM(source_shape.shape, jnp.float32),
-                columns,
-                pltpu.VMEM((8 * 48, 128), jnp.float32),
-                pltpu.VMEM((slots + 64, 8), jnp.float32),
-                pltpu.VMEM((2 * (shards - 1) * 48, 128), jnp.float32),
-                pltpu.VMEM(((shards - 1) * (slots + 16), 8), jnp.float32),
-            ]
-        else:
-            out_shape = [source_shape] * fresh + [target_shape] * (fresh + every)
-            scratch = [columns]
-        outs = pl.pallas_call(
-            functools.partial(meet, slots, shares, known, fresh, last),
-            out_shape=out_shape,
-            in_specs=[whole] * (fresh + 3 * known),
-            out_specs=(whole, whole) if last else [whole] * (2 * fresh + every),
-            scratch_shapes=scratch,
-            compiler_params=limit,
-            name=f"meet_{every}",
-        )(*sent[known:every], *sources, *targets, *sums)
-        if last:
-            break
+        outs = call(
+            functools.partial(meet, slots, shares, known, fresh),
+            [*sent[known:every], *sources, *targets, *sums],
+            [source_shape] * fresh + [target_shape] * (fresh + every),
+            [rows((slots, 8))],
+        )
         sources += outs[:fresh]
         targets += outs[fresh : 2 * fresh]
         sums = list(outs[2 * fresh :])
         known = every
-    own, part = outs
-    parts = [part]
-    if len(shares) == 2:
-        parts.append(lax.ppermute(part, "act", [(i, i ^ 1) for i in range(owners)]))
+    source, own = call(
+        functools.partial(meet_own, slots, shares),
+        [sent[known], targets[0], sums[0]],
+        (source_shape, own_shape),
+        [rows((max(shares) * 6, 128)), rows((slots + max(shares), 8))],
+    )
+    own = with_other(own)
+    forces = call(
+        functools.partial(meet_rest, slots, shares, known),
+        [sent[known], source, *sources, *targets[1:], *sums[1:]],
+        jax.ShapeDtypeStruct((8, known * slots), jnp.float32),
+        [rows((slots, 8)), rows((2 * known * 48, 128)), rows((known * (slots + 16), 8))],
+        2 * known * max(shares) * size,
+    )
+    forces = with_other(forces)
     first = slots // 128
-    again, target, still = pl.pallas_call(
-        functools.partial(meet_still, slots, shards),
-        out_shape=(own_shape, target_shape, target_shape),
-        in_specs=[whole] * (shards + 1),
-        out_specs=(whole,) * 3,
-        scratch_shapes=[pltpu.VMEM((7, shards * (size // 128 - first) * 8, 128), jnp.float32)],
-        compiler_params=limit,
-        name="meet_still",
-    )(*sent, own)
-    return pl.pallas_call(
-        functools.partial(finish, slots, shards, len(parts)),
-        out_shape=jax.ShapeDtypeStruct((12, size), jnp.float32),
-        in_specs=[whole] * (shards + len(parts) + 6),
-        out_specs=whole,
-        scratch_shapes=[
-            pltpu.VMEM((7, shards * first * 8, 128), jnp.float32),
-            pltpu.VMEM((8 * 48, 128), jnp.float32),
-            pltpu.VMEM((slots + 64, 8), jnp.float32),
-        ],
-        compiler_params=limit,
-        name="finish",
-    )(*sent, *parts, own, again, target, still, star_state, place)
+    own, again, target, still = call(
+        functools.partial(meet_still, slots, shards, parts),
+        [*sent, *own],
+        (own_shape, own_shape, target_shape, target_shape),
+        [rows((7, shards * (size // 128 - first) * 8, 128))],
+        slots * shards * (size - slots),
+    )
+    return call(
+        functools.partial(finish, slots, shards, parts),
+        [*sent, *forces, own, again, target, still, star_state, place],
+        jax.ShapeDtypeStruct((12, size), jnp.float32),
+        [rows((7, shards * first * 8, 128)), rows((8 * 48, 128)), rows((slots + 64, 8))],
+    )
 
 
 def solution(mesh):

time: 16.1 us -> 16.8 us (1.043)
  waiting for transfers between devices: 0.01 us -> 1.79 us
  Pallas kernels: 8.41 us -> 7.16 us
    pallas_call x5 -> x6, Pallas kernels: 7.17 us -> 5.92 us  [call(): pl.pallas_call(body, out_shape=out_shape, in_specs=[whole] * len(operands...]
    ppermute x3, waiting for transfers between devices: 0.01 us -> 0.96 us  [direct_per_device(): sent.append(lax.ppermute(message, 'src', pairs))]
    ppermute x1 -> x2, waiting for transfers between devices: 0.01 us -> 0.83 us  [with_other(): lax.ppermute(part, 'act', [(i, i ^ 1) for i in range(owners)])]
    ppermute x1 -> x2, starting transfers between devices: 0.43 us -> 0.54 us  [with_other(): lax.ppermute(part, 'act', [(i, i ^ 1) for i in range(owners)])]
  transfers between devices with their start and end apart: 4 -> 5, of which waited for: 0 -> 3; matrix products, arithmetic and copies ran while one was open for 0% -> 0% of each run, Pallas kernels for 25% -> 18%
where the time goes in v10:
time: 16.8 us; the launch traced here: 16.6 us
  starting transfers between devices  7.58 us (45%)
  Pallas kernels  7.16 us (43%)
  waiting for transfers between devices  1.79 us (11%)
    ppermute x3, starting transfers between devices, direct_per_device(): sent.append(lax.ppermute(message, 'src', pairs))  7.04 us
    pallas_call x6, Pallas kernels, call(): pl.pallas_call(body, out_shape=out_shape, in_specs=[whole] * len(operands...  5.92 us
    pallas_call x1, Pallas kernels, direct_per_device(): pl.pallas_call(lambda *refs: prepare(slots, size * shards, *refs), out_sh...  1.24 us
    ppermute x3, waiting for transfers between devices, direct_per_device(): sent.append(lax.ppermute(message, 'src', pairs))  0.96 us
    ppermute x2, waiting for transfers between devices, with_other(): lax.ppermute(part, 'act', [(i, i ^ 1) for i in range(owners)])  0.83 us
    ppermute x2, starting transfers between devices, with_other(): lax.ppermute(part, 'act', [(i, i ^ 1) for i in range(owners)])  0.54 us
  transfers between devices with their start and end apart: 5, of which 3 were waited for; matrix products, arithmetic and copies ran while one was open for 0% of the time, Pallas kernels for 18%

profile of v10, /device:TPU:0, one launch (start us, length us, event | category | flops | bytes accessed | tf_op | source)
XLA Modules:
  0.0 16.6 jit_solution(3231132543804946820)
XLA Ops:
  0.0 1.2 %prepare.1 = (f32[16,512]{1,0:T(8,128)S(1)}, f32[8,512]{1,0:T(8,128)S(1)}) custom-call(f32[12,512]{1,0:T(8,128)} %refs_10_.1, f32[1,512]{1,0:T(1,128)} %bitcast.3, f32[1,512]{1,0:T(1,128)} %bitcast.4, s32[1,512]{1,0:T(1,128)} %bitcast.5), custom_call_target="tpu_custom_call" | custom-call | tf_op jit(solution)/shard_map/prepare/pallas_call | solution.py:456
  1.2 3.1 %collective-permute-start = (f32[16,512]{1,0:T(8,128)S(1)}, f32[16,512]{1,0:T(8,128)S(1)}, u32[]{:S(2)}, u32[]{:S(2)}) collective-permute-start(f32[16,512]{1,0:T(8,128)S(1)} %get-tuple-element.24.refs_0_), channel_id=1, source_target_pairs={{0,4},{4,8},{8,12},{12,0},{1,5},{5,9},{9,13},{13,1},{2,6},{6,10},{... | collective-permute-start | bytes 98312 | tf_op jit(solution)/shard_map/ppermute | solution.py:482
  4.4 2.6 %collective-permute-start.1 = (f32[16,512]{1,0:T(8,128)S(1)}, f32[16,512]{1,0:T(8,128)S(1)}, u32[]{:S(2)}, u32[]{:S(2)}) collective-permute-start(f32[16,512]{1,0:T(8,128)S(1)} %get-tuple-element.24.refs_0_), channel_id=1, source_target_pairs={{0,8},{4,12},{8,0},{12,4},{1,9},{5,13},{9,1},{13,5},{2,10},{6,14},... | collective-permute-start | bytes 98312 | tf_op jit(solution)/shard_map/ppermute | solution.py:482
  6.9 1.3 %collective-permute-start.2 = (f32[16,512]{1,0:T(8,128)S(1)}, f32[16,512]{1,0:T(8,128)S(1)}, u32[]{:S(2)}, u32[]{:S(2)}) collective-permute-start(f32[16,512]{1,0:T(8,128)S(1)} %get-tuple-element.24.refs_0_), channel_id=1, source_target_pairs={{0,12},{4,0},{8,4},{12,8},{1,13},{5,1},{9,5},{13,9},{2,14},{6,2},{... | collective-permute-start | bytes 98312 | tf_op jit(solution)/shard_map/ppermute | solution.py:482
  8.3 0.0 collective-permute-done.refs_1_
  8.3 0.8 %shard_map.46 = (f32[7,32,128]{2,1,0:T(8,128)S(1)}, f32[7,32,128]{2,1,0:T(8,128)S(1)}, f32[6,128,128]{2,1,0:T(8,128)S(1)}, f32[6,128,128]{2,1,0:T(8,128)S(1)}, f...) custom-call(f32[16,512]{1,0:T(8,128)S(1)} %get-tuple-element.24.refs_0_, f32[16,512]{1,0:T(8,128)S(1)} %collective-permute-done.refs_1_), custom_call_target="tpu_custom_call" | custom-call | tf_op jit(solution)/shard_map/pallas_call | solution.py:499
  9.1 0.4 %collective-permute-done.1.refs_0_.refs_2_ = f32[16,512]{1,0:T(8,128)S(1)} collective-permute-done((f32[16,512]{1,0:T(8,128)S(1)}, f32[16,512]{1,0:T(8,128)S(1)}, u32[]{:S(2)}, u32[]{:S(2)}) %collective-permute-start.1) | collective-permute-done | bytes 32800 | tf_op jit(solution)/shard_map/ppermute | solution.py:482
  9.5 0.8 %shard_map.47 = (f32[7,32,128]{2,1,0:T(8,128)S(1)}, f32[6,128,128]{2,1,0:T(8,128)S(1)}, f32[6,128,128]{2,1,0:T(8,128)S(1)}, f32[6,128,128]{2,1,0:T(8,128)S(1)}, f32[6,128,128]{2,1,0:T(8,128)S(1)}) custom-call(f32[16,512]{1,0:T(8,128)S(1)} %collective-permute-done.1.refs_0_.refs_2_, f32[7,32,128]{2,1,0:T(8,128)S(1)} %get-tuple-element.26.refs_1_.refs_0_, ...), custom_call_target="tpu_custom_call" | custom-call | tf_op jit(solution)/shard_map/pallas_call | solution.py:499
  10.3 0.5 %collective-permute-done.2.sent_ref.refs_3_ = f32[16,512]{1,0:T(8,128)S(1)} collective-permute-done((f32[16,512]{1,0:T(8,128)S(1)}, f32[16,512]{1,0:T(8,128)S(1)}, u32[]{:S(2)}, u32[]{:S(2)}) %collective-permute-start.2) | collective-permute-done | bytes 32800 | tf_op jit(solution)/shard_map/ppermute | solution.py:482
  10.9 0.3 %shard_map.48 = (f32[7,32,128]{2,1,0:T(8,128)S(1)}, f32[8,128]{1,0:T(8,128)S(1)}) custom-call(f32[16,512]{1,0:T(8,128)S(1)} %collective-permute-done.2.sent_ref.refs_3_, f32[6,128,128]{2,1,0:T(8,128)S(1)} %get-tuple-element.25.refs_3_.target_ref, f32[6,128,128]{2,1,0:T(8,128)S(1)} %get-tuple-element.31.before_ref), custom_call_target="tpu_custom_call" | custom-call | tf_op jit(solution)/shard_map/pallas_call | solution.py:499
  11.1 1.3 %shard_map.49.refs_4_ = f32[8,384]{1,0:T(8,128)S(1)} custom-call(f32[16,512]{1,0:T(8,128)S(1)} %collective-permute-done.2.sent_ref.refs_3_, f32[7,32,128]{2,1,0:T(8,128)S(1)} %get-tuple-element.32.source_ref, f32[7,32,128]{2,1,0:T(8,128)S(1)} %get-tuple-element.26.refs_1_.refs_0_, f32[7,32,128]{2,1,0:T(8,128)S(1)} %get-tuple-element.27.refs_2_.refs_1_, ...), custom_call_target="tpu_custom_call" | custom-call | flops 10076160 | tf_op jit(solution)/shard_map/pallas_call | solution.py:499
  12.4 0.1 collective-permute-start.3
  12.5 0.0 copy-start
  12.5 0.5 %collective-permute-start.4 = (f32[8,128]{1,0:T(8,128)S(1)}, f32[8,128]{1,0:T(8,128)S(1)}, u32[]{:S(2)}, u32[]{:S(2)}) collective-permute-start(f32[8,128]{1,0:T(8,128)S(1)} %get-tuple-element.37.refs_4_), channel_id=1, source_target_pairs={{0,1},{1,0},{2,3},{3,2},{4,5},{5,4},{6,7},{7,6},{8,9},{9,8},{10,11... | collective-permute-start | bytes 12296 | tf_op jit(solution)/shard_map/ppermute | solution.py:495
  13.0 0.8 %collective-permute-done.4.refs_5_ = f32[8,128]{1,0:T(8,128)S(1)} collective-permute-done((f32[8,128]{1,0:T(8,128)S(1)}, f32[8,128]{1,0:T(8,128)S(1)}, u32[]{:S(2)}, u32[]{:S(2)}) %collective-permute-start.4) | collective-permute-done | bytes 4128 | tf_op jit(solution)/shard_map/ppermute | solution.py:495
  13.8 1.4 %shard_map.50 = (f32[8,128]{1,0:T(8,128)S(1)}, f32[8,128]{1,0:T(8,128)S(1)}, f32[6,128,128]{2,1,0:T(8,128)S(1)}, f32[6,128,128]{2,1,0:T(8,128)S(1)}) custom-call(f32[16,512]{1,0:T(8,128)S(1)} %get-tuple-element.24.refs_0_, f32[16,512]{1,0:T(8,128)S(1)} %collective-permute-done.refs_1_, f32[16,512]{1,0:T(8,128)S(1)} %collective-permute-done.1.refs_0_.refs_2_, ...), custom_call_target="tpu_custom_call" | custom-call | flops 8060928 | tf_op jit(solution)/shard_map/pallas_call | solution.py:499
  15.2 0.0 collective-permute-done.3.refs_5_
  15.2 0.0 copy-done
  15.2 1.4 %shard_map.51 = f32[12,512]{1,0:T(8,128)} custom-call(f32[16,512]{1,0:T(8,128)S(1)} %get-tuple-element.24.refs_0_, f32[16,512]{1,0:T(8,128)S(1)} %collective-permute-done.refs_1_, f32[16,512]{1,0:T(8,128)S(1)} %collective-permute-done.1.refs_0_.refs_2_, f32[16,512]{1,0:T(8,128)S(1)} %collective-permute-done.2.sent_ref.refs_3_, ...), custom_call_target="tpu_custom_call" | custom-call | tf_op jit(solution)/shard_map/pallas_call | solution.py:499
Async XLA Ops:
  1.2 7.0 %collective-permute-start = (f32[16,512]{1,0:T(8,128)S(1)}, f32[16,512]{1,0:T(8,128)S(1)}, u32[]{:S(2)}, u32[]{:S(2)}) collective-permute-start(f32[16,512]{1,0:T(8,128)S(1)} %get-tuple-element.24.refs_0_), channel_id=1, source_target_pairs={{0,4},{4,8},{8,12},{12,0},{1,5},{5,9},{9,13},{13,1},{2,6},{6,10},{... | collective-permute-start | bytes 98312 | tf_op jit(solution)/shard_map/ppermute | solution.py:482
  4.4 5.2 %collective-permute-start.1 = (f32[16,512]{1,0:T(8,128)S(1)}, f32[16,512]{1,0:T(8,128)S(1)}, u32[]{:S(2)}, u32[]{:S(2)}) collective-permute-start(f32[16,512]{1,0:T(8,128)S(1)} %get-tuple-element.24.refs_0_), channel_id=1, source_target_pairs={{0,8},{4,12},{8,0},{12,4},{1,9},{5,13},{9,1},{13,5},{2,10},{6,14},... | collective-permute-start | bytes 98312 | tf_op jit(solution)/shard_map/ppermute | solution.py:482
  6.9 3.9 %collective-permute-start.2 = (f32[16,512]{1,0:T(8,128)S(1)}, f32[16,512]{1,0:T(8,128)S(1)}, u32[]{:S(2)}, u32[]{:S(2)}) collective-permute-start(f32[16,512]{1,0:T(8,128)S(1)} %get-tuple-element.24.refs_0_), channel_id=1, source_target_pairs={{0,12},{4,0},{8,4},{12,8},{1,13},{5,1},{9,5},{13,9},{2,14},{6,2},{... | collective-permute-start | bytes 98312 | tf_op jit(solution)/shard_map/ppermute | solution.py:482
  12.4 2.8 %collective-permute-start.3 = (f32[8,384]{1,0:T(8,128)S(1)}, f32[8,384]{1,0:T(8,128)S(1)}, u32[]{:S(2)}, u32[]{:S(2)}) collective-permute-start(f32[8,384]{1,0:T(8,128)S(1)} %shard_map.49.refs_4_), channel_id=1, source_target_pairs={{0,1},{1,0},{2,3},{3,2},{4,5},{5,4},{6,7},{7,6},{8,9},{9,8},{10,11... | collective-permute-start | bytes 36872 | tf_op jit(solution)/shard_map/ppermute | solution.py:495
  12.5 2.7 %copy-start = (f32[12,512]{1,0:T(8,128)S(1)}, f32[12,512]{1,0:T(8,128)}, u32[]{:S(2)}) copy-start(f32[12,512]{1,0:T(8,128)} %refs_10_.1) | copy-start | bytes 73732
  12.5 1.3 %collective-permute-start.4 = (f32[8,128]{1,0:T(8,128)S(1)}, f32[8,128]{1,0:T(8,128)S(1)}, u32[]{:S(2)}, u32[]{:S(2)}) collective-permute-start(f32[8,128]{1,0:T(8,128)S(1)} %get-tuple-element.37.refs_4_), channel_id=1, source_target_pairs={{0,1},{1,0},{2,3},{3,2},{4,5},{5,4},{6,7},{7,6},{8,9},{9,8},{10,11... | collective-permute-start | bytes 12296 | tf_op jit(solution)/shard_map/ppermute | solution.py:495

commit v11 on v10

--- a/solution.py
+++ b/solution.py
@@ -305,9 +305,6 @@
 
 
 def on_member(shares, run):
-    if len(shares) == 1:
-        run(0, shares[0])
-        return
     member = lax.rem(lax.axis_index("act"), len(shares))
     for m in range(len(shares)):
 
@@ -343,31 +340,49 @@
     on_member(shares, run)
 
 
-def meet_own(slots, shares, sent_ref, target_ref, before_ref, source_ref, own_ref, *scratch):
+def meet_own(slots, shares, sent_ref, own_target, own_before, *refs):
+    known = len(refs) - 9
+    sources = refs[:known]
+    source_ref, own_ref, late_ref, target_ref, own_partial, own_sums, partial_ref, sums_ref, _ = refs[known:]
     spread_sources(sent_ref[0:8, :], source_ref, 0)
 
-    def run(start, count):
-        group = (target_ref, None, before_ref, (source_ref,), None)
+    def own(start, count):
+        group = (own_target, None, own_before, (source_ref,), None)
         own_ref[...] = run_pairs(
-            [group], slots, start, count, count // 8, True, scratch[0], scratch[1]
+            [group], slots, start, count, count // 8, True, own_partial, own_sums
         )[0]
 
-    on_member(shares, run)
-
-
-def meet_rest(slots, shares, known, sent_ref, source_ref, *refs):
-    sources, targets, before = refs[:known], refs[known : 2 * known - 1], refs[2 * known - 1 : 3 * known - 2]
-    forces_ref, columns_ref, partial_ref, sums_ref = refs[3 * known - 2 :]
-    columns_ref[...] = jnp.transpose(sent_ref[0:8, 0:slots])
+    def late():
+        group = (target_ref, None, None, sources + (source_ref,), None)
+        late_ref[...] = run_pairs([group], slots, 0, slots, 4, True, partial_ref, sums_ref)[0]
+
+    member = lax.rem(lax.axis_index("act"), 2)
+
+    @pl.when(member == 0)
+    def _():
+        late_ref[...] = jnp.zeros_like(late_ref)
+        own(0, shares[0])
+
+    @pl.when(member == 1)
+    def _():
+        spread_targets(sent_ref[0:8, 0:slots], target_ref, 0, slots)
+        own(shares[0], shares[1])
+        late()
+
+
+def meet_rest(slots, shares, source_ref, late_ref, *refs):
+    known = (len(refs) - 3) // 2
+    targets, before = refs[:known], refs[known : 2 * known]
+    forces_ref, partial_ref, sums_ref = refs[2 * known :]
 
     def run(start, count):
         groups = [(t, None, b, (source_ref,), None) for t, b in zip(targets, before)]
-        groups.append((None, columns_ref, None, sources + (source_ref,), None))
-        forces = run_pairs(groups, slots, start, count, 2, True, partial_ref, sums_ref)
+        forces = run_pairs(groups, slots, start, count, 4, True, partial_ref, sums_ref)
         for d in range(known):
             forces_ref[:, d * slots : (d + 1) * slots] = forces[d]
 
     on_member(shares, run)
+    forces_ref[:, known * slots : (known + 1) * slots] = late_ref[...]
 
 
 def first_step(slots, sent, forces):
@@ -483,15 +498,10 @@
 
     limit = pltpu.CompilerParams(vmem_limit_bytes=16 * 2**20)
     owners = lax.axis_size("act")
-    shares = (slots,)
-    if owners % 2 == 0:
-        first_share = slots * 3 // 8 // 16 * 16
-        shares = (first_share, slots - first_share)
+    shares = (slots // 2, slots - slots // 2)
     parts = len(shares)
 
     def with_other(part):
-        if parts == 1:
-            return [part]
         return [part, lax.ppermute(part, "act", [(i, i ^ 1) for i in range(owners)])]
 
     def call(body, operands, out_shape, scratch=(), pairs=0):
@@ -526,19 +536,27 @@
         targets += outs[fresh : 2 * fresh]
         sums = list(outs[2 * fresh :])
         known = every
-    source, own = call(
+    source, own, late = call(
         functools.partial(meet_own, slots, shares),
-        [sent[known], targets[0], sums[0]],
-        (source_shape, own_shape),
-        [rows((max(shares) * 6, 128)), rows((slots + max(shares), 8))],
-    )
+        [sent[known], targets[0], sums[0], *sources],
+        (source_shape, own_shape, own_shape),
+        [
+            rows(target_shape.shape),
+            rows((max(shares) * 6, 128)),
+            rows((slots + max(shares), 8)),
+            rows((4 * 48, 128)),
+            rows((slots + 32, 8)),
+            rows((slots, 8)),
+        ],
+    )
+    others = known - 1
     own = with_other(own)
     forces = call(
-        functools.partial(meet_rest, slots, shares, known),
-        [sent[known], source, *sources, *targets[1:], *sums[1:]],
+        functools.partial(meet_rest, slots, shares),
+        [source, late, *targets[1:], *sums[1:]],
         jax.ShapeDtypeStruct((8, known * slots), jnp.float32),
-        [rows((slots, 8)), rows((2 * known * 48, 128)), rows((known * (slots + 16), 8))],
-        2 * known * max(shares) * size,
+        [rows((4 * others * 48, 128)), rows((others * (slots + 32), 8))],
+        others * max(shares) * size,
     )
     forces = with_other(forces)
     first = slots // 128
@@ -567,7 +585,7 @@
         P(("groups", "src", "act")),
     )
     out_specs = P(None, ("groups", "src"))
-    few = 3 <= mesh.shape["src"] <= MAX_DIRECT
+    few = 3 <= mesh.shape["src"] <= MAX_DIRECT and mesh.shape["act"] % 2 == 0
     return jax.shard_map(
         direct_per_device if few else gather_per_device,
         mesh=mesh,

time: 16.8 us -> 16.4 us (0.976)
  waiting for transfers between devices: 1.79 us -> 1.52 us
    ppermute x3, waiting for transfers between devices: 0.96 us -> 0.45 us  [direct_per_device(): sent.append(lax.ppermute(message, 'src', pairs))]
    ppermute x2, waiting for transfers between devices: 0.83 us -> 1.07 us  [with_other(): lax.ppermute(part, 'act', [(i, i ^ 1) for i in range(owners)])]
  transfers between devices with their start and end apart: 5 -> 5, of which waited for: 3 -> 3; matrix products, arithmetic and copies ran while one was open for 0% -> 0% of each run, Pallas kernels for 18% -> 22%
where the time goes in v11:
time: 16.4 us; the launch traced here: 16.2 us
  starting transfers between devices  7.6 us (46%)
  Pallas kernels  7.04 us (43%)
  waiting for transfers between devices  1.52 us (9%)
    ppermute x3, starting transfers between devices, direct_per_device(): sent.append(lax.ppermute(message, 'src', pairs))  7.04 us
    pallas_call x6, Pallas kernels, call(): pl.pallas_call(body, out_shape=out_shape, in_specs=[whole] * len(operands...  5.8 us
    pallas_call x1, Pallas kernels, direct_per_device(): pl.pallas_call(lambda *refs: prepare(slots, size * shards, *refs), out_sh...  1.24 us
    ppermute x2, waiting for transfers between devices, with_other(): lax.ppermute(part, 'act', [(i, i ^ 1) for i in range(owners)])  1.07 us
    ppermute x2, starting transfers between devices, with_other(): lax.ppermute(part, 'act', [(i, i ^ 1) for i in range(owners)])  0.55 us
    ppermute x3, waiting for transfers between devices, direct_per_device(): sent.append(lax.ppermute(message, 'src', pairs))  0.45 us
  transfers between devices with their start and end apart: 5, of which 3 were waited for; matrix products, arithmetic and copies ran while one was open for 0% of the time, Pallas kernels for 22%

profile of v11, /device:TPU:0, one launch (start us, length us, event | category | flops | bytes accessed | tf_op | source)
XLA Modules:
  0.0 16.2 jit_solution(7588298546363506740)
XLA Ops:
  0.0 1.2 %prepare.1 = (f32[16,512]{1,0:T(8,128)S(1)}, f32[8,512]{1,0:T(8,128)S(1)}) custom-call(f32[12,512]{1,0:T(8,128)} %refs_10_.1, f32[1,512]{1,0:T(1,128)} %bitcast.3, f32[1,512]{1,0:T(1,128)} %bitcast.4, s32[1,512]{1,0:T(1,128)} %bitcast.5), custom_call_target="tpu_custom_call" | custom-call | tf_op jit(solution)/shard_map/prepare/pallas_call | solution.py:471
  1.2 3.1 %collective-permute-start = (f32[16,512]{1,0:T(8,128)S(1)}, f32[16,512]{1,0:T(8,128)S(1)}, u32[]{:S(2)}, u32[]{:S(2)}) collective-permute-start(f32[16,512]{1,0:T(8,128)S(1)} %get-tuple-element.25.refs_0_), channel_id=1, source_target_pairs={{0,4},{4,8},{8,12},{12,0},{1,5},{5,9},{9,13},{13,1},{2,6},{6,10},{... | collective-permute-start | bytes 98312 | tf_op jit(solution)/shard_map/ppermute | solution.py:497
  4.4 2.6 %collective-permute-start.1 = (f32[16,512]{1,0:T(8,128)S(1)}, f32[16,512]{1,0:T(8,128)S(1)}, u32[]{:S(2)}, u32[]{:S(2)}) collective-permute-start(f32[16,512]{1,0:T(8,128)S(1)} %get-tuple-element.25.refs_0_), channel_id=1, source_target_pairs={{0,8},{4,12},{8,0},{12,4},{1,9},{5,13},{9,1},{13,5},{2,10},{6,14},... | collective-permute-start | bytes 98312 | tf_op jit(solution)/shard_map/ppermute | solution.py:497
  6.9 1.3 %collective-permute-start.2 = (f32[16,512]{1,0:T(8,128)S(1)}, f32[16,512]{1,0:T(8,128)S(1)}, u32[]{:S(2)}, u32[]{:S(2)}) collective-permute-start(f32[16,512]{1,0:T(8,128)S(1)} %get-tuple-element.25.refs_0_), channel_id=1, source_target_pairs={{0,12},{4,0},{8,4},{12,8},{1,13},{5,1},{9,5},{13,9},{2,14},{6,2},{... | collective-permute-start | bytes 98312 | tf_op jit(solution)/shard_map/ppermute | solution.py:497
  8.3 0.0 collective-permute-done.refs_1_
  8.3 1.0 %shard_map.46 = (f32[7,32,128]{2,1,0:T(8,128)S(1)}, f32[7,32,128]{2,1,0:T(8,128)S(1)}, f32[6,128,128]{2,1,0:T(8,128)S(1)}, f32[6,128,128]{2,1,0:T(8,128)S(1)}, f...) custom-call(f32[16,512]{1,0:T(8,128)S(1)} %get-tuple-element.25.refs_0_, f32[16,512]{1,0:T(8,128)S(1)} %collective-permute-done.refs_1_), custom_call_target="tpu_custom_call" | custom-call | tf_op jit(solution)/shard_map/pallas_call | solution.py:509
  9.3 0.2 %collective-permute-done.1.refs_0_.refs_2_ = f32[16,512]{1,0:T(8,128)S(1)} collective-permute-done((f32[16,512]{1,0:T(8,128)S(1)}, f32[16,512]{1,0:T(8,128)S(1)}, u32[]{:S(2)}, u32[]{:S(2)}) %collective-permute-start.1) | collective-permute-done | bytes 32800 | tf_op jit(solution)/shard_map/ppermute | solution.py:497
  9.5 1.1 %shard_map.47 = (f32[7,32,128]{2,1,0:T(8,128)S(1)}, f32[6,128,128]{2,1,0:T(8,128)S(1)}, f32[6,128,128]{2,1,0:T(8,128)S(1)}, f32[6,128,128]{2,1,0:T(8,128)S(1)}, f32[6,128,128]{2,1,0:T(8,128)S(1)}) custom-call(f32[16,512]{1,0:T(8,128)S(1)} %collective-permute-done.1.refs_0_.refs_2_, f32[7,32,128]{2,1,0:T(8,128)S(1)} %get-tuple-element.27.refs_1_.refs_0_, ...), custom_call_target="tpu_custom_call" | custom-call | tf_op jit(solution)/shard_map/pallas_call | solution.py:509
  10.6 0.3 %collective-permute-done.2.sent_ref.refs_3_ = f32[16,512]{1,0:T(8,128)S(1)} collective-permute-done((f32[16,512]{1,0:T(8,128)S(1)}, f32[16,512]{1,0:T(8,128)S(1)}, u32[]{:S(2)}, u32[]{:S(2)}) %collective-permute-start.2) | collective-permute-done | bytes 32800 | tf_op jit(solution)/shard_map/ppermute | solution.py:497
  10.9 0.3 %shard_map.48 = (f32[7,32,128]{2,1,0:T(8,128)S(1)}, f32[8,128]{1,0:T(8,128)S(1)}, f32[8,128]{1,0:T(8,128)S(1)}) custom-call(f32[16,512]{1,0:T(8,128)S(1)} %collective-permute-done.2.sent_ref.refs_3_, f32[6,128,128]{2,1,0:T(8,128)S(1)} %get-tuple-element.26.refs_3_.own_target, f32[6,128,128]{2,1,0:T(8,128)S(1)} %get-tuple-element.32.own_before, ...), custom_call_target="tpu_custom_call" | custom-call | tf_op jit(solution)/shard_map/pallas_call | solution.py:509
  11.2 0.6 %shard_map.49.refs_4_ = f32[8,384]{1,0:T(8,128)S(1)} custom-call(f32[7,32,128]{2,1,0:T(8,128)S(1)} %get-tuple-element.34.source_ref, f32[8,128]{1,0:T(8,128)S(1)} %get-tuple-element.35.late_ref, f32[6,128,128]{2,1,0:T(8,128)S(1)} %get-tuple-element.29.refs_4_.refs_0_, f32[6,128,128]{2,1,0:T(8,128)S(1)} %get-tuple-element.36.refs_1_, ...), custom_call_target="tpu_custom_call" | custom-call | flops 2686976 | tf_op jit(solution)/shard_map/pallas_call | solution.py:509
  11.8 0.5 %collective-permute-start.3 = (f32[8,384]{1,0:T(8,128)S(1)}, f32[8,384]{1,0:T(8,128)S(1)}, u32[]{:S(2)}, u32[]{:S(2)}) collective-permute-start(f32[8,384]{1,0:T(8,128)S(1)} %shard_map.49.refs_4_), channel_id=1, source_target_pairs={{0,1},{1,0},{2,3},{3,2},{4,5},{5,4},{6,7},{7,6},{8,9},{9,8},{10,11... | collective-permute-start | bytes 36872 | tf_op jit(solution)/shard_map/ppermute | solution.py:505
  12.2 0.0 copy-start
  12.2 0.1 collective-permute-start.4
  12.3 1.1 %collective-permute-done.4.refs_5_ = f32[8,128]{1,0:T(8,128)S(1)} collective-permute-done((f32[8,128]{1,0:T(8,128)S(1)}, f32[8,128]{1,0:T(8,128)S(1)}, u32[]{:S(2)}, u32[]{:S(2)}) %collective-permute-start.4) | collective-permute-done | bytes 4128 | tf_op jit(solution)/shard_map/ppermute | solution.py:505
  13.4 1.4 %shard_map.50 = (f32[8,128]{1,0:T(8,128)S(1)}, f32[8,128]{1,0:T(8,128)S(1)}, f32[6,128,128]{2,1,0:T(8,128)S(1)}, f32[6,128,128]{2,1,0:T(8,128)S(1)}) custom-call(f32[16,512]{1,0:T(8,128)S(1)} %get-tuple-element.25.refs_0_, f32[16,512]{1,0:T(8,128)S(1)} %collective-permute-done.refs_1_, f32[16,512]{1,0:T(8,128)S(1)} %collective-permute-done.1.refs_0_.refs_2_, ...), custom_call_target="tpu_custom_call" | custom-call | flops 8060928 | tf_op jit(solution)/shard_map/pallas_call | solution.py:509
  14.8 0.0 collective-permute-done.3.refs_5_
  14.8 0.0 copy-done
  14.8 1.4 %shard_map.51 = f32[12,512]{1,0:T(8,128)} custom-call(f32[16,512]{1,0:T(8,128)S(1)} %get-tuple-element.25.refs_0_, f32[16,512]{1,0:T(8,128)S(1)} %collective-permute-done.refs_1_, f32[16,512]{1,0:T(8,128)S(1)} %collective-permute-done.1.refs_0_.refs_2_, f32[16,512]{1,0:T(8,128)S(1)} %collective-permute-done.2.sent_ref.refs_3_, ...), custom_call_target="tpu_custom_call" | custom-call | tf_op jit(solution)/shard_map/pallas_call | solution.py:509
Async XLA Ops:
  1.2 7.0 %collective-permute-start = (f32[16,512]{1,0:T(8,128)S(1)}, f32[16,512]{1,0:T(8,128)S(1)}, u32[]{:S(2)}, u32[]{:S(2)}) collective-permute-start(f32[16,512]{1,0:T(8,128)S(1)} %get-tuple-element.25.refs_0_), channel_id=1, source_target_pairs={{0,4},{4,8},{8,12},{12,0},{1,5},{5,9},{9,13},{13,1},{2,6},{6,10},{... | collective-permute-start | bytes 98312 | tf_op jit(solution)/shard_map/ppermute | solution.py:497
  4.4 5.2 %collective-permute-start.1 = (f32[16,512]{1,0:T(8,128)S(1)}, f32[16,512]{1,0:T(8,128)S(1)}, u32[]{:S(2)}, u32[]{:S(2)}) collective-permute-start(f32[16,512]{1,0:T(8,128)S(1)} %get-tuple-element.25.refs_0_), channel_id=1, source_target_pairs={{0,8},{4,12},{8,0},{12,4},{1,9},{5,13},{9,1},{13,5},{2,10},{6,14},... | collective-permute-start | bytes 98312 | tf_op jit(solution)/shard_map/ppermute | solution.py:497
  6.9 3.9 %collective-permute-start.2 = (f32[16,512]{1,0:T(8,128)S(1)}, f32[16,512]{1,0:T(8,128)S(1)}, u32[]{:S(2)}, u32[]{:S(2)}) collective-permute-start(f32[16,512]{1,0:T(8,128)S(1)} %get-tuple-element.25.refs_0_), channel_id=1, source_target_pairs={{0,12},{4,0},{8,4},{12,8},{1,13},{5,1},{9,5},{13,9},{2,14},{6,2},{... | collective-permute-start | bytes 98312 | tf_op jit(solution)/shard_map/ppermute | solution.py:497
  11.8 3.0 %collective-permute-start.3 = (f32[8,384]{1,0:T(8,128)S(1)}, f32[8,384]{1,0:T(8,128)S(1)}, u32[]{:S(2)}, u32[]{:S(2)}) collective-permute-start(f32[8,384]{1,0:T(8,128)S(1)} %shard_map.49.refs_4_), channel_id=1, source_target_pairs={{0,1},{1,0},{2,3},{3,2},{4,5},{5,4},{6,7},{7,6},{8,9},{9,8},{10,11... | collective-permute-start | bytes 36872 | tf_op jit(solution)/shard_map/ppermute | solution.py:505
  12.2 2.6 %copy-start = (f32[12,512]{1,0:T(8,128)S(1)}, f32[12,512]{1,0:T(8,128)}, u32[]{:S(2)}) copy-start(f32[12,512]{1,0:T(8,128)} %refs_10_.1) | copy-start | bytes 73732
  12.2 1.2 %collective-permute-start.4 = (f32[8,128]{1,0:T(8,128)S(1)}, f32[8,128]{1,0:T(8,128)S(1)}, u32[]{:S(2)}, u32[]{:S(2)}) collective-permute-start(f32[8,128]{1,0:T(8,128)S(1)} %get-tuple-element.39.refs_4_), channel_id=1, source_target_pairs={{0,1},{1,0},{2,3},{3,2},{4,5},{5,4},{6,7},{7,6},{8,9},{9,8},{10,11... | collective-permute-start | bytes 12296 | tf_op jit(solution)/shard_map/ppermute | solution.py:505

commit v12 on v11

--- a/solution.py
+++ b/solution.py
@@ -340,10 +340,10 @@
     on_member(shares, run)
 
 
-def meet_own(slots, shares, sent_ref, own_target, own_before, *refs):
-    known = len(refs) - 9
+def meet_own(slots, shares, early, sent_ref, own_target, own_before, *refs):
+    known = len(refs) - 8
     sources = refs[:known]
-    source_ref, own_ref, late_ref, target_ref, own_partial, own_sums, partial_ref, sums_ref, _ = refs[known:]
+    source_ref, own_ref, late_ref, target_ref, own_partial, own_sums, partial_ref, sums_ref = refs[known:]
     spread_sources(sent_ref[0:8, :], source_ref, 0)
 
     def own(start, count):
@@ -352,37 +352,58 @@
             [group], slots, start, count, count // 8, True, own_partial, own_sums
         )[0]
 
-    def late():
-        group = (target_ref, None, None, sources + (source_ref,), None)
-        late_ref[...] = run_pairs([group], slots, 0, slots, 4, True, partial_ref, sums_ref)[0]
-
     member = lax.rem(lax.axis_index("act"), 2)
 
     @pl.when(member == 0)
     def _():
         late_ref[...] = jnp.zeros_like(late_ref)
+        spread_targets(sent_ref[0:8, 0:slots], target_ref, early, slots - early)
         own(0, shares[0])
 
     @pl.when(member == 1)
     def _():
         spread_targets(sent_ref[0:8, 0:slots], target_ref, 0, slots)
         own(shares[0], shares[1])
-        late()
-
-
-def meet_rest(slots, shares, source_ref, late_ref, *refs):
-    known = (len(refs) - 3) // 2
-    targets, before = refs[:known], refs[known : 2 * known]
-    forces_ref, partial_ref, sums_ref = refs[2 * known :]
+        group = (target_ref, None, None, sources + (source_ref,), None)
+        late_ref[...] = run_pairs([group], slots, 0, early, 4, True, partial_ref, sums_ref)[0]
+
+
+def meet_rest(slots, shares, early, source_ref, late_ref, late_target, *refs):
+    known = (len(refs) - 4) // 3
+    sources, targets, before = refs[: known + 1], refs[known + 1 : 2 * known + 1], refs[2 * known + 1 : 3 * known + 1]
+    forces_ref, partial_ref, sums_ref = refs[3 * known + 1 :]
+    half = (slots - early) // 2
+    used = half * 6
 
     def run(start, count):
+        group = (late_target, None, None, sources + (source_ref,), None)
+        first = early if start == 0 else early + half
+        late = run_pairs(
+            [group],
+            slots,
+            first,
+            half,
+            half // 8,
+            True,
+            partial_ref.at[0:used],
+            sums_ref.at[0 : slots + half],
+        )[0]
+        forces_ref[:, known * slots : (known + 1) * slots] = late_ref[...] + late
         groups = [(t, None, b, (source_ref,), None) for t, b in zip(targets, before)]
-        forces = run_pairs(groups, slots, start, count, 4, True, partial_ref, sums_ref)
+        forces = run_pairs(
+            groups,
+            slots,
+            start,
+            count,
+            count // 8,
+            True,
+            partial_ref.at[used : used + count * known * 6],
+            sums_ref.at[slots + half : slots + half + known * (slots + count)],
+        )
         for d in range(known):
             forces_ref[:, d * slots : (d + 1) * slots] = forces[d]
 
     on_member(shares, run)
-    forces_ref[:, known * slots : (known + 1) * slots] = late_ref[...]
 
 
 def first_step(slots, sent, forces):
@@ -536,26 +557,29 @@
         targets += outs[fresh : 2 * fresh]
         sums = list(outs[2 * fresh :])
         known = every
-    source, own, late = call(
-        functools.partial(meet_own, slots, shares),
+    early = slots * 3 // 4
+    source, own, late, late_target = call(
+        functools.partial(meet_own, slots, shares, early),
         [sent[known], targets[0], sums[0], *sources],
-        (source_shape, own_shape, own_shape),
+        (source_shape, own_shape, own_shape, target_shape),
         [
-            rows(target_shape.shape),
             rows((max(shares) * 6, 128)),
             rows((slots + max(shares), 8)),
             rows((4 * 48, 128)),
             rows((slots + 32, 8)),
-            rows((slots, 8)),
         ],
     )
     others = known - 1
+    half = (slots - early) // 2
     own = with_other(own)
     forces = call(
-        functools.partial(meet_rest, slots, shares),
-        [source, late, *targets[1:], *sums[1:]],
+        functools.partial(meet_rest, slots, shares, early),
+        [source, late, late_target, *sources, *targets[1:], *sums[1:]],
         jax.ShapeDtypeStruct((8, known * slots), jnp.float32),
-        [rows((4 * others * 48, 128)), rows((others * (slots + 32), 8))],
+        [
+            rows((half * 6 + max(shares) * others * 6, 128)),
+            rows((slots + half + others * (slots + max(shares)), 8)),
+        ],
         others * max(shares) * size,
     )
     forces = with_other(forces)

time: 16.4 us -> 16.4 us (level)
  Pallas kernels: 7.04 us -> 7.29 us
  waiting for transfers between devices: 1.52 us -> 1.28 us
    pallas_call x6, Pallas kernels: 5.8 us -> 6.05 us  [call(): pl.pallas_call(body, out_shape=out_shape, in_specs=[whole] * len(operands...]
    ppermute x2, waiting for transfers between devices: 1.07 us -> 0.83 us  [with_other(): lax.ppermute(part, 'act', [(i, i ^ 1) for i in range(owners)])]
where the time goes in v12:
time: 16.4 us; the launch traced here: 16.2 us
  starting transfers between devices  7.58 us (46%)
  Pallas kernels  7.29 us (44%)
  waiting for transfers between devices  1.28 us (8%)
    ppermute x3, starting transfers between devices, direct_per_device(): sent.append(lax.ppermute(message, 'src', pairs))  7.04 us
    pallas_call x6, Pallas kernels, call(): pl.pallas_call(body, out_shape=out_shape, in_specs=[whole] * len(operands...  6.05 us
    pallas_call x1, Pallas kernels, direct_per_device(): pl.pallas_call(lambda *refs: prepare(slots, size * shards, *refs), out_sh...  1.24 us
    ppermute x2, waiting for transfers between devices, with_other(): lax.ppermute(part, 'act', [(i, i ^ 1) for i in range(owners)])  0.83 us
    ppermute x2, starting transfers between devices, with_other(): lax.ppermute(part, 'act', [(i, i ^ 1) for i in range(owners)])  0.54 us
    ppermute x3, waiting for transfers between devices, direct_per_device(): sent.append(lax.ppermute(message, 'src', pairs))  0.45 us
  transfers between devices with their start and end apart: 5, of which 3 were waited for; matrix products, arithmetic and copies ran while one was open for 0% of the time, Pallas kernels for 22%

profile of v12, /device:TPU:0, one launch (start us, length us, event | category | flops | bytes accessed | tf_op | source)
XLA Modules:
  0.0 16.2 jit_solution(7104473060999031731)
XLA Ops:
  0.0 1.2 %prepare.1 = (f32[16,512]{1,0:T(8,128)S(1)}, f32[8,512]{1,0:T(8,128)S(1)}) custom-call(f32[12,512]{1,0:T(8,128)} %refs_10_.1, f32[1,512]{1,0:T(1,128)} %bitcast.3, f32[1,512]{1,0:T(1,128)} %bitcast.4, s32[1,512]{1,0:T(1,128)} %bitcast.5), custom_call_target="tpu_custom_call" | custom-call | tf_op jit(solution)/shard_map/prepare/pallas_call | solution.py:492
  1.2 3.1 %collective-permute-start = (f32[16,512]{1,0:T(8,128)S(1)}, f32[16,512]{1,0:T(8,128)S(1)}, u32[]{:S(2)}, u32[]{:S(2)}) collective-permute-start(f32[16,512]{1,0:T(8,128)S(1)} %get-tuple-element.26.refs_0_), channel_id=1, source_target_pairs={{0,4},{4,8},{8,12},{12,0},{1,5},{5,9},{9,13},{13,1},{2,6},{6,10},{... | collective-permute-start | bytes 98312 | tf_op jit(solution)/shard_map/ppermute | solution.py:518
  4.4 2.6 %collective-permute-start.1 = (f32[16,512]{1,0:T(8,128)S(1)}, f32[16,512]{1,0:T(8,128)S(1)}, u32[]{:S(2)}, u32[]{:S(2)}) collective-permute-start(f32[16,512]{1,0:T(8,128)S(1)} %get-tuple-element.26.refs_0_), channel_id=1, source_target_pairs={{0,8},{4,12},{8,0},{12,4},{1,9},{5,13},{9,1},{13,5},{2,10},{6,14},... | collective-permute-start | bytes 98312 | tf_op jit(solution)/shard_map/ppermute | solution.py:518
  6.9 1.3 %collective-permute-start.2 = (f32[16,512]{1,0:T(8,128)S(1)}, f32[16,512]{1,0:T(8,128)S(1)}, u32[]{:S(2)}, u32[]{:S(2)}) collective-permute-start(f32[16,512]{1,0:T(8,128)S(1)} %get-tuple-element.26.refs_0_), channel_id=1, source_target_pairs={{0,12},{4,0},{8,4},{12,8},{1,13},{5,1},{9,5},{13,9},{2,14},{6,2},{... | collective-permute-start | bytes 98312 | tf_op jit(solution)/shard_map/ppermute | solution.py:518
  8.3 0.0 collective-permute-done.refs_1_
  8.3 1.0 %shard_map.46 = (f32[7,32,128]{2,1,0:T(8,128)S(1)}, f32[7,32,128]{2,1,0:T(8,128)S(1)}, f32[6,128,128]{2,1,0:T(8,128)S(1)}, f32[6,128,128]{2,1,0:T(8,128)S(1)}, f...) custom-call(f32[16,512]{1,0:T(8,128)S(1)} %get-tuple-element.26.refs_0_, f32[16,512]{1,0:T(8,128)S(1)} %collective-permute-done.refs_1_), custom_call_target="tpu_custom_call" | custom-call | tf_op jit(solution)/shard_map/pallas_call | solution.py:530
  9.3 0.2 %collective-permute-done.1.refs_0_.refs_2_ = f32[16,512]{1,0:T(8,128)S(1)} collective-permute-done((f32[16,512]{1,0:T(8,128)S(1)}, f32[16,512]{1,0:T(8,128)S(1)}, u32[]{:S(2)}, u32[]{:S(2)}) %collective-permute-start.1) | collective-permute-done | bytes 32800 | tf_op jit(solution)/shard_map/ppermute | solution.py:518
  9.5 1.1 %shard_map.47 = (f32[7,32,128]{2,1,0:T(8,128)S(1)}, f32[6,128,128]{2,1,0:T(8,128)S(1)}, f32[6,128,128]{2,1,0:T(8,128)S(1)}, f32[6,128,128]{2,1,0:T(8,128)S(1)}, f32[6,128,128]{2,1,0:T(8,128)S(1)}) custom-call(f32[16,512]{1,0:T(8,128)S(1)} %collective-permute-done.1.refs_0_.refs_2_, f32[7,32,128]{2,1,0:T(8,128)S(1)} %get-tuple-element.28.refs_1_.refs_0_, ...), custom_call_target="tpu_custom_call" | custom-call | tf_op jit(solution)/shard_map/pallas_call | solution.py:530
  10.6 0.3 %collective-permute-done.2.sent_ref.refs_3_ = f32[16,512]{1,0:T(8,128)S(1)} collective-permute-done((f32[16,512]{1,0:T(8,128)S(1)}, f32[16,512]{1,0:T(8,128)S(1)}, u32[]{:S(2)}, u32[]{:S(2)}) %collective-permute-start.2) | collective-permute-done | bytes 32800 | tf_op jit(solution)/shard_map/ppermute | solution.py:518
  10.9 0.4 %shard_map.48 = (f32[7,32,128]{2,1,0:T(8,128)S(1)}, f32[8,128]{1,0:T(8,128)S(1)}, f32[8,128]{1,0:T(8,128)S(1)}, f32[6,128,128]{2,1,0:T(8,128)S(1)}) custom-call(f32[16,512]{1,0:T(8,128)S(1)} %collective-permute-done.2.sent_ref.refs_3_, f32[6,128,128]{2,1,0:T(8,128)S(1)} %get-tuple-element.27.refs_3_.own_target, ...), custom_call_target="tpu_custom_call" | custom-call | tf_op jit(solution)/shard_map/pallas_call | solution.py:530
  11.3 0.8 %shard_map.49.refs_4_ = f32[8,384]{1,0:T(8,128)S(1)} custom-call(f32[7,32,128]{2,1,0:T(8,128)S(1)} %get-tuple-element.35.source_ref, f32[8,128]{1,0:T(8,128)S(1)} %get-tuple-element.36.late_ref, f32[6,128,128]{2,1,0:T(8,128)S(1)} %get-tuple-element.37.late_target, f32[7,32,128]{2,1,0:T(8,128)S(1)} %get-tuple-element.28.refs_1_.refs_0_, ...), custom_call_target="tpu_custom_call" | custom-call | flops 2686976 | tf_op jit(solution)/shard_map/pallas_call | solution.py:530
  12.0 0.1 collective-permute-start.3
  12.1 0.0 copy-start
  12.1 0.5 %collective-permute-start.4 = (f32[8,128]{1,0:T(8,128)S(1)}, f32[8,128]{1,0:T(8,128)S(1)}, u32[]{:S(2)}, u32[]{:S(2)}) collective-permute-start(f32[8,128]{1,0:T(8,128)S(1)} %get-tuple-element.41.refs_4_), channel_id=1, source_target_pairs={{0,1},{1,0},{2,3},{3,2},{4,5},{5,4},{6,7},{7,6},{8,9},{9,8},{10,11... | collective-permute-start | bytes 12296 | tf_op jit(solution)/shard_map/ppermute | solution.py:526
  12.6 0.8 %collective-permute-done.4.refs_5_ = f32[8,128]{1,0:T(8,128)S(1)} collective-permute-done((f32[8,128]{1,0:T(8,128)S(1)}, f32[8,128]{1,0:T(8,128)S(1)}, u32[]{:S(2)}, u32[]{:S(2)}) %collective-permute-start.4) | collective-permute-done | bytes 4128 | tf_op jit(solution)/shard_map/ppermute | solution.py:526
  13.4 1.4 %shard_map.50 = (f32[8,128]{1,0:T(8,128)S(1)}, f32[8,128]{1,0:T(8,128)S(1)}, f32[6,128,128]{2,1,0:T(8,128)S(1)}, f32[6,128,128]{2,1,0:T(8,128)S(1)}) custom-call(f32[16,512]{1,0:T(8,128)S(1)} %get-tuple-element.26.refs_0_, f32[16,512]{1,0:T(8,128)S(1)} %collective-permute-done.refs_1_, f32[16,512]{1,0:T(8,128)S(1)} %collective-permute-done.1.refs_0_.refs_2_, ...), custom_call_target="tpu_custom_call" | custom-call | flops 8060928 | tf_op jit(solution)/shard_map/pallas_call | solution.py:530
  14.8 0.0 collective-permute-done.3.refs_5_
  14.8 0.0 copy-done
  14.8 1.4 %shard_map.51 = f32[12,512]{1,0:T(8,128)} custom-call(f32[16,512]{1,0:T(8,128)S(1)} %get-tuple-element.26.refs_0_, f32[16,512]{1,0:T(8,128)S(1)} %collective-permute-done.refs_1_, f32[16,512]{1,0:T(8,128)S(1)} %collective-permute-done.1.refs_0_.refs_2_, f32[16,512]{1,0:T(8,128)S(1)} %collective-permute-done.2.sent_ref.refs_3_, ...), custom_call_target="tpu_custom_call" | custom-call | tf_op jit(solution)/shard_map/pallas_call | solution.py:530
Async XLA Ops:
  1.2 7.0 %collective-permute-start = (f32[16,512]{1,0:T(8,128)S(1)}, f32[16,512]{1,0:T(8,128)S(1)}, u32[]{:S(2)}, u32[]{:S(2)}) collective-permute-start(f32[16,512]{1,0:T(8,128)S(1)} %get-tuple-element.26.refs_0_), channel_id=1, source_target_pairs={{0,4},{4,8},{8,12},{12,0},{1,5},{5,9},{9,13},{13,1},{2,6},{6,10},{... | collective-permute-start | bytes 98312 | tf_op jit(solution)/shard_map/ppermute | solution.py:518
  4.4 5.2 %collective-permute-start.1 = (f32[16,512]{1,0:T(8,128)S(1)}, f32[16,512]{1,0:T(8,128)S(1)}, u32[]{:S(2)}, u32[]{:S(2)}) collective-permute-start(f32[16,512]{1,0:T(8,128)S(1)} %get-tuple-element.26.refs_0_), channel_id=1, source_target_pairs={{0,8},{4,12},{8,0},{12,4},{1,9},{5,13},{9,1},{13,5},{2,10},{6,14},... | collective-permute-start | bytes 98312 | tf_op jit(solution)/shard_map/ppermute | solution.py:518
  6.9 3.9 %collective-permute-start.2 = (f32[16,512]{1,0:T(8,128)S(1)}, f32[16,512]{1,0:T(8,128)S(1)}, u32[]{:S(2)}, u32[]{:S(2)}) collective-permute-start(f32[16,512]{1,0:T(8,128)S(1)} %get-tuple-element.26.refs_0_), channel_id=1, source_target_pairs={{0,12},{4,0},{8,4},{12,8},{1,13},{5,1},{9,5},{13,9},{2,14},{6,2},{... | collective-permute-start | bytes 98312 | tf_op jit(solution)/shard_map/ppermute | solution.py:518
  12.0 2.8 %collective-permute-start.3 = (f32[8,384]{1,0:T(8,128)S(1)}, f32[8,384]{1,0:T(8,128)S(1)}, u32[]{:S(2)}, u32[]{:S(2)}) collective-permute-start(f32[8,384]{1,0:T(8,128)S(1)} %shard_map.49.refs_4_), channel_id=1, source_target_pairs={{0,1},{1,0},{2,3},{3,2},{4,5},{5,4},{6,7},{7,6},{8,9},{9,8},{10,11... | collective-permute-start | bytes 36872 | tf_op jit(solution)/shard_map/ppermute | solution.py:526
  12.1 2.7 %copy-start = (f32[12,512]{1,0:T(8,128)S(1)}, f32[12,512]{1,0:T(8,128)}, u32[]{:S(2)}) copy-start(f32[12,512]{1,0:T(8,128)} %refs_10_.1) | copy-start | bytes 73732
  12.1 1.3 %collective-permute-start.4 = (f32[8,128]{1,0:T(8,128)S(1)}, f32[8,128]{1,0:T(8,128)S(1)}, u32[]{:S(2)}, u32[]{:S(2)}) collective-permute-start(f32[8,128]{1,0:T(8,128)S(1)} %get-tuple-element.41.refs_4_), channel_id=1, source_target_pairs={{0,1},{1,0},{2,3},{3,2},{4,5},{5,4},{6,7},{7,6},{8,9},{9,8},{10,11... | collective-permute-start | bytes 12296 | tf_op jit(solution)/shard_map/ppermute | solution.py:526

commit v13 on v9

--- a/solution.py
+++ b/solution.py
@@ -303,7 +303,7 @@
     ]
 
 
-def meet(slots, shares, known, fresh, last, *refs):
+def meet(slots, shares, late_shares, known, fresh, last, *refs):
     every = known + fresh
     sent, refs = refs[:fresh], refs[fresh:]
     old_sources, old_targets, before = refs[:known], refs[known : 2 * known], refs[2 * known : 3 * known]
@@ -311,10 +311,9 @@
     own_ref = forces_ref = own_partial = own_sums = partial_ref = sums_ref = None
     if last:
         own_ref, forces_ref, refs = refs[0], refs[1], refs[2:]
-        new_sources, refs = refs[:fresh], refs[fresh:]
-        new_targets = (None,) * fresh
+        new_sources, new_targets, refs = refs[:fresh], refs[fresh : 2 * fresh], refs[2 * fresh :]
         after = (None,) * every
-        columns_ref, own_partial, own_sums, partial_ref, sums_ref = refs
+        columns_ref, own_partial, own_sums, partial_ref, sums_ref, late_partial, late_sums = refs
     else:
         new_sources, new_targets, after = refs[:fresh], refs[fresh : 2 * fresh], refs[2 * fresh : 2 * fresh + every]
         columns_ref = refs[2 * fresh + every]
@@ -322,7 +321,7 @@
 
     for d in range(fresh):
         spread_sources(sent[d][0:8, :], new_sources[d], 0)
-        if known + d > 0:
+        if known + d > 0 and not last:
             columns_ref[...] = jnp.transpose(sent[d][0:8, 0:slots])
     if known == 0:
         spread_targets(sent[0][0:8, 0:slots], new_targets[0], 0, slots)
@@ -333,27 +332,34 @@
     if last:
         own_ref[...] = own[0]
 
-    def run(start, count):
+    def run(member):
+        start, count = sum(shares[:member]), shares[member]
         groups = []
         for d in range(1, known):
             groups.append((old_targets[d], None, before[d], new_sources, after[d]))
-        for d in range(max(known, 1), every):
-            groups.append((new_targets[d - known], columns_ref, None, sources, after[d]))
-        together = 4 if known == 0 else 2
-        forces = run_pairs(groups, slots, start, count, together, last, partial_ref, sums_ref)
-        if last:
-            for d in range(1, every):
-                forces_ref[:, (d - 1) * slots : d * slots] = forces[d - 1]
-
-    if len(shares) == 1:
-        run(0, slots)
-        return
-    member = lax.rem(lax.axis_index("act"), len(shares))
-    for m in range(len(shares)):
+        if not last:
+            for d in range(max(known, 1), every):
+                groups.append((new_targets[d - known], columns_ref, None, sources, after[d]))
+            together = 4 if known == 0 else 2
+            run_pairs(groups, slots, start, count, together, False, None, None)
+            return
+        late_start, late_count = sum(late_shares[:member]), late_shares[member]
+        spread_targets(sent[0][0:8, 0:slots], new_targets[0], late_start, late_count)
+        forces = run_pairs(groups, slots, start, count, 4, True, partial_ref, sums_ref)
+        late = (new_targets[0], None, None, sources, None)
+        together = min(4, late_count // 8)
+        forces += run_pairs(
+            [late], slots, late_start, late_count, together, True, late_partial, late_sums
+        )
+        for d in range(1, every):
+            forces_ref[:, (d - 1) * slots : d * slots] = forces[d - 1]
+
+    member = lax.rem(lax.axis_index("act"), 2)
+    for m in range(2):
 
         @pl.when(member == m)
         def _():
-            run(sum(shares[:m]), shares[m])
+            run(m)
 
 
 def first_step(slots, sent, forces):
@@ -467,10 +473,8 @@
 
     limit = pltpu.CompilerParams(vmem_limit_bytes=16 * 2**20)
     owners = lax.axis_size("act")
-    shares = (slots,)
-    if owners % 2 == 0:
-        first_share = slots * 3 // 8 // 16 * 16
-        shares = (first_share, slots - first_share)
+    shares = (slots // 2, slots - slots // 2)
+    late_shares = (slots // 8, slots - slots // 8)
     source_shape = jax.ShapeDtypeStruct((7, size // 16, 128), jnp.float32)
     target_shape = jax.ShapeDtypeStruct((6, slots, 128), jnp.float32)
     own_shape = jax.ShapeDtypeStruct((8, slots), jnp.float32)
@@ -484,17 +488,20 @@
             out_shape = (own_shape, jax.ShapeDtypeStruct((8, (shards - 1) * slots), jnp.float32))
             scratch = [
                 pltpu.VMEM(source_shape.shape, jnp.float32),
+                pltpu.VMEM(target_shape.shape, jnp.float32),
                 columns,
                 pltpu.VMEM((8 * 48, 128), jnp.float32),
                 pltpu.VMEM((slots + 64, 8), jnp.float32),
-                pltpu.VMEM((2 * (shards - 1) * 48, 128), jnp.float32),
-                pltpu.VMEM(((shards - 1) * (slots + 16), 8), jnp.float32),
+                pltpu.VMEM((4 * (known - 1) * 48, 128), jnp.float32),
+                pltpu.VMEM(((known - 1) * (slots + 32), 8), jnp.float32),
+                pltpu.VMEM((4 * 48, 128), jnp.float32),
+                pltpu.VMEM((slots + 32, 8), jnp.float32),
             ]
         else:
             out_shape = [source_shape] * fresh + [target_shape] * (fresh + every)
             scratch = [columns]
         outs = pl.pallas_call(
-            functools.partial(meet, slots, shares, known, fresh, last),
+            functools.partial(meet, slots, shares, late_shares, known, fresh, last),
             out_shape=out_shape,
             in_specs=[whole] * (fresh + 3 * known),
             out_specs=(whole, whole) if last else [whole] * (2 * fresh + every),
@@ -547,7 +554,7 @@
         P(("groups", "src", "act")),
     )
     out_specs = P(None, ("groups", "src"))
-    few = 3 <= mesh.shape["src"] <= MAX_DIRECT
+    few = 3 <= mesh.shape["src"] <= MAX_DIRECT and mesh.shape["act"] % 2 == 0
     return jax.shard_map(
         direct_per_device if few else gather_per_device,
         mesh=mesh,

time: 16.1 us -> 16.1 us (level)
  transfers between devices with their start and end apart: 4 -> 4, of which waited for: 0 -> 0; matrix products, arithmetic and copies ran while one was open for 0% -> 0% of each run, Pallas kernels for 25% -> 27%
where the time goes in v13:
time: 16.1 us; the launch traced here: 15.9 us
  Pallas kernels  8.47 us (53%)
  starting transfers between devices  7.37 us (46%)
    ppermute x3, starting transfers between devices, direct_per_device(): sent.append(lax.ppermute(message, 'src', pairs))  7.04 us
    pallas_call x3, Pallas kernels, direct_per_device(): pl.pallas_call(functools.partial(meet, slots, shares, late_shares, known,...  4.45 us
    pallas_call x1, Pallas kernels, direct_per_device(): pl.pallas_call(functools.partial(meet_still, slots, shards), out_shape=(o...  1.39 us
    pallas_call x1, Pallas kernels, direct_per_device(): pl.pallas_call(functools.partial(finish, slots, shards, len(parts)), out_...  1.38 us
    pallas_call x1, Pallas kernels, direct_per_device(): pl.pallas_call(lambda *refs: prepare(slots, size * shards, *refs), out_sh...  1.24 us
    ppermute x1, starting transfers between devices, direct_per_device(): parts.append(lax.ppermute(part, 'act', [(i, i ^ 1) for i in range(owners)]))  0.33 us
  transfers between devices with their start and end apart: 4, of which 0 were waited for; matrix products, arithmetic and copies ran while one was open for 0% of the time, Pallas kernels for 27%

profile of v13, /device:TPU:0, one launch (start us, length us, event | category | flops | bytes accessed | tf_op | source)
XLA Modules:
  0.0 15.9 jit_solution(5856843479347544432)
XLA Ops:
  0.0 1.2 %prepare.1 = (f32[16,512]{1,0:T(8,128)S(1)}, f32[8,512]{1,0:T(8,128)S(1)}) custom-call(f32[12,512]{1,0:T(8,128)} %refs_10_.1, f32[1,512]{1,0:T(1,128)} %bitcast.3, f32[1,512]{1,0:T(1,128)} %bitcast.4, s32[1,512]{1,0:T(1,128)} %bitcast.5), custom_call_target="tpu_custom_call" | custom-call | tf_op jit(solution)/shard_map/prepare/pallas_call | solution.py:446
  1.2 3.1 %collective-permute-start = (f32[16,512]{1,0:T(8,128)S(1)}, f32[16,512]{1,0:T(8,128)S(1)}, u32[]{:S(2)}, u32[]{:S(2)}) collective-permute-start(f32[16,512]{1,0:T(8,128)S(1)} %get-tuple-element.23.refs_0_), channel_id=1, source_target_pairs={{0,4},{4,8},{8,12},{12,0},{1,5},{5,9},{9,13},{13,1},{2,6},{6,10},{... | collective-permute-start | bytes 98312 | tf_op jit(solution)/shard_map/ppermute | solution.py:472
  4.4 2.6 %collective-permute-start.1 = (f32[16,512]{1,0:T(8,128)S(1)}, f32[16,512]{1,0:T(8,128)S(1)}, u32[]{:S(2)}, u32[]{:S(2)}) collective-permute-start(f32[16,512]{1,0:T(8,128)S(1)} %get-tuple-element.23.refs_0_), channel_id=1, source_target_pairs={{0,8},{4,12},{8,0},{12,4},{1,9},{5,13},{9,1},{13,5},{2,10},{6,14},... | collective-permute-start | bytes 98312 | tf_op jit(solution)/shard_map/ppermute | solution.py:472
  6.9 1.3 %collective-permute-start.2 = (f32[16,512]{1,0:T(8,128)S(1)}, f32[16,512]{1,0:T(8,128)S(1)}, u32[]{:S(2)}, u32[]{:S(2)}) collective-permute-start(f32[16,512]{1,0:T(8,128)S(1)} %get-tuple-element.23.refs_0_), channel_id=1, source_target_pairs={{0,12},{4,0},{8,4},{12,8},{1,13},{5,1},{9,5},{13,9},{2,14},{6,2},{... | collective-permute-start | bytes 98312 | tf_op jit(solution)/shard_map/ppermute | solution.py:472
  8.3 0.0 collective-permute-done.refs_1_
  8.3 1.6 %meet_2.1 = (f32[7,32,128]{2,1,0:T(8,128)S(1)}, f32[7,32,128]{2,1,0:T(8,128)S(1)}, f32[6,128,128]{2,1,0:T(8,128)S(1)}, f32[6,128,128]{2,1,0:T(8,128)S(1)}, f32[6...) custom-call(f32[16,512]{1,0:T(8,128)S(1)} %get-tuple-element.23.refs_0_, f32[16,512]{1,0:T(8,128)S(1)} %collective-permute-done.refs_1_), custom_call_target="tpu_custom_call" | custom-call | tf_op jit(solution)/shard_map/meet_2/pallas_call | solution.py:503
  9.9 0.0 collective-permute-done.1.refs_0_.refs_2_
  9.9 1.4 %meet_3.1 = (f32[7,32,128]{2,1,0:T(8,128)S(1)}, f32[6,128,128]{2,1,0:T(8,128)S(1)}, f32[6,128,128]{2,1,0:T(8,128)S(1)}, f32[6,128,128]{2,1,0:T(8,128)S(1)}, f32[6,128,128]{2,1,0:T(8,128)S(1)}) custom-call(f32[16,512]{1,0:T(8,128)S(1)} %collective-permute-done.1.refs_0_.refs_2_, f32[7,32,128]{2,1,0:T(8,128)S(1)} %get-tuple-element.24.refs_1_, ...), custom_call_target="tpu_custom_call" | custom-call | tf_op jit(solution)/shard_map/meet_3/pallas_call | solution.py:503
  11.3 0.0 collective-permute-done.2.refs_0_.refs_3_
  11.3 1.5 %meet_4.1 = (f32[8,128]{1,0:T(8,128)S(1)}, f32[8,384]{1,0:T(8,128)S(1)}) custom-call(f32[16,512]{1,0:T(8,128)S(1)} %collective-permute-done.2.refs_0_.refs_3_, f32[7,32,128]{2,1,0:T(8,128)S(1)} %get-tuple-element.24.refs_1_, f32[7,32,128]{2,1,0:T(8,128)S(1)} %get-tuple-element.25.refs_2_, f32[7,32,128]{2,1,0:T(8,128)S(1)} %get-tuple-element.30.refs_3_, ...), custom_call_target="tpu_custom_call" | custom-call | tf_op jit(solution)/shard_map/meet_4/pallas_call | solution.py:503
  12.8 0.3 %collective-permute-start.3 = (f32[8,384]{1,0:T(8,128)S(1)}, f32[8,384]{1,0:T(8,128)S(1)}, u32[]{:S(2)}, u32[]{:S(2)}) collective-permute-start(f32[8,384]{1,0:T(8,128)S(1)} %get-tuple-element.35.refs_4_), channel_id=1, source_target_pairs={{0,1},{1,0},{2,3},{3,2},{4,5},{5,4},{6,7},{7,6},{8,9},{9,8},{10,11... | collective-permute-start | bytes 36872 | tf_op jit(solution)/shard_map/ppermute | solution.py:521
  13.1 0.0 copy-start
  13.1 1.4 %meet_still.1 = (f32[8,128]{1,0:T(8,128)S(1)}, f32[6,128,128]{2,1,0:T(8,128)S(1)}, f32[6,128,128]{2,1,0:T(8,128)S(1)}) custom-call(f32[16,512]{1,0:T(8,128)S(1)} %get-tuple-element.23.refs_0_, f32[16,512]{1,0:T(8,128)S(1)} %collective-permute-done.refs_1_, f32[16,512]{1,0:T(8,128)S(1)} %collective-permute-done.1.refs_0_.refs_2_, ...), custom_call_target="tpu_custom_call" | custom-call | tf_op jit(solution)/shard_map/meet_still/pallas_call | solution.py:523
  14.5 0.0 collective-permute-done.3.refs_5_
  14.5 0.0 copy-done
  14.5 1.4 %finish.1 = f32[12,512]{1,0:T(8,128)} custom-call(f32[16,512]{1,0:T(8,128)S(1)} %get-tuple-element.23.refs_0_, f32[16,512]{1,0:T(8,128)S(1)} %collective-permute-done.refs_1_, f32[16,512]{1,0:T(8,128)S(1)} %collective-permute-done.1.refs_0_.refs_2_, f32[16,512]{1,0:T(8,128)S(1)} %collective-permute-done.2.refs_0_.refs_3_, ...), custom_call_target="tpu_custom_call" | custom-call | tf_op jit(solution)/shard_map/finish/pallas_call | solution.py:532
Async XLA Ops:
  1.2 7.0 %collective-permute-start = (f32[16,512]{1,0:T(8,128)S(1)}, f32[16,512]{1,0:T(8,128)S(1)}, u32[]{:S(2)}, u32[]{:S(2)}) collective-permute-start(f32[16,512]{1,0:T(8,128)S(1)} %get-tuple-element.23.refs_0_), channel_id=1, source_target_pairs={{0,4},{4,8},{8,12},{12,0},{1,5},{5,9},{9,13},{13,1},{2,6},{6,10},{... | collective-permute-start | bytes 98312 | tf_op jit(solution)/shard_map/ppermute | solution.py:472
  4.4 5.6 %collective-permute-start.1 = (f32[16,512]{1,0:T(8,128)S(1)}, f32[16,512]{1,0:T(8,128)S(1)}, u32[]{:S(2)}, u32[]{:S(2)}) collective-permute-start(f32[16,512]{1,0:T(8,128)S(1)} %get-tuple-element.23.refs_0_), channel_id=1, source_target_pairs={{0,8},{4,12},{8,0},{12,4},{1,9},{5,13},{9,1},{13,5},{2,10},{6,14},... | collective-permute-start | bytes 98312 | tf_op jit(solution)/shard_map/ppermute | solution.py:472
  6.9 4.3 %collective-permute-start.2 = (f32[16,512]{1,0:T(8,128)S(1)}, f32[16,512]{1,0:T(8,128)S(1)}, u32[]{:S(2)}, u32[]{:S(2)}) collective-permute-start(f32[16,512]{1,0:T(8,128)S(1)} %get-tuple-element.23.refs_0_), channel_id=1, source_target_pairs={{0,12},{4,0},{8,4},{12,8},{1,13},{5,1},{9,5},{13,9},{2,14},{6,2},{... | collective-permute-start | bytes 98312 | tf_op jit(solution)/shard_map/ppermute | solution.py:472
  12.8 1.7 %collective-permute-start.3 = (f32[8,384]{1,0:T(8,128)S(1)}, f32[8,384]{1,0:T(8,128)S(1)}, u32[]{:S(2)}, u32[]{:S(2)}) collective-permute-start(f32[8,384]{1,0:T(8,128)S(1)} %get-tuple-element.35.refs_4_), channel_id=1, source_target_pairs={{0,1},{1,0},{2,3},{3,2},{4,5},{5,4},{6,7},{7,6},{8,9},{9,8},{10,11... | collective-permute-start | bytes 36872 | tf_op jit(solution)/shard_map/ppermute | solution.py:521
  13.1 1.4 %copy-start = (f32[12,512]{1,0:T(8,128)S(1)}, f32[12,512]{1,0:T(8,128)}, u32[]{:S(2)}) copy-start(f32[12,512]{1,0:T(8,128)} %refs_10_.1) | copy-start | bytes 73732

commit v14 on v12

--- a/solution.py
+++ b/solution.py
@@ -251,7 +251,9 @@
         for g in range(many):
             here = pl.ds(base + 8 * g, 8)
             for j, (target_ref, columns_ref, before_ref, sources, after_ref) in enumerate(groups):
-                if columns_ref is None:
+                if not sources:
+                    target = None
+                elif columns_ref is None:
                     target = [target_ref[r, here, :] for r in range(6)]
                 else:
                     columns = columns_ref[here, :]
@@ -313,13 +315,13 @@
             run(sum(shares[:m]), shares[m])
 
 
-def meet(slots, shares, known, fresh, *refs):
+def meet(slots, shares, known, fresh, tail, *refs):
     every = known + fresh
     sent, refs = refs[:fresh], refs[fresh:]
     old_sources, old_targets, before = refs[:known], refs[known : 2 * known], refs[2 * known : 3 * known]
     refs = refs[3 * known :]
     new_sources, new_targets, after = refs[:fresh], refs[fresh : 2 * fresh], refs[2 * fresh : 2 * fresh + every]
-    columns_ref = refs[2 * fresh + every]
+    refs = refs[2 * fresh + every :]
     sources = old_sources + new_sources
 
     def run(start, count):
@@ -330,78 +332,90 @@
             spread_sources(sent[d][0:8, :], new_sources[d], 0)
             in_loop = None
             if known:
-                in_loop = columns_ref
-                columns_ref[...] = jnp.transpose(sent[d][0:8, 0:slots])
+                in_loop = refs[-1]
+                in_loop[...] = jnp.transpose(sent[d][0:8, 0:slots])
+            elif d == 0 and start > 0:
+                spread_targets(sent[d][0:8, 0:slots], new_targets[d], 0, slots)
             else:
                 spread_targets(sent[d][0:8, 0:slots], new_targets[d], start, count)
             groups.append((new_targets[d], in_loop, None, sources, after[known + d]))
         run_pairs(groups, slots, start, count, 2, False, None, None)
+        if tail:
+            part_ref, partial_ref, sums_ref = refs[0:3]
+            if start == 0:
+                group = (None, None, after[0], (), None)
+                part_ref[...] = run_pairs(
+                    [group], slots, start, count, count // 8, True, partial_ref, sums_ref
+                )[0]
+            else:
+                part_ref[...] = jnp.zeros_like(part_ref)
 
     on_member(shares, run)
 
 
-def meet_own(slots, shares, early, sent_ref, own_target, own_before, *refs):
+def meet_own(slots, shares, early, sent_ref, part_ref, own_target, own_before, *refs):
     known = len(refs) - 8
     sources = refs[:known]
     source_ref, own_ref, late_ref, target_ref, own_partial, own_sums, partial_ref, sums_ref = refs[known:]
     spread_sources(sent_ref[0:8, :], source_ref, 0)
-
-    def own(start, count):
-        group = (own_target, None, own_before, (source_ref,), None)
-        own_ref[...] = run_pairs(
-            [group], slots, start, count, count // 8, True, own_partial, own_sums
-        )[0]
-
     member = lax.rem(lax.axis_index("act"), 2)
 
     @pl.when(member == 0)
     def _():
         late_ref[...] = jnp.zeros_like(late_ref)
-        spread_targets(sent_ref[0:8, 0:slots], target_ref, early, slots - early)
-        own(0, shares[0])
+        own_ref[...] = part_ref[...]
 
     @pl.when(member == 1)
     def _():
         spread_targets(sent_ref[0:8, 0:slots], target_ref, 0, slots)
-        own(shares[0], shares[1])
+        rows, width = max(shares) * 6, slots + max(shares)
+        own = []
+        for m, before in enumerate((None, own_before)):
+            group = (own_target, None, before, (source_ref,), None)
+            own += run_pairs(
+                [group],
+                slots,
+                sum(shares[:m]),
+                shares[m],
+                shares[m] // 8,
+                True,
+                own_partial.at[m * rows : (m + 1) * rows],
+                own_sums.at[m * width : (m + 1) * width],
+            )
+        own_ref[...] = own[0] + own[1]
         group = (target_ref, None, None, sources + (source_ref,), None)
         late_ref[...] = run_pairs([group], slots, 0, early, 4, True, partial_ref, sums_ref)[0]
 
 
-def meet_rest(slots, shares, early, source_ref, late_ref, late_target, *refs):
-    known = (len(refs) - 4) // 3
+def meet_rest(slots, shares, late_shares, sent_ref, source_ref, late_ref, late_target, *refs):
+    known = (len(refs) - 7) // 3
     sources, targets, before = refs[: known + 1], refs[known + 1 : 2 * known + 1], refs[2 * known + 1 : 3 * known + 1]
-    forces_ref, partial_ref, sums_ref = refs[3 * known + 1 :]
-    half = (slots - early) // 2
-    used = half * 6
+    forces_ref, partial_ref, sums_ref, late_partial, late_sums, target_ref = refs[3 * known + 1 :]
 
     def run(start, count):
-        group = (late_target, None, None, sources + (source_ref,), None)
-        first = early if start == 0 else early + half
+        member = 0 if start == 0 else 1
+        first, many = slots - sum(late_shares[member:]), late_shares[member]
+        goal = late_target
+        if member == 0:
+            goal = target_ref
+            spread_targets(sent_ref[0:8, 0:slots], target_ref, first, many)
+        groups = [(t, None, b, (source_ref,), None) for t, b in zip(targets, before)]
+        forces = run_pairs(groups, slots, start, count, 4, True, partial_ref, sums_ref)
+        for d in range(known):
+            forces_ref[:, d * slots : (d + 1) * slots] = forces[d]
+        group = (goal, None, None, sources + (source_ref,), None)
+        together = max(many // 16, 1)
         late = run_pairs(
             [group],
             slots,
             first,
-            half,
-            half // 8,
+            many,
+            together,
             True,
-            partial_ref.at[0:used],
-            sums_ref.at[0 : slots + half],
+            late_partial,
+            late_sums.at[0 : slots + 8 * together],
         )[0]
         forces_ref[:, known * slots : (known + 1) * slots] = late_ref[...] + late
-        groups = [(t, None, b, (source_ref,), None) for t, b in zip(targets, before)]
-        forces = run_pairs(
-            groups,
-            slots,
-            start,
-            count,
-            count // 8,
-            True,
-            partial_ref.at[used : used + count * known * 6],
-            sums_ref.at[slots + half : slots + half + known * (slots + count)],
-        )
-        for d in range(known):
-            forces_ref[:, d * slots : (d + 1) * slots] = forces[d]
 
     on_member(shares, run)
 
@@ -547,38 +561,44 @@
     known = 0
     for fresh in [2] + [1] * (shards - 3):
         every = known + fresh
+        tail = every == shards - 1
         outs = call(
-            functools.partial(meet, slots, shares, known, fresh),
+            functools.partial(meet, slots, shares, known, fresh, tail),
             [*sent[known:every], *sources, *targets, *sums],
-            [source_shape] * fresh + [target_shape] * (fresh + every),
-            [rows((slots, 8))],
+            [source_shape] * fresh + [target_shape] * (fresh + every) + [own_shape] * tail,
+            [rows((max(shares) * 6, 128)), rows((slots + max(shares), 8))] * tail
+            + [rows((slots, 8))],
         )
         sources += outs[:fresh]
         targets += outs[fresh : 2 * fresh]
-        sums = list(outs[2 * fresh :])
+        sums = list(outs[2 * fresh : 2 * fresh + every])
         known = every
-    early = slots * 3 // 4
+    early = slots // 2
+    late_shares = (slots * 3 // 8, slots // 8)
     source, own, late, late_target = call(
         functools.partial(meet_own, slots, shares, early),
-        [sent[known], targets[0], sums[0], *sources],
+        [sent[known], outs[-1], targets[0], sums[0], *sources],
         (source_shape, own_shape, own_shape, target_shape),
         [
-            rows((max(shares) * 6, 128)),
-            rows((slots + max(shares), 8)),
+            rows((2 * max(shares) * 6, 128)),
+            rows((2 * (slots + max(shares)), 8)),
             rows((4 * 48, 128)),
             rows((slots + 32, 8)),
         ],
     )
     others = known - 1
-    half = (slots - early) // 2
+    together = max(late_shares) // 16
     own = with_other(own)
     forces = call(
-        functools.partial(meet_rest, slots, shares, early),
-        [source, late, late_target, *sources, *targets[1:], *sums[1:]],
+        functools.partial(meet_rest, slots, shares, late_shares),
+        [sent[known], source, late, late_target, *sources, *targets[1:], *sums[1:]],
         jax.ShapeDtypeStruct((8, known * slots), jnp.float32),
         [
-            rows((half * 6 + max(shares) * others * 6, 128)),
-            rows((slots + half + others * (slots + max(shares)), 8)),
+            rows((4 * others * 48, 128)),
+            rows((others * (slots + 32), 8)),
+            rows((together * 48, 128)),
+            rows((slots + 8 * together, 8)),
+            rows(target_shape.shape),
         ],
         others * max(shares) * size,
     )

time: 16.4 us -> 16.7 us (1.018)
  Pallas kernels: 7.29 us -> 7.85 us
  waiting for transfers between devices: 1.28 us -> 1.07 us
    pallas_call x6, Pallas kernels: 6.05 us -> 6.61 us  [call(): pl.pallas_call(body, out_shape=out_shape, in_specs=[whole] * len(operands...]
    ppermute x3, waiting for transfers between devices: 0.45 us -> 0.24 us  [direct_per_device(): sent.append(lax.ppermute(message, 'src', pairs))]
where the time goes in v14:
time: 16.7 us; the launch traced here: 16.6 us
  Pallas kernels  7.85 us (47%)
  starting transfers between devices  7.58 us (45%)
  waiting for transfers between devices  1.07 us (6%)
    ppermute x3, starting transfers between devices, direct_per_device(): sent.append(lax.ppermute(message, 'src', pairs))  7.04 us
    pallas_call x6, Pallas kernels, call(): pl.pallas_call(body, out_shape=out_shape, in_specs=[whole] * len(operands...  6.61 us
    pallas_call x1, Pallas kernels, direct_per_device(): pl.pallas_call(lambda *refs: prepare(slots, size * shards, *refs), out_sh...  1.24 us
    ppermute x2, waiting for transfers between devices, with_other(): lax.ppermute(part, 'act', [(i, i ^ 1) for i in range(owners)])  0.83 us
    ppermute x2, starting transfers between devices, with_other(): lax.ppermute(part, 'act', [(i, i ^ 1) for i in range(owners)])  0.53 us
  transfers between devices with their start and end apart: 5, of which 3 were waited for; matrix products, arithmetic and copies ran while one was open for 0% of the time, Pallas kernels for 22%

profile of v14, /device:TPU:0, one launch (start us, length us, event | category | flops | bytes accessed | tf_op | source)
XLA Modules:
  0.0 16.6 jit_solution(17710203848270914251)
XLA Ops:
  0.0 1.2 %prepare.1 = (f32[16,512]{1,0:T(8,128)S(1)}, f32[8,512]{1,0:T(8,128)S(1)}) custom-call(f32[12,512]{1,0:T(8,128)} %refs_10_.1, f32[1,512]{1,0:T(1,128)} %bitcast.3, f32[1,512]{1,0:T(1,128)} %bitcast.4, s32[1,512]{1,0:T(1,128)} %bitcast.5), custom_call_target="tpu_custom_call" | custom-call | tf_op jit(solution)/shard_map/prepare/pallas_call | solution.py:506
  1.2 3.1 %collective-permute-start = (f32[16,512]{1,0:T(8,128)S(1)}, f32[16,512]{1,0:T(8,128)S(1)}, u32[]{:S(2)}, u32[]{:S(2)}) collective-permute-start(f32[16,512]{1,0:T(8,128)S(1)} %get-tuple-element.27.refs_0_), channel_id=1, source_target_pairs={{0,4},{4,8},{8,12},{12,0},{1,5},{5,9},{9,13},{13,1},{2,6},{6,10},{... | collective-permute-start | bytes 98312 | tf_op jit(solution)/shard_map/ppermute | solution.py:532
  4.4 2.6 %collective-permute-start.1 = (f32[16,512]{1,0:T(8,128)S(1)}, f32[16,512]{1,0:T(8,128)S(1)}, u32[]{:S(2)}, u32[]{:S(2)}) collective-permute-start(f32[16,512]{1,0:T(8,128)S(1)} %get-tuple-element.27.refs_0_), channel_id=1, source_target_pairs={{0,8},{4,12},{8,0},{12,4},{1,9},{5,13},{9,1},{13,5},{2,10},{6,14},... | collective-permute-start | bytes 98312 | tf_op jit(solution)/shard_map/ppermute | solution.py:532
  6.9 1.3 %collective-permute-start.2 = (f32[16,512]{1,0:T(8,128)S(1)}, f32[16,512]{1,0:T(8,128)S(1)}, u32[]{:S(2)}, u32[]{:S(2)}) collective-permute-start(f32[16,512]{1,0:T(8,128)S(1)} %get-tuple-element.27.refs_0_), channel_id=1, source_target_pairs={{0,12},{4,0},{8,4},{12,8},{1,13},{5,1},{9,5},{13,9},{2,14},{6,2},{... | collective-permute-start | bytes 98312 | tf_op jit(solution)/shard_map/ppermute | solution.py:532
  8.3 0.0 collective-permute-done.refs_1_
  8.3 1.0 %shard_map.46 = (f32[7,32,128]{2,1,0:T(8,128)S(1)}, f32[7,32,128]{2,1,0:T(8,128)S(1)}, f32[6,128,128]{2,1,0:T(8,128)S(1)}, f32[6,128,128]{2,1,0:T(8,128)S(1)}, f...) custom-call(f32[16,512]{1,0:T(8,128)S(1)} %get-tuple-element.27.refs_0_, f32[16,512]{1,0:T(8,128)S(1)} %collective-permute-done.refs_1_), custom_call_target="tpu_custom_call" | custom-call | tf_op jit(solution)/shard_map/pallas_call | solution.py:544
  9.3 0.2 %collective-permute-done.1.refs_0_.refs_2_ = f32[16,512]{1,0:T(8,128)S(1)} collective-permute-done((f32[16,512]{1,0:T(8,128)S(1)}, f32[16,512]{1,0:T(8,128)S(1)}, u32[]{:S(2)}, u32[]{:S(2)}) %collective-permute-start.1) | collective-permute-done | bytes 32800 | tf_op jit(solution)/shard_map/ppermute | solution.py:532
  9.5 1.3 %shard_map.47 = (f32[7,32,128]{2,1,0:T(8,128)S(1)}, f32[6,128,128]{2,1,0:T(8,128)S(1)}, f32[6,128,128]{2,1,0:T(8,128)S(1)}, f32[6,128,128]{2,1,0:T(8,128)S(1)}, ...) custom-call(f32[16,512]{1,0:T(8,128)S(1)} %collective-permute-done.1.refs_0_.refs_2_, ...), custom_call_target="tpu_custom_call" | custom-call | tf_op jit(solution)/shard_map/pallas_call | solution.py:544
  10.8 0.1 collective-permute-done.2.sent_ref.refs_3_
  10.9 1.5 %shard_map.49.refs_4_ = f32[8,384]{1,0:T(8,128)S(1)} custom-call(f32[16,512]{1,0:T(8,128)S(1)} %collective-permute-done.2.sent_ref.refs_3_, f32[7,32,128]{2,1,0:T(8,128)S(1)} %get-tuple-element.37.source_ref, f32[8,128]{1,0:T(8,128)S(1)} %get-tuple-element.38.late_ref, f32[6,128,128]{2,1,0:T(8,128)S(1)} %get-tuple-element.39.late_target, ...), custom_call_target="tpu_custom_call" | custom-call | flops 2686976 | tf_op jit(solution)/shard_map/pallas_call | solution.py:544
  12.4 0.0 collective-permute-start.3
  12.4 0.0 copy-start
  12.5 0.5 %collective-permute-start.4 = (f32[8,128]{1,0:T(8,128)S(1)}, f32[8,128]{1,0:T(8,128)S(1)}, u32[]{:S(2)}, u32[]{:S(2)}) collective-permute-start(f32[8,128]{1,0:T(8,128)S(1)} %get-tuple-element.43.refs_4_), channel_id=1, source_target_pairs={{0,1},{1,0},{2,3},{3,2},{4,5},{5,4},{6,7},{7,6},{8,9},{9,8},{10,11... | collective-permute-start | bytes 12296 | tf_op jit(solution)/shard_map/ppermute | solution.py:540
  12.9 0.8 %collective-permute-done.4.refs_5_ = f32[8,128]{1,0:T(8,128)S(1)} collective-permute-done((f32[8,128]{1,0:T(8,128)S(1)}, f32[8,128]{1,0:T(8,128)S(1)}, u32[]{:S(2)}, u32[]{:S(2)}) %collective-permute-start.4) | collective-permute-done | bytes 4128 | tf_op jit(solution)/shard_map/ppermute | solution.py:540
  13.8 1.4 %shard_map.50 = (f32[8,128]{1,0:T(8,128)S(1)}, f32[8,128]{1,0:T(8,128)S(1)}, f32[6,128,128]{2,1,0:T(8,128)S(1)}, f32[6,128,128]{2,1,0:T(8,128)S(1)}) custom-call(f32[16,512]{1,0:T(8,128)S(1)} %get-tuple-element.27.refs_0_, f32[16,512]{1,0:T(8,128)S(1)} %collective-permute-done.refs_1_, f32[16,512]{1,0:T(8,128)S(1)} %collective-permute-done.1.refs_0_.refs_2_, ...), custom_call_target="tpu_custom_call" | custom-call | flops 8060928 | tf_op jit(solution)/shard_map/pallas_call | solution.py:544
  15.2 0.0 collective-permute-done.3.refs_5_
  15.2 0.0 copy-done
  15.2 1.4 %shard_map.51 = f32[12,512]{1,0:T(8,128)} custom-call(f32[16,512]{1,0:T(8,128)S(1)} %get-tuple-element.27.refs_0_, f32[16,512]{1,0:T(8,128)S(1)} %collective-permute-done.refs_1_, f32[16,512]{1,0:T(8,128)S(1)} %collective-permute-done.1.refs_0_.refs_2_, f32[16,512]{1,0:T(8,128)S(1)} %collective-permute-done.2.sent_ref.refs_3_, ...), custom_call_target="tpu_custom_call" | custom-call | tf_op jit(solution)/shard_map/pallas_call | solution.py:544
  (1 shorter events, 0.0 us)
Async XLA Ops:
  1.2 7.0 %collective-permute-start = (f32[16,512]{1,0:T(8,128)S(1)}, f32[16,512]{1,0:T(8,128)S(1)}, u32[]{:S(2)}, u32[]{:S(2)}) collective-permute-start(f32[16,512]{1,0:T(8,128)S(1)} %get-tuple-element.27.refs_0_), channel_id=1, source_target_pairs={{0,4},{4,8},{8,12},{12,0},{1,5},{5,9},{9,13},{13,1},{2,6},{6,10},{... | collective-permute-start | bytes 98312 | tf_op jit(solution)/shard_map/ppermute | solution.py:532
  4.4 5.2 %collective-permute-start.1 = (f32[16,512]{1,0:T(8,128)S(1)}, f32[16,512]{1,0:T(8,128)S(1)}, u32[]{:S(2)}, u32[]{:S(2)}) collective-permute-start(f32[16,512]{1,0:T(8,128)S(1)} %get-tuple-element.27.refs_0_), channel_id=1, source_target_pairs={{0,8},{4,12},{8,0},{12,4},{1,9},{5,13},{9,1},{13,5},{2,10},{6,14},... | collective-permute-start | bytes 98312 | tf_op jit(solution)/shard_map/ppermute | solution.py:532
  6.9 3.9 %collective-permute-start.2 = (f32[16,512]{1,0:T(8,128)S(1)}, f32[16,512]{1,0:T(8,128)S(1)}, u32[]{:S(2)}, u32[]{:S(2)}) collective-permute-start(f32[16,512]{1,0:T(8,128)S(1)} %get-tuple-element.27.refs_0_), channel_id=1, source_target_pairs={{0,12},{4,0},{8,4},{12,8},{1,13},{5,1},{9,5},{13,9},{2,14},{6,2},{... | collective-permute-start | bytes 98312 | tf_op jit(solution)/shard_map/ppermute | solution.py:532
  12.4 2.8 %collective-permute-start.3 = (f32[8,384]{1,0:T(8,128)S(1)}, f32[8,384]{1,0:T(8,128)S(1)}, u32[]{:S(2)}, u32[]{:S(2)}) collective-permute-start(f32[8,384]{1,0:T(8,128)S(1)} %shard_map.49.refs_4_), channel_id=1, source_target_pairs={{0,1},{1,0},{2,3},{3,2},{4,5},{5,4},{6,7},{7,6},{8,9},{9,8},{10,11... | collective-permute-start | bytes 36872 | tf_op jit(solution)/shard_map/ppermute | solution.py:540
  12.4 2.7 %copy-start = (f32[12,512]{1,0:T(8,128)S(1)}, f32[12,512]{1,0:T(8,128)}, u32[]{:S(2)}) copy-start(f32[12,512]{1,0:T(8,128)} %refs_10_.1) | copy-start | bytes 73732
  12.5 1.3 %collective-permute-start.4 = (f32[8,128]{1,0:T(8,128)S(1)}, f32[8,128]{1,0:T(8,128)S(1)}, u32[]{:S(2)}, u32[]{:S(2)}) collective-permute-start(f32[8,128]{1,0:T(8,128)S(1)} %get-tuple-element.43.refs_4_), channel_id=1, source_target_pairs={{0,1},{1,0},{2,3},{3,2},{4,5},{5,4},{6,7},{7,6},{8,9},{9,8},{10,11... | collective-permute-start | bytes 12296 | tf_op jit(solution)/shard_map/ppermute | solution.py:540

commit v15 on v12

--- a/solution.py
+++ b/solution.py
@@ -349,7 +349,7 @@
     def own(start, count):
         group = (own_target, None, own_before, (source_ref,), None)
         own_ref[...] = run_pairs(
-            [group], slots, start, count, count // 8, True, own_partial, own_sums
+            [group], slots, start, count, 4, True, own_partial, own_sums
         )[0]
 
     member = lax.rem(lax.axis_index("act"), 2)
@@ -365,43 +365,33 @@
         spread_targets(sent_ref[0:8, 0:slots], target_ref, 0, slots)
         own(shares[0], shares[1])
         group = (target_ref, None, None, sources + (source_ref,), None)
-        late_ref[...] = run_pairs([group], slots, 0, early, 4, True, partial_ref, sums_ref)[0]
+        late_ref[...] = run_pairs([group], slots, 0, early, 2, True, partial_ref, sums_ref)[0]
 
 
 def meet_rest(slots, shares, early, source_ref, late_ref, late_target, *refs):
     known = (len(refs) - 4) // 3
     sources, targets, before = refs[: known + 1], refs[known + 1 : 2 * known + 1], refs[2 * known + 1 : 3 * known + 1]
     forces_ref, partial_ref, sums_ref = refs[3 * known + 1 :]
-    half = (slots - early) // 2
-    used = half * 6
 
     def run(start, count):
-        group = (late_target, None, None, sources + (source_ref,), None)
-        first = early if start == 0 else early + half
-        late = run_pairs(
-            [group],
-            slots,
-            first,
-            half,
-            half // 8,
-            True,
-            partial_ref.at[0:used],
-            sums_ref.at[0 : slots + half],
-        )[0]
-        forces_ref[:, known * slots : (known + 1) * slots] = late_ref[...] + late
         groups = [(t, None, b, (source_ref,), None) for t, b in zip(targets, before)]
-        forces = run_pairs(
-            groups,
-            slots,
-            start,
-            count,
-            count // 8,
-            True,
-            partial_ref.at[used : used + count * known * 6],
-            sums_ref.at[slots + half : slots + half + known * (slots + count)],
-        )
+        forces = run_pairs(groups, slots, start, count, 4, True, partial_ref, sums_ref)
         for d in range(known):
             forces_ref[:, d * slots : (d + 1) * slots] = forces[d]
+        late = late_ref[...]
+        if start == 0:
+            group = (late_target, None, None, sources + (source_ref,), None)
+            late += run_pairs(
+                [group],
+                slots,
+                early,
+                slots - early,
+                1,
+                True,
+                partial_ref.at[0:48],
+                sums_ref.at[0 : slots + 8],
+            )[0]
+        forces_ref[:, known * slots : (known + 1) * slots] = late
 
     on_member(shares, run)
 
@@ -557,7 +547,7 @@
         targets += outs[fresh : 2 * fresh]
         sums = list(outs[2 * fresh :])
         known = every
-    early = slots * 3 // 4
+    early = slots * 7 // 8
     source, own, late, late_target = call(
         functools.partial(meet_own, slots, shares, early),
         [sent[known], targets[0], sums[0], *sources],
@@ -570,15 +560,14 @@
         ],
     )
     others = known - 1
-    half = (slots - early) // 2
     own = with_other(own)
     forces = call(
         functools.partial(meet_rest, slots, shares, early),
         [source, late, late_target, *sources, *targets[1:], *sums[1:]],
         jax.ShapeDtypeStruct((8, known * slots), jnp.float32),
         [
-            rows((half * 6 + max(shares) * others * 6, 128)),
-            rows((slots + half + others * (slots + max(shares)), 8)),
+            rows((4 * others * 48, 128)),
+            rows((others * (slots + 32), 8)),
         ],
         others * max(shares) * size,
     )

time: 16.4 us -> 16.7 us (1.018)
  Pallas kernels: 7.29 us -> 7.58 us
    pallas_call x6, Pallas kernels: 6.05 us -> 6.34 us  [call(): pl.pallas_call(body, out_shape=out_shape, in_specs=[whole] * len(operands...]
  transfers between devices with their start and end apart: 5 -> 5, of which waited for: 3 -> 3; matrix products, arithmetic and copies ran while one was open for 0% -> 0% of each run, Pallas kernels for 22% -> 21%
where the time goes in v15:
time: 16.7 us; the launch traced here: 16.5 us
  Pallas kernels  7.58 us (45%)
  starting transfers between devices  7.58 us (45%)
  waiting for transfers between devices  1.28 us (8%)
    ppermute x3, starting transfers between devices, direct_per_device(): sent.append(lax.ppermute(message, 'src', pairs))  7.04 us
    pallas_call x6, Pallas kernels, call(): pl.pallas_call(body, out_shape=out_shape, in_specs=[whole] * len(operands...  6.34 us
    pallas_call x1, Pallas kernels, direct_per_device(): pl.pallas_call(lambda *refs: prepare(slots, size * shards, *refs), out_sh...  1.24 us
    ppermute x2, waiting for transfers between devices, with_other(): lax.ppermute(part, 'act', [(i, i ^ 1) for i in range(owners)])  0.83 us
    ppermute x2, starting transfers between devices, with_other(): lax.ppermute(part, 'act', [(i, i ^ 1) for i in range(owners)])  0.54 us
    ppermute x3, waiting for transfers between devices, direct_per_device(): sent.append(lax.ppermute(message, 'src', pairs))  0.45 us
  transfers between devices with their start and end apart: 5, of which 3 were waited for; matrix products, arithmetic and copies ran while one was open for 0% of the time, Pallas kernels for 21%

profile of v15, /device:TPU:0, one launch (start us, length us, event | category | flops | bytes accessed | tf_op | source)
XLA Modules:
  0.0 16.5 jit_solution(14329781735923530923)
XLA Ops:
  0.0 1.2 %prepare.1 = (f32[16,512]{1,0:T(8,128)S(1)}, f32[8,512]{1,0:T(8,128)S(1)}) custom-call(f32[12,512]{1,0:T(8,128)} %refs_10_.1, f32[1,512]{1,0:T(1,128)} %bitcast.3, f32[1,512]{1,0:T(1,128)} %bitcast.4, s32[1,512]{1,0:T(1,128)} %bitcast.5), custom_call_target="tpu_custom_call" | custom-call | tf_op jit(solution)/shard_map/prepare/pallas_call | solution.py:482
  1.2 3.1 %collective-permute-start = (f32[16,512]{1,0:T(8,128)S(1)}, f32[16,512]{1,0:T(8,128)S(1)}, u32[]{:S(2)}, u32[]{:S(2)}) collective-permute-start(f32[16,512]{1,0:T(8,128)S(1)} %get-tuple-element.26.refs_0_), channel_id=1, source_target_pairs={{0,4},{4,8},{8,12},{12,0},{1,5},{5,9},{9,13},{13,1},{2,6},{6,10},{... | collective-permute-start | bytes 98312 | tf_op jit(solution)/shard_map/ppermute | solution.py:508
  4.4 2.6 %collective-permute-start.1 = (f32[16,512]{1,0:T(8,128)S(1)}, f32[16,512]{1,0:T(8,128)S(1)}, u32[]{:S(2)}, u32[]{:S(2)}) collective-permute-start(f32[16,512]{1,0:T(8,128)S(1)} %get-tuple-element.26.refs_0_), channel_id=1, source_target_pairs={{0,8},{4,12},{8,0},{12,4},{1,9},{5,13},{9,1},{13,5},{2,10},{6,14},... | collective-permute-start | bytes 98312 | tf_op jit(solution)/shard_map/ppermute | solution.py:508
  6.9 1.3 %collective-permute-start.2 = (f32[16,512]{1,0:T(8,128)S(1)}, f32[16,512]{1,0:T(8,128)S(1)}, u32[]{:S(2)}, u32[]{:S(2)}) collective-permute-start(f32[16,512]{1,0:T(8,128)S(1)} %get-tuple-element.26.refs_0_), channel_id=1, source_target_pairs={{0,12},{4,0},{8,4},{12,8},{1,13},{5,1},{9,5},{13,9},{2,14},{6,2},{... | collective-permute-start | bytes 98312 | tf_op jit(solution)/shard_map/ppermute | solution.py:508
  8.3 0.0 collective-permute-done.refs_1_
  8.3 1.0 %shard_map.46 = (f32[7,32,128]{2,1,0:T(8,128)S(1)}, f32[7,32,128]{2,1,0:T(8,128)S(1)}, f32[6,128,128]{2,1,0:T(8,128)S(1)}, f32[6,128,128]{2,1,0:T(8,128)S(1)}, f...) custom-call(f32[16,512]{1,0:T(8,128)S(1)} %get-tuple-element.26.refs_0_, f32[16,512]{1,0:T(8,128)S(1)} %collective-permute-done.refs_1_), custom_call_target="tpu_custom_call" | custom-call | tf_op jit(solution)/shard_map/pallas_call | solution.py:520
  9.3 0.2 %collective-permute-done.1.refs_0_.refs_2_ = f32[16,512]{1,0:T(8,128)S(1)} collective-permute-done((f32[16,512]{1,0:T(8,128)S(1)}, f32[16,512]{1,0:T(8,128)S(1)}, u32[]{:S(2)}, u32[]{:S(2)}) %collective-permute-start.1) | collective-permute-done | bytes 32800 | tf_op jit(solution)/shard_map/ppermute | solution.py:508
  9.5 1.1 %shard_map.47 = (f32[7,32,128]{2,1,0:T(8,128)S(1)}, f32[6,128,128]{2,1,0:T(8,128)S(1)}, f32[6,128,128]{2,1,0:T(8,128)S(1)}, f32[6,128,128]{2,1,0:T(8,128)S(1)}, f32[6,128,128]{2,1,0:T(8,128)S(1)}) custom-call(f32[16,512]{1,0:T(8,128)S(1)} %collective-permute-done.1.refs_0_.refs_2_, f32[7,32,128]{2,1,0:T(8,128)S(1)} %get-tuple-element.28.refs_1_.refs_0_, ...), custom_call_target="tpu_custom_call" | custom-call | tf_op jit(solution)/shard_map/pallas_call | solution.py:520
  10.6 0.3 %collective-permute-done.2.sent_ref.refs_3_ = f32[16,512]{1,0:T(8,128)S(1)} collective-permute-done((f32[16,512]{1,0:T(8,128)S(1)}, f32[16,512]{1,0:T(8,128)S(1)}, u32[]{:S(2)}, u32[]{:S(2)}) %collective-permute-start.2) | collective-permute-done | bytes 32800 | tf_op jit(solution)/shard_map/ppermute | solution.py:508
  10.9 0.5 %shard_map.48 = (f32[7,32,128]{2,1,0:T(8,128)S(1)}, f32[8,128]{1,0:T(8,128)S(1)}, f32[8,128]{1,0:T(8,128)S(1)}, f32[6,128,128]{2,1,0:T(8,128)S(1)}) custom-call(f32[16,512]{1,0:T(8,128)S(1)} %collective-permute-done.2.sent_ref.refs_3_, f32[6,128,128]{2,1,0:T(8,128)S(1)} %get-tuple-element.27.refs_3_.own_target, ...), custom_call_target="tpu_custom_call" | custom-call | tf_op jit(solution)/shard_map/pallas_call | solution.py:520
  11.4 0.9 %shard_map.49.refs_4_ = f32[8,384]{1,0:T(8,128)S(1)} custom-call(f32[7,32,128]{2,1,0:T(8,128)S(1)} %get-tuple-element.35.source_ref, f32[8,128]{1,0:T(8,128)S(1)} %get-tuple-element.36.late_ref, f32[6,128,128]{2,1,0:T(8,128)S(1)} %get-tuple-element.37.late_target, f32[7,32,128]{2,1,0:T(8,128)S(1)} %get-tuple-element.28.refs_1_.refs_0_, ...), custom_call_target="tpu_custom_call" | custom-call | flops 2686976 | tf_op jit(solution)/shard_map/pallas_call | solution.py:520
  12.3 0.1 collective-permute-start.3
  12.4 0.0 copy-start
  12.4 0.5 %collective-permute-start.4 = (f32[8,128]{1,0:T(8,128)S(1)}, f32[8,128]{1,0:T(8,128)S(1)}, u32[]{:S(2)}, u32[]{:S(2)}) collective-permute-start(f32[8,128]{1,0:T(8,128)S(1)} %get-tuple-element.41.refs_4_), channel_id=1, source_target_pairs={{0,1},{1,0},{2,3},{3,2},{4,5},{5,4},{6,7},{7,6},{8,9},{9,8},{10,11... | collective-permute-start | bytes 12296 | tf_op jit(solution)/shard_map/ppermute | solution.py:516
  12.9 0.8 %collective-permute-done.4.refs_5_ = f32[8,128]{1,0:T(8,128)S(1)} collective-permute-done((f32[8,128]{1,0:T(8,128)S(1)}, f32[8,128]{1,0:T(8,128)S(1)}, u32[]{:S(2)}, u32[]{:S(2)}) %collective-permute-start.4) | collective-permute-done | bytes 4128 | tf_op jit(solution)/shard_map/ppermute | solution.py:516
  13.7 1.4 %shard_map.50 = (f32[8,128]{1,0:T(8,128)S(1)}, f32[8,128]{1,0:T(8,128)S(1)}, f32[6,128,128]{2,1,0:T(8,128)S(1)}, f32[6,128,128]{2,1,0:T(8,128)S(1)}) custom-call(f32[16,512]{1,0:T(8,128)S(1)} %get-tuple-element.26.refs_0_, f32[16,512]{1,0:T(8,128)S(1)} %collective-permute-done.refs_1_, f32[16,512]{1,0:T(8,128)S(1)} %collective-permute-done.1.refs_0_.refs_2_, ...), custom_call_target="tpu_custom_call" | custom-call | flops 8060928 | tf_op jit(solution)/shard_map/pallas_call | solution.py:520
  15.1 0.0 collective-permute-done.3.refs_5_
  15.1 0.0 copy-done
  15.1 1.4 %shard_map.51 = f32[12,512]{1,0:T(8,128)} custom-call(f32[16,512]{1,0:T(8,128)S(1)} %get-tuple-element.26.refs_0_, f32[16,512]{1,0:T(8,128)S(1)} %collective-permute-done.refs_1_, f32[16,512]{1,0:T(8,128)S(1)} %collective-permute-done.1.refs_0_.refs_2_, f32[16,512]{1,0:T(8,128)S(1)} %collective-permute-done.2.sent_ref.refs_3_, ...), custom_call_target="tpu_custom_call" | custom-call | tf_op jit(solution)/shard_map/pallas_call | solution.py:520
Async XLA Ops:
  1.2 7.0 %collective-permute-start = (f32[16,512]{1,0:T(8,128)S(1)}, f32[16,512]{1,0:T(8,128)S(1)}, u32[]{:S(2)}, u32[]{:S(2)}) collective-permute-start(f32[16,512]{1,0:T(8,128)S(1)} %get-tuple-element.26.refs_0_), channel_id=1, source_target_pairs={{0,4},{4,8},{8,12},{12,0},{1,5},{5,9},{9,13},{13,1},{2,6},{6,10},{... | collective-permute-start | bytes 98312 | tf_op jit(solution)/shard_map/ppermute | solution.py:508
  4.4 5.2 %collective-permute-start.1 = (f32[16,512]{1,0:T(8,128)S(1)}, f32[16,512]{1,0:T(8,128)S(1)}, u32[]{:S(2)}, u32[]{:S(2)}) collective-permute-start(f32[16,512]{1,0:T(8,128)S(1)} %get-tuple-element.26.refs_0_), channel_id=1, source_target_pairs={{0,8},{4,12},{8,0},{12,4},{1,9},{5,13},{9,1},{13,5},{2,10},{6,14},... | collective-permute-start | bytes 98312 | tf_op jit(solution)/shard_map/ppermute | solution.py:508
  6.9 3.9 %collective-permute-start.2 = (f32[16,512]{1,0:T(8,128)S(1)}, f32[16,512]{1,0:T(8,128)S(1)}, u32[]{:S(2)}, u32[]{:S(2)}) collective-permute-start(f32[16,512]{1,0:T(8,128)S(1)} %get-tuple-element.26.refs_0_), channel_id=1, source_target_pairs={{0,12},{4,0},{8,4},{12,8},{1,13},{5,1},{9,5},{13,9},{2,14},{6,2},{... | collective-permute-start | bytes 98312 | tf_op jit(solution)/shard_map/ppermute | solution.py:508
  12.3 2.8 %collective-permute-start.3 = (f32[8,384]{1,0:T(8,128)S(1)}, f32[8,384]{1,0:T(8,128)S(1)}, u32[]{:S(2)}, u32[]{:S(2)}) collective-permute-start(f32[8,384]{1,0:T(8,128)S(1)} %shard_map.49.refs_4_), channel_id=1, source_target_pairs={{0,1},{1,0},{2,3},{3,2},{4,5},{5,4},{6,7},{7,6},{8,9},{9,8},{10,11... | collective-permute-start | bytes 36872 | tf_op jit(solution)/shard_map/ppermute | solution.py:516
  12.4 2.7 %copy-start = (f32[12,512]{1,0:T(8,128)S(1)}, f32[12,512]{1,0:T(8,128)}, u32[]{:S(2)}) copy-start(f32[12,512]{1,0:T(8,128)} %refs_10_.1) | copy-start | bytes 73732
  12.4 1.3 %collective-permute-start.4 = (f32[8,128]{1,0:T(8,128)S(1)}, f32[8,128]{1,0:T(8,128)S(1)}, u32[]{:S(2)}, u32[]{:S(2)}) collective-permute-start(f32[8,128]{1,0:T(8,128)S(1)} %get-tuple-element.41.refs_4_), channel_id=1, source_target_pairs={{0,1},{1,0},{2,3},{3,2},{4,5},{5,4},{6,7},{7,6},{8,9},{9,8},{10,11... | collective-permute-start | bytes 12296 | tf_op jit(solution)/shard_map/ppermute | solution.py:516

commit v16 on v15

--- a/solution.py
+++ b/solution.py
@@ -349,7 +349,7 @@
     def own(start, count):
         group = (own_target, None, own_before, (source_ref,), None)
         own_ref[...] = run_pairs(
-            [group], slots, start, count, 4, True, own_partial, own_sums
+            [group], slots, start, count, count // 8, True, own_partial, own_sums
         )[0]
 
     member = lax.rem(lax.axis_index("act"), 2)
@@ -365,7 +365,7 @@
         spread_targets(sent_ref[0:8, 0:slots], target_ref, 0, slots)
         own(shares[0], shares[1])
         group = (target_ref, None, None, sources + (source_ref,), None)
-        late_ref[...] = run_pairs([group], slots, 0, early, 2, True, partial_ref, sums_ref)[0]
+        late_ref[...] = run_pairs([group], slots, 0, early, 4, True, partial_ref, sums_ref)[0]
 
 
 def meet_rest(slots, shares, early, source_ref, late_ref, late_target, *refs):
@@ -386,10 +386,10 @@
                 slots,
                 early,
                 slots - early,
-                1,
+                2,
                 True,
-                partial_ref.at[0:48],
-                sums_ref.at[0 : slots + 8],
+                partial_ref.at[0:96],
+                sums_ref.at[0 : slots + 16],
             )[0]
         forces_ref[:, known * slots : (known + 1) * slots] = late
 

time: 16.7 us -> 16.4 us (0.982)
  Pallas kernels: 7.58 us -> 7.28 us
    pallas_call x6, Pallas kernels: 6.34 us -> 6.04 us  [call(): pl.pallas_call(body, out_shape=out_shape, in_specs=[whole] * len(operands...]
  transfers between devices with their start and end apart: 5 -> 5, of which waited for: 3 -> 3; matrix products, arithmetic and copies ran while one was open for 0% -> 0% of each run, Pallas kernels for 21% -> 22%
where the time goes in v16:
time: 16.4 us; the launch traced here: 16.2 us
  starting transfers between devices  7.59 us (46%)
  Pallas kernels  7.28 us (44%)
  waiting for transfers between devices  1.28 us (8%)
    ppermute x3, starting transfers between devices, direct_per_device(): sent.append(lax.ppermute(message, 'src', pairs))  7.04 us
    pallas_call x6, Pallas kernels, call(): pl.pallas_call(body, out_shape=out_shape, in_specs=[whole] * len(operands...  6.04 us
    pallas_call x1, Pallas kernels, direct_per_device(): pl.pallas_call(lambda *refs: prepare(slots, size * shards, *refs), out_sh...  1.24 us
    ppermute x2, waiting for transfers between devices, with_other(): lax.ppermute(part, 'act', [(i, i ^ 1) for i in range(owners)])  0.83 us
    ppermute x2, starting transfers between devices, with_other(): lax.ppermute(part, 'act', [(i, i ^ 1) for i in range(owners)])  0.55 us
    ppermute x3, waiting for transfers between devices, direct_per_device(): sent.append(lax.ppermute(message, 'src', pairs))  0.45 us
  transfers between devices with their start and end apart: 5, of which 3 were waited for; matrix products, arithmetic and copies ran while one was open for 0% of the time, Pallas kernels for 22%

profile of v16, /device:TPU:0, one launch (start us, length us, event | category | flops | bytes accessed | tf_op | source)
XLA Modules:
  0.0 16.2 jit_solution(3750277956918761626)
XLA Ops:
  0.0 1.2 %prepare.1 = (f32[16,512]{1,0:T(8,128)S(1)}, f32[8,512]{1,0:T(8,128)S(1)}) custom-call(f32[12,512]{1,0:T(8,128)} %refs_10_.1, f32[1,512]{1,0:T(1,128)} %bitcast.3, f32[1,512]{1,0:T(1,128)} %bitcast.4, s32[1,512]{1,0:T(1,128)} %bitcast.5), custom_call_target="tpu_custom_call" | custom-call | tf_op jit(solution)/shard_map/prepare/pallas_call | solution.py:482
  1.2 3.1 %collective-permute-start = (f32[16,512]{1,0:T(8,128)S(1)}, f32[16,512]{1,0:T(8,128)S(1)}, u32[]{:S(2)}, u32[]{:S(2)}) collective-permute-start(f32[16,512]{1,0:T(8,128)S(1)} %get-tuple-element.26.refs_0_), channel_id=1, source_target_pairs={{0,4},{4,8},{8,12},{12,0},{1,5},{5,9},{9,13},{13,1},{2,6},{6,10},{... | collective-permute-start | bytes 98312 | tf_op jit(solution)/shard_map/ppermute | solution.py:508
  4.4 2.6 %collective-permute-start.1 = (f32[16,512]{1,0:T(8,128)S(1)}, f32[16,512]{1,0:T(8,128)S(1)}, u32[]{:S(2)}, u32[]{:S(2)}) collective-permute-start(f32[16,512]{1,0:T(8,128)S(1)} %get-tuple-element.26.refs_0_), channel_id=1, source_target_pairs={{0,8},{4,12},{8,0},{12,4},{1,9},{5,13},{9,1},{13,5},{2,10},{6,14},... | collective-permute-start | bytes 98312 | tf_op jit(solution)/shard_map/ppermute | solution.py:508
  6.9 1.3 %collective-permute-start.2 = (f32[16,512]{1,0:T(8,128)S(1)}, f32[16,512]{1,0:T(8,128)S(1)}, u32[]{:S(2)}, u32[]{:S(2)}) collective-permute-start(f32[16,512]{1,0:T(8,128)S(1)} %get-tuple-element.26.refs_0_), channel_id=1, source_target_pairs={{0,12},{4,0},{8,4},{12,8},{1,13},{5,1},{9,5},{13,9},{2,14},{6,2},{... | collective-permute-start | bytes 98312 | tf_op jit(solution)/shard_map/ppermute | solution.py:508
  8.3 0.0 collective-permute-done.refs_1_
  8.3 1.0 %shard_map.46 = (f32[7,32,128]{2,1,0:T(8,128)S(1)}, f32[7,32,128]{2,1,0:T(8,128)S(1)}, f32[6,128,128]{2,1,0:T(8,128)S(1)}, f32[6,128,128]{2,1,0:T(8,128)S(1)}, f...) custom-call(f32[16,512]{1,0:T(8,128)S(1)} %get-tuple-element.26.refs_0_, f32[16,512]{1,0:T(8,128)S(1)} %collective-permute-done.refs_1_), custom_call_target="tpu_custom_call" | custom-call | tf_op jit(solution)/shard_map/pallas_call | solution.py:520
  9.3 0.2 %collective-permute-done.1.refs_0_.refs_2_ = f32[16,512]{1,0:T(8,128)S(1)} collective-permute-done((f32[16,512]{1,0:T(8,128)S(1)}, f32[16,512]{1,0:T(8,128)S(1)}, u32[]{:S(2)}, u32[]{:S(2)}) %collective-permute-start.1) | collective-permute-done | bytes 32800 | tf_op jit(solution)/shard_map/ppermute | solution.py:508
  9.5 1.1 %shard_map.47 = (f32[7,32,128]{2,1,0:T(8,128)S(1)}, f32[6,128,128]{2,1,0:T(8,128)S(1)}, f32[6,128,128]{2,1,0:T(8,128)S(1)}, f32[6,128,128]{2,1,0:T(8,128)S(1)}, f32[6,128,128]{2,1,0:T(8,128)S(1)}) custom-call(f32[16,512]{1,0:T(8,128)S(1)} %collective-permute-done.1.refs_0_.refs_2_, f32[7,32,128]{2,1,0:T(8,128)S(1)} %get-tuple-element.28.refs_1_.refs_0_, ...), custom_call_target="tpu_custom_call" | custom-call | tf_op jit(solution)/shard_map/pallas_call | solution.py:520
  10.6 0.3 %collective-permute-done.2.sent_ref.refs_3_ = f32[16,512]{1,0:T(8,128)S(1)} collective-permute-done((f32[16,512]{1,0:T(8,128)S(1)}, f32[16,512]{1,0:T(8,128)S(1)}, u32[]{:S(2)}, u32[]{:S(2)}) %collective-permute-start.2) | collective-permute-done | bytes 32800 | tf_op jit(solution)/shard_map/ppermute | solution.py:508
  10.9 0.4 %shard_map.48 = (f32[7,32,128]{2,1,0:T(8,128)S(1)}, f32[8,128]{1,0:T(8,128)S(1)}, f32[8,128]{1,0:T(8,128)S(1)}, f32[6,128,128]{2,1,0:T(8,128)S(1)}) custom-call(f32[16,512]{1,0:T(8,128)S(1)} %collective-permute-done.2.sent_ref.refs_3_, f32[6,128,128]{2,1,0:T(8,128)S(1)} %get-tuple-element.27.refs_3_.own_target, ...), custom_call_target="tpu_custom_call" | custom-call | tf_op jit(solution)/shard_map/pallas_call | solution.py:520
  11.2 0.8 %shard_map.49.refs_4_ = f32[8,384]{1,0:T(8,128)S(1)} custom-call(f32[7,32,128]{2,1,0:T(8,128)S(1)} %get-tuple-element.35.source_ref, f32[8,128]{1,0:T(8,128)S(1)} %get-tuple-element.36.late_ref, f32[6,128,128]{2,1,0:T(8,128)S(1)} %get-tuple-element.37.late_target, f32[7,32,128]{2,1,0:T(8,128)S(1)} %get-tuple-element.28.refs_1_.refs_0_, ...), custom_call_target="tpu_custom_call" | custom-call | flops 2686976 | tf_op jit(solution)/shard_map/pallas_call | solution.py:520
  12.0 0.1 collective-permute-start.3
  12.1 0.0 copy-start
  12.1 0.5 %collective-permute-start.4 = (f32[8,128]{1,0:T(8,128)S(1)}, f32[8,128]{1,0:T(8,128)S(1)}, u32[]{:S(2)}, u32[]{:S(2)}) collective-permute-start(f32[8,128]{1,0:T(8,128)S(1)} %get-tuple-element.41.refs_4_), channel_id=1, source_target_pairs={{0,1},{1,0},{2,3},{3,2},{4,5},{5,4},{6,7},{7,6},{8,9},{9,8},{10,11... | collective-permute-start | bytes 12296 | tf_op jit(solution)/shard_map/ppermute | solution.py:516
  12.6 0.8 %collective-permute-done.4.refs_5_ = f32[8,128]{1,0:T(8,128)S(1)} collective-permute-done((f32[8,128]{1,0:T(8,128)S(1)}, f32[8,128]{1,0:T(8,128)S(1)}, u32[]{:S(2)}, u32[]{:S(2)}) %collective-permute-start.4) | collective-permute-done | bytes 4128 | tf_op jit(solution)/shard_map/ppermute | solution.py:516
  13.4 1.4 %shard_map.50 = (f32[8,128]{1,0:T(8,128)S(1)}, f32[8,128]{1,0:T(8,128)S(1)}, f32[6,128,128]{2,1,0:T(8,128)S(1)}, f32[6,128,128]{2,1,0:T(8,128)S(1)}) custom-call(f32[16,512]{1,0:T(8,128)S(1)} %get-tuple-element.26.refs_0_, f32[16,512]{1,0:T(8,128)S(1)} %collective-permute-done.refs_1_, f32[16,512]{1,0:T(8,128)S(1)} %collective-permute-done.1.refs_0_.refs_2_, ...), custom_call_target="tpu_custom_call" | custom-call | flops 8060928 | tf_op jit(solution)/shard_map/pallas_call | solution.py:520
  14.8 0.0 collective-permute-done.3.refs_5_
  14.8 0.0 copy-done
  14.8 1.4 %shard_map.51 = f32[12,512]{1,0:T(8,128)} custom-call(f32[16,512]{1,0:T(8,128)S(1)} %get-tuple-element.26.refs_0_, f32[16,512]{1,0:T(8,128)S(1)} %collective-permute-done.refs_1_, f32[16,512]{1,0:T(8,128)S(1)} %collective-permute-done.1.refs_0_.refs_2_, f32[16,512]{1,0:T(8,128)S(1)} %collective-permute-done.2.sent_ref.refs_3_, ...), custom_call_target="tpu_custom_call" | custom-call | tf_op jit(solution)/shard_map/pallas_call | solution.py:520
Async XLA Ops:
  1.2 7.0 %collective-permute-start = (f32[16,512]{1,0:T(8,128)S(1)}, f32[16,512]{1,0:T(8,128)S(1)}, u32[]{:S(2)}, u32[]{:S(2)}) collective-permute-start(f32[16,512]{1,0:T(8,128)S(1)} %get-tuple-element.26.refs_0_), channel_id=1, source_target_pairs={{0,4},{4,8},{8,12},{12,0},{1,5},{5,9},{9,13},{13,1},{2,6},{6,10},{... | collective-permute-start | bytes 98312 | tf_op jit(solution)/shard_map/ppermute | solution.py:508
  4.4 5.2 %collective-permute-start.1 = (f32[16,512]{1,0:T(8,128)S(1)}, f32[16,512]{1,0:T(8,128)S(1)}, u32[]{:S(2)}, u32[]{:S(2)}) collective-permute-start(f32[16,512]{1,0:T(8,128)S(1)} %get-tuple-element.26.refs_0_), channel_id=1, source_target_pairs={{0,8},{4,12},{8,0},{12,4},{1,9},{5,13},{9,1},{13,5},{2,10},{6,14},... | collective-permute-start | bytes 98312 | tf_op jit(solution)/shard_map/ppermute | solution.py:508
  6.9 3.9 %collective-permute-start.2 = (f32[16,512]{1,0:T(8,128)S(1)}, f32[16,512]{1,0:T(8,128)S(1)}, u32[]{:S(2)}, u32[]{:S(2)}) collective-permute-start(f32[16,512]{1,0:T(8,128)S(1)} %get-tuple-element.26.refs_0_), channel_id=1, source_target_pairs={{0,12},{4,0},{8,4},{12,8},{1,13},{5,1},{9,5},{13,9},{2,14},{6,2},{... | collective-permute-start | bytes 98312 | tf_op jit(solution)/shard_map/ppermute | solution.py:508
  12.0 2.8 %collective-permute-start.3 = (f32[8,384]{1,0:T(8,128)S(1)}, f32[8,384]{1,0:T(8,128)S(1)}, u32[]{:S(2)}, u32[]{:S(2)}) collective-permute-start(f32[8,384]{1,0:T(8,128)S(1)} %shard_map.49.refs_4_), channel_id=1, source_target_pairs={{0,1},{1,0},{2,3},{3,2},{4,5},{5,4},{6,7},{7,6},{8,9},{9,8},{10,11... | collective-permute-start | bytes 36872 | tf_op jit(solution)/shard_map/ppermute | solution.py:516
  12.1 2.7 %copy-start = (f32[12,512]{1,0:T(8,128)S(1)}, f32[12,512]{1,0:T(8,128)}, u32[]{:S(2)}) copy-start(f32[12,512]{1,0:T(8,128)} %refs_10_.1) | copy-start | bytes 73732
  12.1 1.3 %collective-permute-start.4 = (f32[8,128]{1,0:T(8,128)S(1)}, f32[8,128]{1,0:T(8,128)S(1)}, u32[]{:S(2)}, u32[]{:S(2)}) collective-permute-start(f32[8,128]{1,0:T(8,128)S(1)} %get-tuple-element.41.refs_4_), channel_id=1, source_target_pairs={{0,1},{1,0},{2,3},{3,2},{4,5},{5,4},{6,7},{7,6},{8,9},{9,8},{10,11... | collective-permute-start | bytes 12296 | tf_op jit(solution)/shard_map/ppermute | solution.py:516
